TPU v7x, 128 devices: a whole 4x4x4 slice. The times are simulated.
128 devices in a mesh: row: 8 (over x, core), col: 16 (over y, z).
Axes of the slice: x: 4, y: 4, z: 4, core: 2. Of those that a mesh axis runs over, the one named last changes fastest.
Arguments:
- panel_rows: float32 [8192, 4096], P('row', 'col'), may hold values from -0.75 to 0.75
- owner_slot: int32 [16, 16], replicated, may hold values from -1 to 31, as said below
Outputs:
- packed: float32 [8, 32, 512, 512], P('row', 'col')
Inputs may be any that keep to these rules, and one draw needn't show every extreme that they name: For j <= i, owner_slot[i, j] is the position of tile (i, j) among the 32 positions of group i // 2; tiles of one group have distinct positions; entries above the diagonal are -1. Position p lies on the device of col index p // 2.
All inputs are finite; a program needn't handle non-finite values.
Results may differ from a plain program's by a relative error of at most 0.0003.
Values sent between devices are 32-bit elements; how exact they have to be, the bound alone decides.
No kernel may reach another device: no remote copies, remote signals or barrier semaphores. Data moves between devices by JAX's collectives and lax.ppermute only.
A program may use at most 128 MiB of HBM per device.

v0:
```python
import functools

import jax
import jax.numpy as jnp
from jax import lax
from jax.experimental import pallas as pl
from jax.experimental.pallas import tpu as pltpu
from jax.sharding import Mesh
from jax.sharding import PartitionSpec as P


N = 4
VMEM = pltpu.VMEM
SMEM = pltpu.SMEM
GRANT = 16 * 1024 * 1024


def move(value, target):
    pairs = []
    for c in range(2):
        for y in range(N):
            for z in range(N):
                core, gather, scatter = target(c, *((y, z) if c else (z, y)))
                to = (gather, scatter) if c else (scatter, gather)
                pairs.append(((c * N + y) * N + z, (core * N + to[0] % N) * N + to[1] % N))
    return lax.ppermute(value, ("c", "y", "z"), pairs)


def along(value, step):
    return move(value, lambda c, g, r: (c, g + step, r))


def across(value, step):
    return move(value, lambda c, g, r: (c, g, r + step))


def along_other(value, step):
    return move(value, lambda c, g, r: (1 - c, g + step, r))


def swap(value):
    return lax.ppermute(value, "c", [(0, 1), (1, 0)])


def hop(value, pairs):
    return lax.ppermute(value, "x", pairs)


def specs(space, count):
    return [pl.BlockSpec(memory_space=space)] * count


def cut_kernel(q, group, at_ref, slab_ref, *refs):
    for step in range(N):
        part = lax.rem(at_ref[1] + step, N)
        for block in range(2):
            start = pl.multiple_of((2 * block + at_ref[0]) * N * q + part * q, q)
            row = (2 * group + block) * q
            refs[step - N][row : row + q, :] = slab_ref[pl.ds(start, q), :]


def cut(at, slab, held):
    rows, inner = slab.shape
    q = rows // 16
    return pl.pallas_call(
        functools.partial(cut_kernel, q, 1 if held else 0),
        out_shape=[jax.ShapeDtypeStruct((4 * q, inner), slab.dtype)] * N,
        in_specs=specs(SMEM, 1) + specs(VMEM, 1 + len(held)),
        out_specs=specs(VMEM, N),
        input_output_aliases={2 + k: k for k in range(len(held))},
        compiler_params=pltpu.CompilerParams(vmem_limit_bytes=GRANT),
        cost_estimate=pl.CostEstimate(flops=10**6, bytes_accessed=3 * rows * inner * 4, transcendentals=0),
        name="cut",
    )(at, slab, *held)


def product_kernel(q, work, carried, groups, last, tab_ref, *refs):
    slabs = []
    for raw, places in work:
        count = len(groups) if raw else 1
        slabs.append((raw, refs[:count], list(zip(places, refs[count:]))))
        refs = refs[count + len(places) :]
    total_ref, refs = (refs[0], refs[1:]) if carried else (None, refs)
    raws = sum(raw for raw, _ in work)
    if last:
        (*outs, acc, b_parts, a_part), a_parts = refs, []
        a_parts.append(a_part)
    else:
        acc, a_parts, b_parts = refs[0], list(refs[1 : 1 + raws]), refs[-1]
    wide, side = 4 * q, 4 * q

    def halves(value, place, at):
        inner = value.shape[1]
        high = value.astype(jnp.bfloat16)
        place[at, :inner] = high
        place[at, inner:] = (value - high.astype(jnp.float32)).astype(jnp.bfloat16)

    terms = {}
    used = 0
    for raw, a_refs, pieces in slabs:
        if raw:
            parts, base = a_parts.pop(0), groups[0]
            rows = a_refs[0].shape[0]
            for k, ref in enumerate(a_refs):
                halves(ref[...], parts, slice(k * rows, (k + 1) * rows))
        else:
            parts, base = a_refs[0], 0
        for (place, row), ref in pieces:
            at = slice(wide * used, wide * (used + 1))
            halves(ref[row : row + wide, :], b_parts, at)
            terms.setdefault(place, []).append((parts, base, at))
            used += 1

    for n in range(4 * groups[0], 4 * groups[-1] + 4):
        to = n - 4 * groups[0] if last else n
        for place, pairs in terms.items():
            found = None
            for parts, base, at in pairs:
                inner = parts.shape[1] // 2
                column = (n - 4 * base) * side
                for left, right in ((0, 0), (0, 1), (1, 0)):
                    one = lax.dot_general(
                        b_parts[at, left * inner : (left + 1) * inner],
                        parts[column : column + side, right * inner : (right + 1) * inner],
                        (((1,), (1,)), ((), ())),
                        preferred_element_type=jnp.float32,
                    )
                    found = one if found is None else found + one
            rows = slice(wide * place, wide * (place + 1))
            if carried and place < 3:
                found = total_ref[n, rows, :] + found
            acc[to, rows, :] = found

    if last:
        offset = 0
        for ref in outs:
            first = (offset // 8 * 2 + groups[0]) * 8 + offset % 8

            def place(k, carry, ref=ref, first=first):
                code = tab_ref[first + k]
                safe = jnp.maximum(code, 0)
                start = pl.multiple_of((safe // 2) * q, q)
                for b in range(2):
                    tile = acc[(safe % 2) * 2 + b, pl.ds(start, q), :]
                    ref[k, :, b * side : (b + 1) * side] = jnp.where(code >= 0, tile, 0.0)
                return carry

            lax.fori_loop(0, ref.shape[0], place, 0, unroll=4)
            offset += ref.shape[0]


def product(tab, work, total, groups, sizes):
    args, form, raws, used = [tab], [], 0, 0
    for rows, slices in work:
        raw = rows[0].dtype == jnp.float32
        args += list(rows) + [piece for piece, _ in slices.values()]
        raws, used = raws + raw, used + len(slices)
        form.append((raw, tuple((place, row) for place, (_, row) in slices.items())))
    wide = next(iter(work[0][1].values()))[0].shape[1]
    q, rows, last = wide // 4, 4 * wide, bool(sizes)
    if total is not None:
        args.append(total)
    parts = (len(groups) * rows, 2 * wide)
    b_scratch = VMEM((wide * used, 2 * wide), jnp.bfloat16)
    if last:
        out_shape = [jax.ShapeDtypeStruct((k, q, rows // 2), jnp.float32) for k in sizes]
        scratch = [VMEM((4, rows, wide), jnp.float32), b_scratch, VMEM(parts, jnp.bfloat16)]
    else:
        out_shape = [jax.ShapeDtypeStruct((8, 3 * wide, wide), jnp.float32)]
        out_shape += [jax.ShapeDtypeStruct(parts, jnp.bfloat16)] * raws
        scratch = [b_scratch]
    return pl.pallas_call(
        functools.partial(product_kernel, q, form, total is not None, groups, last),
        out_shape=out_shape,
        in_specs=specs(SMEM, 1) + specs(VMEM, len(args) - 1),
        out_specs=specs(VMEM, len(out_shape)),
        scratch_shapes=scratch,
        input_output_aliases={} if last or total is None else {len(args) - 1: 0},
        compiler_params=pltpu.CompilerParams(vmem_limit_bytes=GRANT),
        cost_estimate=pl.CostEstimate(
            flops=12 * rows * rows * wide * len(groups), bytes_accessed=12 * rows * wide * 4, transcendentals=0
        ),
    )(*args)


def join_kernel(q, at_ref, *refs):
    pieces, out_ref, held = refs[:8], refs[8], refs[9]
    for index in range(8):
        kind = at_ref[0] if index < N else 1 - at_ref[0]
        mine = at_ref[1] if index < N else at_ref[2]
        part = lax.rem(mine + N - index % N, N)
        start = pl.multiple_of((kind * N + part) * q, q)
        for slot in range(2):
            held[slot, pl.ds(start, q), :] = pieces[index][slot]
    for slot in range(2):
        out_ref[0, slot] = held[slot].T


def join(at, pieces):
    _, q, half = pieces[0].shape
    return pl.pallas_call(
        functools.partial(join_kernel, q),
        out_shape=jax.ShapeDtypeStruct((1, 2, half, half), jnp.float32),
        in_specs=specs(SMEM, 1) + specs(VMEM, 8),
        out_specs=pl.BlockSpec(memory_space=VMEM),
        scratch_shapes=[VMEM((2, half, half), jnp.float32)],
        compiler_params=pltpu.CompilerParams(vmem_limit_bytes=GRANT),
        cost_estimate=pl.CostEstimate(flops=10**6, bytes_accessed=16 * half * half, transcendentals=0),
        name="join",
    )(at, *pieces)


def tile_codes(owner, x, c, gather, scatter):
    blocks = owner.shape[0]
    i = lax.broadcasted_iota(jnp.int32, (blocks, blocks), 0)
    j = lax.broadcasted_iota(jnp.int32, (blocks, blocks), 1)
    group = j // 2
    behind = (x - group // 2 + N) % N
    array = jnp.where(behind < 2, behind, 5 - behind) * 2 + jnp.where(group % 2 == c, 0, 1)
    code = jnp.where(j <= i, (array * 2 + j % 2) * 2 + i % 2 + 1, 0)
    index = jnp.arange(64, dtype=jnp.int32)
    far = (scatter + index // 16) % N
    mine = (index // 8) % 2
    near = (gather + (index // 2) % 4) % N
    wanted = jnp.where(c == 0, far * N + near, near * N + far) * 2 + index % 2
    wanted_group = 2 * x + jnp.where(mine == 0, c, 1 - c)
    hit = (owner[None] == wanted[:, None, None]) & ((i // 2)[None] == wanted_group[:, None, None])
    return jnp.sum(jnp.where(hit, code[None], 0), axis=(1, 2)) - 1


def update(panel, owner):
    x, c, y, z = (lax.axis_index(name) for name in "xcyz")
    gather, scatter = jnp.where(c == 0, z, y), jnp.where(c == 0, y, z)
    at = jnp.stack([c, gather, scatter]).astype(jnp.int32)
    tab = tile_codes(owner, x, c, gather, scatter)

    other = swap(panel)
    up, down = [along(panel, 1)], [along(panel, -1)]
    first, *sends = cut(at, other, cut(at, panel, []))
    small = [along(sends[s - 1], s) for s in range(1, N)]
    up.append(along(other, 1))
    down.append(along(other, -1))
    beyond = [along(up[0], 1), along(down[1], -1)]

    onward, wrap = [(0, 1), (1, 2), (2, 3)], [(0, 3)]
    both = jnp.concatenate([small[0], small[2]])
    a1, a3 = hop(first, onward), hop(first, wrap)
    b1, b3 = hop(both, onward), hop(both, wrap + [(1, 0)])
    c1, c3 = hop(small[1], onward), hop(small[1], wrap)
    a2, c2 = hop(a1, onward[1:]), hop(c1, onward[1:])
    b2 = hop(b3, wrap + [(3, 2)])

    wide = first.shape[0]
    low, high = [(v, 0) for v in (both, b1, b3, b2)], [(v, wide) for v in (both, b1, b3, b2)]
    zero, far = [(v, 0) for v in (first, a1, a3, a2)], [(v, 0) for v in (small[1], c1, c3, c2)]
    three, four = range(3), range(4)
    total, own_parts = product(tab, [((panel, other), dict(zip(three, zero)))], None, (0, 1), ())
    total, up_parts, down_parts = product(
        tab, [(up, dict(zip(three, low))), (down, dict(zip(three, high)))], total, (0, 1), ()
    )
    rest = [((own_parts,), {3: zero[3]}), ((up_parts,), {3: low[3]}), ((down_parts,), {3: high[3]})]
    own1, near1, far1, last1 = product(tab, [((beyond[1],), dict(zip(four, far)))] + rest, total, (1,), (8, 8, 8, 8))
    up_far, down_near = across(far1, 1), across(last1, -1)
    own0, near0, near0b, far0, last0 = product(
        tab, [((beyond[0],), dict(zip(four, far)))] + rest, total, (0,), (8, 4, 4, 8, 8)
    )
    down_far = across(far0, -1)
    up_near = across(near0, 1)
    up_sum = across(near1 + up_far, 1)
    up_near = [up_near, across(near0b, 1)]
    down_sum = across(last0 + down_far, -1)

    found, passed = [], []
    for s in range(N):
        part, piece = slice(2 * s, 2 * s + 2), slice(2 * (s % 2), 2 * (s % 2) + 2)
        theirs = own1[part] + up_sum[part] + down_near[part]
        mine = own0[part] + down_sum[part] + up_near[s // 2][piece]
        passed.append(along_other(theirs, s))
        found.append(mine if s == 0 else along(mine, s))
    return join(at, found + passed)


def solution(mesh):
    grid = Mesh(mesh.devices.reshape(N, 2, N, N), ("x", "c", "y", "z"))
    return jax.shard_map(
        update,
        mesh=grid,
        in_specs=(P(("x", "c"), ("y", "z")), P()),
        out_specs=P(("x", "c"), ("y", "z"), None, None),
        check_vma=False,
    )
```

profile of v0, /device:TPU:1, one launch (start us, length us, event | category | flops | bytes accessed | tf_op | source)
XLA Modules:
  0.0 159.9 jit_solution(6398451412544410631)
XLA Ops:
  0.0 1.4 collective-permute-start.2
  1.4 1.4 collective-permute-start
  2.8 1.4 collective-permute-start.15
  4.2 0.0 collective-permute-done.2.slab_ref.refs_1_
  4.3 2.5 %collective-permute-start.16 = (f32[1024,256]{1,0:T(8,128)S(1)}, f32[1024,256]{1,0:T(8,128)}, u32[]{:S(2)}, u32[]{:S(2)}) collective-permute-start(f32[1024,256]{1,0:T(8,128)S(1)} %collective-permute-done.2.slab_ref.refs_1_), channel_id=1, source_target_pairs={{0,3},{1,0},{2,1},{3,2},{4,7},{5,4},{6,5},{7,6},{8,11},{9,8},{10,9... | collective-permute-start | bytes 3145736 | tf_op jit(solution)/shard_map/ppermute | solution.py:26
  6.7 0.1 pad_add_fusion.at_ref
  6.8 1.2 copy-done
  8.0 0.6 cut.2
  8.6 0.6 cut.3
  9.2 3.9 %collective-permute-start.7 = (f32[256,256]{1,0:T(8,128)S(1)}, f32[256,256]{1,0:T(8,128)}, u32[]{:S(2)}, u32[]{:S(2)}) collective-permute-start(f32[256,256]{1,0:T(8,128)S(1)} %get-tuple-element.32.refs_2_), channel_id=1, source_target_pairs={{0,32},{32,64},{64,96},{1,33},{33,65},{65,97},{2,34},{34,66},{66,9... | collective-permute-start | bytes 786440 | tf_op jit(solution)/shard_map/ppermute | solution.py:46
  13.1 3.9 %collective-permute-done.refs_0_ = f32[1024,256]{1,0:T(8,128)} collective-permute-done((f32[1024,256]{1,0:T(8,128)}, f32[1024,256]{1,0:T(8,128)}, u32[]{:S(2)}, u32[]{:S(2)}) %collective-permute-start) | collective-permute-done | bytes 1048608 | tf_op jit(solution)/shard_map/ppermute | solution.py:26
  17.0 1.5 collective-permute-start.12
  18.5 1.2 collective-permute-start.3
  19.7 0.1 broadcast_select_fusion
  19.8 0.2 select_reduce_fusion
  20.0 0.0 collective-permute-done.7.refs_3_
  20.0 4.4 %collective-permute-start.8 = (f32[256,256]{1,0:T(8,128)S(1)}, f32[256,256]{1,0:T(8,128)S(1)}, u32[]{:S(2)}, u32[]{:S(2)}) collective-permute-start(f32[256,256]{1,0:T(8,128)S(1)} %get-tuple-element.32.refs_2_), channel_id=1, source_target_pairs={{0,96},{1,97},{2,98},{3,99},{4,100},{5,101},{6,102},{7,103},{8,104... | collective-permute-start | bytes 786440 | tf_op jit(solution)/shard_map/ppermute | solution.py:46
  24.4 0.0 collective-permute-done.11
  24.4 0.7 collective-permute-start.10
  25.1 0.4 collective-permute-done.3.refs_1_
  25.5 3.1 %collective-permute-start.4 = (f32[256,256]{1,0:T(8,128)S(1)}, f32[256,256]{1,0:T(8,128)S(1)}, u32[]{:S(2)}, u32[]{:S(2)}) collective-permute-start(f32[256,256]{1,0:T(8,128)S(1)} %collective-permute-done.3.refs_1_), channel_id=1, source_target_pairs={{0,32},{32,64},{64,96},{1,33},{33,65},{65,97},{2,34},{34,66},{66,9... | collective-permute-start | bytes 786440 | tf_op jit(solution)/shard_map/ppermute | solution.py:46
  28.6 2.5 %collective-permute-done.12 = f32[256,256]{1,0:T(8,128)} collective-permute-done((f32[256,256]{1,0:T(8,128)S(1)}, f32[256,256]{1,0:T(8,128)}, u32[]{:S(2)}, u32[]{:S(2)}) %collective-permute-start.12) | collective-permute-done | bytes 262176 | tf_op jit(solution)/shard_map/ppermute | solution.py:26
  31.1 4.4 %collective-permute-start.5 = (f32[256,256]{1,0:T(8,128)S(1)}, f32[256,256]{1,0:T(8,128)S(1)}, u32[]{:S(2)}, u32[]{:S(2)}) collective-permute-start(f32[256,256]{1,0:T(8,128)S(1)} %collective-permute-done.3.refs_1_), channel_id=1, source_target_pairs={{0,96},{1,97},{2,98},{3,99},{4,100},{5,101},{6,102},{7,103},{8,104... | collective-permute-start | bytes 786440 | tf_op jit(solution)/shard_map/ppermute | solution.py:46
  35.5 1.0 constant_dynamic-update-slice_fusion.1
  36.5 1.0 constant_dynamic-update-slice_fusion.refs_2_.refs_7_
  37.4 0.0 collective-permute-done.8.refs_4_
  37.5 6.1 %collective-permute-start.1 = (f32[1024,256]{1,0:T(8,128)}, f32[1024,256]{1,0:T(8,128)S(1)}, u32[]{:S(2)}, u32[]{:S(2)}) collective-permute-start(f32[1024,256]{1,0:T(8,128)} %collective-permute-done.refs_0_), channel_id=1, source_target_pairs={{0,1},{1,2},{2,3},{3,0},{4,5},{5,6},{6,7},{7,4},{8,9},{9,10},{10,1... | collective-permute-start | bytes 3145736 | tf_op jit(solution)/shard_map/ppermute | solution.py:26
  43.6 0.0 collective-permute-done.4.refs_2_
  43.6 1.3 collective-permute-start.13
  44.9 0.0 collective-permute-done.5.refs_3_
  44.9 1.9 %collective-permute-start.14 = (f32[512,256]{1,0:T(8,128)S(1)}, f32[512,256]{1,0:T(8,128)S(1)}, u32[]{:S(2)}, u32[]{:S(2)}) collective-permute-start(f32[512,256]{1,0:T(8,128)S(1)} %constant_dynamic-update-slice_fusion.refs_2_.refs_7_), channel_id=1, source_target_pairs={{0,96},{32,0},{1,97},{33,1},{2,98},{34,2},{3,99},{35,3},{4,100},{3... | collective-permute-start | bytes 1572872 | tf_op jit(solution)/shard_map/ppermute | solution.py:46
  46.8 0.0 collective-permute-done.16.refs_6_
  46.8 5.4 %collective-permute-start.25 = (f32[1024,256]{1,0:T(8,128)}, f32[1024,256]{1,0:T(8,128)S(1)}, u32[]{:S(2)}, u32[]{:S(2)}) collective-permute-start(f32[1024,256]{1,0:T(8,128)} %collective-permute-done.16.refs_6_), channel_id=1, source_target_pairs={{0,3},{1,0},{2,1},{3,2},{4,7},{5,4},{6,5},{7,6},{8,11},{9,8},{10,9... | collective-permute-start | bytes 3145736 | tf_op jit(solution)/shard_map/ppermute | solution.py:26
  52.2 3.7 %shard_map.28 = (f32[8,768,256]{2,1,0:T(8,128)S(1)}, bf16[2048,512]{1,0:T(8,128)(2,1)S(1)}) custom-call(s32[64]{0:T(128)S(1)} %broadcast_add_fusion.2.tab_ref, f32[1024,256]{1,0:T(8,128)S(1)} %copy-done.1, f32[1024,256]{1,0:T(8,128)S(1)} %collective-permute-done.2.slab_ref.refs_1_, f32[256,256]{1,0:T(8,128)S(1)} %get-tuple-element.32.refs_2_, ...), custom_call_target="tpu_custom_call" | custom-call | flops 6442450944 | bytes 12582912 | tf_op jit(solution)/shard_map/pallas_call | solution.py:172
  55.9 0.0 collective-permute-done.13.refs_3_.refs_8_
  55.9 0.7 collective-permute-start.9
  56.6 0.7 collective-permute-done.14.refs_4_.refs_9_
  57.3 0.7 collective-permute-start.6
  58.0 4.2 %collective-permute-start.17 = (f32[512,256]{1,0:T(8,128)S(1)}, f32[512,256]{1,0:T(8,128)S(1)}, u32[]{:S(2)}, u32[]{:S(2)}) collective-permute-start(f32[512,256]{1,0:T(8,128)S(1)} %collective-permute-done.14.refs_4_.refs_9_), channel_id=1, source_target_pairs={{0,96},{96,64},{1,97},{97,65},{2,98},{98,66},{3,99},{99,67},{4,100... | collective-permute-start | bytes 1572872 | tf_op jit(solution)/shard_map/ppermute | solution.py:46
  62.2 7.6 %shard_map.29 = (f32[8,768,256]{2,1,0:T(8,128)S(1)}, bf16[2048,512]{1,0:T(8,128)(2,1)S(1)}, bf16[2048,512]{1,0:T(8,128)(2,1)S(1)}) custom-call(s32[64]{0:T(128)S(1)} %broadcast_add_fusion.2.tab_ref, f32[1024,256]{1,0:T(8,128)} %collective-permute-done.refs_0_, f32[1024,256]{1,0:T(8,128)S(1)} %collective-permute-done.10.refs_1_, ...), custom_call_target="tpu_custom_call", output_to_operand_aliasing={{0}: (11, {})} | custom-call | flops 6442450944 | bytes 12582912 | tf_op jit(solution)/shard_map/pallas_call | solution.py:172
  69.9 4.3 %shard_map.30 = (f32[8,64,512]{2,1,0:T(8,128)S(1)}, f32[4,64,512]{2,1,0:T(8,128)S(1)}, f32[4,64,512]{2,1,0:T(8,128)S(1)}, f32[8,64,512]{2,1,0:T(8,128)S(1)}, f32[8,64,512]{2,1,0:T(8,128)S(1)}) custom-call(s32[64]{0:T(128)S(1)} %broadcast_add_fusion.2.tab_ref, f32[1024,256]{1,0:T(8,128)S(1)} %collective-permute-done.1.refs_0_, ...), custom_call_target="tpu_custom_call" | custom-call | flops 3221225472 | bytes 12582912 | tf_op jit(solution)/shard_map/pallas_call | solution.py:172
  74.1 4.0 %collective-permute-start.18 = (f32[8,64,512]{2,1,0:T(8,128)S(1)}, f32[8,64,512]{2,1,0:T(8,128)S(1)}, u32[]{:S(2)}, u32[]{:S(2)}) collective-permute-start(f32[8,64,512]{2,1,0:T(8,128)S(1)} %get-tuple-element.42), channel_id=1, source_target_pairs={{0,12},{1,13},{2,14},{3,15},{4,0},{5,1},{6,2},{7,3},{8,4},{9,5},{1... | collective-permute-start | bytes 3145736 | tf_op jit(solution)/shard_map/ppermute | solution.py:26
  78.1 4.3 %shard_map.31 = (f32[8,64,512]{2,1,0:T(8,128)S(1)}, f32[8,64,512]{2,1,0:T(8,128)S(1)}, f32[8,64,512]{2,1,0:T(8,128)S(1)}, f32[8,64,512]{2,1,0:T(8,128)S(1)}) custom-call(s32[64]{0:T(128)S(1)} %broadcast_add_fusion.2.tab_ref, f32[1024,256]{1,0:T(8,128)S(1)} %collective-permute-done.25.refs_0_, f32[256,256]{1,0:T(8,128)S(1)} %collective-permute-done.3.refs_1_, ...), custom_call_target="tpu_custom_call" | custom-call | flops 3221225472 | bytes 12582912 | tf_op jit(solution)/shard_map/pallas_call | solution.py:172
  82.4 0.1 collective-permute-start.26
  82.5 7.4 %collective-permute-done.18 = f32[8,64,512]{2,1,0:T(8,128)S(1)} collective-permute-done((f32[8,64,512]{2,1,0:T(8,128)S(1)}, f32[8,64,512]{2,1,0:T(8,128)S(1)}, u32[]{:S(2)}, u32[]{:S(2)}) %collective-permute-start.18) | collective-permute-done | bytes 1048608 | tf_op jit(solution)/shard_map/ppermute | solution.py:26
  89.8 0.2 add.262
  90.1 3.5 %collective-permute-start.19 = (f32[8,64,512]{2,1,0:T(8,128)S(1)}, f32[8,64,512]{2,1,0:T(8,128)S(1)}, u32[]{:S(2)}, u32[]{:S(2)}) collective-permute-start(f32[8,64,512]{2,1,0:T(8,128)S(1)} %add.262), channel_id=1, source_target_pairs={{0,12},{1,13},{2,14},{3,15},{4,0},{5,1},{6,2},{7,3},{8,4},{9,5},{1... | collective-permute-start | bytes 3145736 | tf_op jit(solution)/shard_map/ppermute | solution.py:26
  93.5 2.2 %collective-permute-start.28 = (f32[8,64,512]{2,1,0:T(8,128)S(1)}, f32[8,64,512]{2,1,0:T(8,128)S(1)}, u32[]{:S(2)}, u32[]{:S(2)}) collective-permute-start(f32[8,64,512]{2,1,0:T(8,128)S(1)} %get-tuple-element.48), channel_id=1, source_target_pairs={{0,12},{1,13},{2,14},{3,15},{4,0},{5,1},{6,2},{7,3},{8,4},{9,5},{1... | collective-permute-start | bytes 3145736 | tf_op jit(solution)/shard_map/ppermute | solution.py:26
  95.7 2.6 %collective-permute-done.26 = f32[8,64,512]{2,1,0:T(8,128)S(1)} collective-permute-done((f32[8,64,512]{2,1,0:T(8,128)S(1)}, f32[8,64,512]{2,1,0:T(8,128)S(1)}, u32[]{:S(2)}, u32[]{:S(2)}) %collective-permute-start.26) | collective-permute-done | bytes 1048608 | tf_op jit(solution)/shard_map/ppermute | solution.py:26
  98.3 0.2 add.271
  98.5 0.3 collective-permute-start.27
  98.8 0.9 collective-permute-start.20
  99.7 1.4 collective-permute-start.22
  101.1 18.4 %collective-permute-done.20 = f32[4,64,512]{2,1,0:T(8,128)S(1)} collective-permute-done((f32[4,64,512]{2,1,0:T(8,128)S(1)}, f32[4,64,512]{2,1,0:T(8,128)S(1)}, u32[]{:S(2)}, u32[]{:S(2)}) %collective-permute-start.20) | collective-permute-done | bytes 524320 | tf_op jit(solution)/shard_map/ppermute | solution.py:26
  119.6 5.6 %collective-permute-done.22 = f32[4,64,512]{2,1,0:T(8,128)S(1)} collective-permute-done((f32[4,64,512]{2,1,0:T(8,128)S(1)}, f32[4,64,512]{2,1,0:T(8,128)S(1)}, u32[]{:S(2)}, u32[]{:S(2)}) %collective-permute-start.22) | collective-permute-done | bytes 524320 | tf_op jit(solution)/shard_map/ppermute | solution.py:26
  125.2 0.4 slice_add_fusion.8
  125.6 8.8 %collective-permute-start.21 = (f32[2,64,512]{2,1,0:T(8,128)S(1)}, f32[2,64,512]{2,1,0:T(8,128)S(1)}, u32[]{:S(2)}, u32[]{:S(2)}) collective-permute-start(f32[2,64,512]{2,1,0:T(8,128)S(1)} %get-tuple-element.58), channel_id=1, source_target_pairs={{0,1},{1,2},{2,3},{3,0},{4,5},{5,6},{6,7},{7,4},{8,9},{9,10},{10,1... | collective-permute-start | bytes 786440 | tf_op jit(solution)/shard_map/ppermute | solution.py:26
  134.4 2.5 %collective-permute-start.24 = (f32[2,64,512]{2,1,0:T(8,128)S(1)}, f32[2,64,512]{2,1,0:T(8,128)S(1)}, u32[]{:S(2)}, u32[]{:S(2)}) collective-permute-start(f32[2,64,512]{2,1,0:T(8,128)S(1)} %get-tuple-element.53), channel_id=1, source_target_pairs={{0,3},{1,0},{2,1},{3,2},{4,7},{5,4},{6,5},{7,6},{8,11},{9,8},{10,9... | collective-permute-start | bytes 786440 | tf_op jit(solution)/shard_map/ppermute | solution.py:26
  136.8 0.4 slice_add_fusion
  137.2 9.1 %collective-permute-start.29 = (f32[2,64,512]{2,1,0:T(8,128)S(1)}, f32[2,64,512]{2,1,0:T(8,128)S(1)}, u32[]{:S(2)}, u32[]{:S(2)}) collective-permute-start(f32[2,64,512]{2,1,0:T(8,128)S(1)} %get-tuple-element.52), channel_id=1, source_target_pairs={{0,16},{1,17},{2,18},{3,19},{4,20},{5,21},{6,22},{7,23},{8,24},{9,... | collective-permute-start | bytes 786440 | tf_op jit(solution)/shard_map/ppermute | solution.py:26
  146.4 5.2 %collective-permute-start.32 = (f32[2,64,512]{2,1,0:T(8,128)S(1)}, f32[2,64,512]{2,1,0:T(8,128)S(1)}, u32[]{:S(2)}, u32[]{:S(2)}) collective-permute-start(f32[2,64,512]{2,1,0:T(8,128)S(1)} %get-tuple-element.49), channel_id=1, source_target_pairs={{0,19},{1,16},{2,17},{3,18},{4,23},{5,20},{6,21},{7,22},{8,27},{9,... | collective-permute-start | bytes 786440 | tf_op jit(solution)/shard_map/ppermute | solution.py:26
  151.6 3.1 %collective-permute-done.30.refs_5_ = f32[2,64,512]{2,1,0:T(8,128)S(1)} collective-permute-done((f32[2,64,512]{2,1,0:T(8,128)S(1)}, f32[2,64,512]{2,1,0:T(8,128)S(1)}, u32[]{:S(2)}, u32[]{:S(2)}) %collective-permute-start.30) | collective-permute-done | bytes 262176 | tf_op jit(solution)/shard_map/ppermute | solution.py:26
  154.7 2.5 %collective-permute-done.31.refs_6_ = f32[2,64,512]{2,1,0:T(8,128)S(1)} collective-permute-done((f32[2,64,512]{2,1,0:T(8,128)S(1)}, f32[2,64,512]{2,1,0:T(8,128)S(1)}, u32[]{:S(2)}, u32[]{:S(2)}) %collective-permute-start.31) | collective-permute-done | bytes 262176 | tf_op jit(solution)/shard_map/ppermute | solution.py:26
  157.3 2.6 %join.1 = f32[1,2,512,512]{3,2,1,0:T(8,128)} custom-call(s32[3]{0:T(128)S(1)} %pad_add_fusion.at_ref, f32[2,64,512]{2,1,0:T(8,128)S(1)} %get-tuple-element.57.refs_0_, f32[2,64,512]{2,1,0:T(8,128)S(1)} %collective-permute-done.21.refs_1_, f32[2,64,512]{2,1,0:T(8,128)S(1)} %collective-permute-done.23.refs_2_, ...), custom_call_target="tpu_custom_call" | custom-call | flops 1000000 | bytes 4194304 | tf_op jit(solution)/shard_map/join/pallas_call | solution.py:201
  (29 shorter events, 0.1 us)
Async XLA Ops:
  0.0 19.8 %copy-start.2 = (s32[16,16]{1,0:T(8,128)S(1)}, s32[16,16]{1,0:T(8,128)}, u32[]{:S(2)}) copy-start(s32[16,16]{1,0:T(8,128)} %param.3) | copy-start | bytes 3076
  0.0 4.2 %collective-permute-start.2 = (f32[1024,256]{1,0:T(8,128)}, f32[1024,256]{1,0:T(8,128)S(1)}, u32[]{:S(2)}, u32[]{:S(2)}) collective-permute-start(f32[1024,256]{1,0:T(8,128)} %refs_0_.1), channel_id=1, source_target_pairs={{0,16},{16,0},{1,17},{17,1},{2,18},{18,2},{3,19},{19,3},{4,20},{20... | collective-permute-start | bytes 3145736 | tf_op jit(solution)/shard_map/ppermute | solution.py:42
  1.4 15.6 %collective-permute-start = (f32[1024,256]{1,0:T(8,128)}, f32[1024,256]{1,0:T(8,128)}, u32[]{:S(2)}, u32[]{:S(2)}) collective-permute-start(f32[1024,256]{1,0:T(8,128)} %refs_0_.1), channel_id=1, source_target_pairs={{0,1},{1,2},{2,3},{3,0},{4,5},{5,6},{6,7},{7,4},{8,9},{9,10},{10,1... | collective-permute-start | bytes 3145736 | tf_op jit(solution)/shard_map/ppermute | solution.py:26
  2.8 15.7 %collective-permute-start.15 = (f32[1024,256]{1,0:T(8,128)}, f32[1024,256]{1,0:T(8,128)}, u32[]{:S(2)}, u32[]{:S(2)}) collective-permute-start(f32[1024,256]{1,0:T(8,128)} %refs_0_.1), channel_id=1, source_target_pairs={{0,3},{1,0},{2,1},{3,2},{4,7},{5,4},{6,5},{7,6},{8,11},{9,8},{10,9... | collective-permute-start | bytes 3145736 | tf_op jit(solution)/shard_map/ppermute | solution.py:26
  4.3 42.6 %collective-permute-start.16 = (f32[1024,256]{1,0:T(8,128)S(1)}, f32[1024,256]{1,0:T(8,128)}, u32[]{:S(2)}, u32[]{:S(2)}) collective-permute-start(f32[1024,256]{1,0:T(8,128)S(1)} %collective-permute-done.2.slab_ref.refs_1_), channel_id=1, source_target_pairs={{0,3},{1,0},{2,1},{3,2},{4,7},{5,4},{6,5},{7,6},{8,11},{9,8},{10,9... | collective-permute-start | bytes 3145736 | tf_op jit(solution)/shard_map/ppermute | solution.py:26
  6.8 1.2 copy-start
  8.0 44.2 %copy-start.1 = (f32[1024,256]{1,0:T(8,128)S(1)}, f32[1024,256]{1,0:T(8,128)}, u32[]{:S(2)}) copy-start(f32[1024,256]{1,0:T(8,128)} %refs_0_.1) | copy-start | bytes 3145732
  9.2 10.8 %collective-permute-start.7 = (f32[256,256]{1,0:T(8,128)S(1)}, f32[256,256]{1,0:T(8,128)}, u32[]{:S(2)}, u32[]{:S(2)}) collective-permute-start(f32[256,256]{1,0:T(8,128)S(1)} %get-tuple-element.32.refs_2_), channel_id=1, source_target_pairs={{0,32},{32,64},{64,96},{1,33},{33,65},{65,97},{2,34},{34,66},{66,9... | collective-permute-start | bytes 786440 | tf_op jit(solution)/shard_map/ppermute | solution.py:46
  13.1 11.3 %collective-permute-start.11 = (f32[256,256]{1,0:T(8,128)S(1)}, f32[256,256]{1,0:T(8,128)}, u32[]{:S(2)}, u32[]{:S(2)}) collective-permute-start(f32[256,256]{1,0:T(8,128)S(1)} %get-tuple-element.34), channel_id=1, source_target_pairs={{0,1},{1,2},{2,3},{3,0},{4,5},{5,6},{6,7},{7,4},{8,9},{9,10},{10,1... | collective-permute-start | bytes 786440 | tf_op jit(solution)/shard_map/ppermute | solution.py:26
  17.0 14.1 %collective-permute-start.12 = (f32[256,256]{1,0:T(8,128)S(1)}, f32[256,256]{1,0:T(8,128)}, u32[]{:S(2)}, u32[]{:S(2)}) collective-permute-start(f32[256,256]{1,0:T(8,128)S(1)} %get-tuple-element.35), channel_id=1, source_target_pairs={{0,3},{1,0},{2,1},{3,2},{4,7},{5,4},{6,5},{7,6},{8,11},{9,8},{10,9... | collective-permute-start | bytes 786440 | tf_op jit(solution)/shard_map/ppermute | solution.py:26
  18.5 7.0 %collective-permute-start.3 = (f32[256,256]{1,0:T(8,128)S(1)}, f32[256,256]{1,0:T(8,128)S(1)}, u32[]{:S(2)}, u32[]{:S(2)}) collective-permute-start(f32[256,256]{1,0:T(8,128)S(1)} %get-tuple-element.31), channel_id=1, source_target_pairs={{0,2},{1,3},{2,0},{3,1},{4,6},{5,7},{6,4},{7,5},{8,10},{9,11},{10,... | collective-permute-start | bytes 786440 | tf_op jit(solution)/shard_map/ppermute | solution.py:26
  20.0 17.5 %collective-permute-start.8 = (f32[256,256]{1,0:T(8,128)S(1)}, f32[256,256]{1,0:T(8,128)S(1)}, u32[]{:S(2)}, u32[]{:S(2)}) collective-permute-start(f32[256,256]{1,0:T(8,128)S(1)} %get-tuple-element.32.refs_2_), channel_id=1, source_target_pairs={{0,96},{1,97},{2,98},{3,99},{4,100},{5,101},{6,102},{7,103},{8,104... | collective-permute-start | bytes 786440 | tf_op jit(solution)/shard_map/ppermute | solution.py:46
  24.4 33.5 %collective-permute-start.10 = (f32[1024,256]{1,0:T(8,128)S(1)}, f32[1024,256]{1,0:T(8,128)S(1)}, u32[]{:S(2)}, u32[]{:S(2)}) collective-permute-start(f32[1024,256]{1,0:T(8,128)S(1)} %collective-permute-done.2.slab_ref.refs_1_), channel_id=1, source_target_pairs={{0,1},{1,2},{2,3},{3,0},{4,5},{5,6},{6,7},{7,4},{8,9},{9,10},{10,1... | collective-permute-start | bytes 3145736 | tf_op jit(solution)/shard_map/ppermute | solution.py:26
  25.5 18.0 %collective-permute-start.4 = (f32[256,256]{1,0:T(8,128)S(1)}, f32[256,256]{1,0:T(8,128)S(1)}, u32[]{:S(2)}, u32[]{:S(2)}) collective-permute-start(f32[256,256]{1,0:T(8,128)S(1)} %collective-permute-done.3.refs_1_), channel_id=1, source_target_pairs={{0,32},{32,64},{64,96},{1,33},{33,65},{65,97},{2,34},{34,66},{66,9... | collective-permute-start | bytes 786440 | tf_op jit(solution)/shard_map/ppermute | solution.py:46
  31.1 13.8 %collective-permute-start.5 = (f32[256,256]{1,0:T(8,128)S(1)}, f32[256,256]{1,0:T(8,128)S(1)}, u32[]{:S(2)}, u32[]{:S(2)}) collective-permute-start(f32[256,256]{1,0:T(8,128)S(1)} %collective-permute-done.3.refs_1_), channel_id=1, source_target_pairs={{0,96},{1,97},{2,98},{3,99},{4,100},{5,101},{6,102},{7,103},{8,104... | collective-permute-start | bytes 786440 | tf_op jit(solution)/shard_map/ppermute | solution.py:46
  37.5 32.4 %collective-permute-start.1 = (f32[1024,256]{1,0:T(8,128)}, f32[1024,256]{1,0:T(8,128)S(1)}, u32[]{:S(2)}, u32[]{:S(2)}) collective-permute-start(f32[1024,256]{1,0:T(8,128)} %collective-permute-done.refs_0_), channel_id=1, source_target_pairs={{0,1},{1,2},{2,3},{3,0},{4,5},{5,6},{6,7},{7,4},{8,9},{9,10},{10,1... | collective-permute-start | bytes 3145736 | tf_op jit(solution)/shard_map/ppermute | solution.py:26
  43.6 12.3 %collective-permute-start.13 = (f32[512,256]{1,0:T(8,128)S(1)}, f32[512,256]{1,0:T(8,128)S(1)}, u32[]{:S(2)}, u32[]{:S(2)}) collective-permute-start(f32[512,256]{1,0:T(8,128)S(1)} %constant_dynamic-update-slice_fusion.refs_2_.refs_7_), channel_id=1, source_target_pairs={{0,32},{32,64},{64,96},{1,33},{33,65},{65,97},{2,34},{34,66},{66,9... | collective-permute-start | bytes 1572872 | tf_op jit(solution)/shard_map/ppermute | solution.py:46
  44.9 12.4 %collective-permute-start.14 = (f32[512,256]{1,0:T(8,128)S(1)}, f32[512,256]{1,0:T(8,128)S(1)}, u32[]{:S(2)}, u32[]{:S(2)}) collective-permute-start(f32[512,256]{1,0:T(8,128)S(1)} %constant_dynamic-update-slice_fusion.refs_2_.refs_7_), channel_id=1, source_target_pairs={{0,96},{32,0},{1,97},{33,1},{2,98},{34,2},{3,99},{35,3},{4,100},{3... | collective-permute-start | bytes 1572872 | tf_op jit(solution)/shard_map/ppermute | solution.py:46
  46.8 31.3 %collective-permute-start.25 = (f32[1024,256]{1,0:T(8,128)}, f32[1024,256]{1,0:T(8,128)S(1)}, u32[]{:S(2)}, u32[]{:S(2)}) collective-permute-start(f32[1024,256]{1,0:T(8,128)} %collective-permute-done.16.refs_6_), channel_id=1, source_target_pairs={{0,3},{1,0},{2,1},{3,2},{4,7},{5,4},{6,5},{7,6},{8,11},{9,8},{10,9... | collective-permute-start | bytes 3145736 | tf_op jit(solution)/shard_map/ppermute | solution.py:26
  55.9 13.9 %collective-permute-start.9 = (f32[256,256]{1,0:T(8,128)}, f32[256,256]{1,0:T(8,128)S(1)}, u32[]{:S(2)}, u32[]{:S(2)}) collective-permute-start(f32[256,256]{1,0:T(8,128)} %collective-permute-done.7.refs_3_), channel_id=1, source_target_pairs={{32,64},{64,96},{33,65},{65,97},{34,66},{66,98},{35,67},{67,99},{3... | collective-permute-start | bytes 786440 | tf_op jit(solution)/shard_map/ppermute | solution.py:46
  57.3 12.6 %collective-permute-start.6 = (f32[256,256]{1,0:T(8,128)S(1)}, f32[256,256]{1,0:T(8,128)S(1)}, u32[]{:S(2)}, u32[]{:S(2)}) collective-permute-start(f32[256,256]{1,0:T(8,128)S(1)} %collective-permute-done.4.refs_2_), channel_id=1, source_target_pairs={{32,64},{64,96},{33,65},{65,97},{34,66},{66,98},{35,67},{67,99},{3... | collective-permute-start | bytes 786440 | tf_op jit(solution)/shard_map/ppermute | solution.py:46
  58.0 11.9 %collective-permute-start.17 = (f32[512,256]{1,0:T(8,128)S(1)}, f32[512,256]{1,0:T(8,128)S(1)}, u32[]{:S(2)}, u32[]{:S(2)}) collective-permute-start(f32[512,256]{1,0:T(8,128)S(1)} %collective-permute-done.14.refs_4_.refs_9_), channel_id=1, source_target_pairs={{0,96},{96,64},{1,97},{97,65},{2,98},{98,66},{3,99},{99,67},{4,100... | collective-permute-start | bytes 1572872 | tf_op jit(solution)/shard_map/ppermute | solution.py:46
  74.1 15.7 %collective-permute-start.18 = (f32[8,64,512]{2,1,0:T(8,128)S(1)}, f32[8,64,512]{2,1,0:T(8,128)S(1)}, u32[]{:S(2)}, u32[]{:S(2)}) collective-permute-start(f32[8,64,512]{2,1,0:T(8,128)S(1)} %get-tuple-element.42), channel_id=1, source_target_pairs={{0,12},{1,13},{2,14},{3,15},{4,0},{5,1},{6,2},{7,3},{8,4},{9,5},{1... | collective-permute-start | bytes 3145736 | tf_op jit(solution)/shard_map/ppermute | solution.py:26
  82.4 15.9 %collective-permute-start.26 = (f32[8,64,512]{2,1,0:T(8,128)S(1)}, f32[8,64,512]{2,1,0:T(8,128)S(1)}, u32[]{:S(2)}, u32[]{:S(2)}) collective-permute-start(f32[8,64,512]{2,1,0:T(8,128)S(1)} %get-tuple-element.47), channel_id=1, source_target_pairs={{0,4},{1,5},{2,6},{3,7},{4,8},{5,9},{6,10},{7,11},{8,12},{9,13},{1... | collective-permute-start | bytes 3145736 | tf_op jit(solution)/shard_map/ppermute | solution.py:26
  90.1 35.2 %collective-permute-start.19 = (f32[8,64,512]{2,1,0:T(8,128)S(1)}, f32[8,64,512]{2,1,0:T(8,128)S(1)}, u32[]{:S(2)}, u32[]{:S(2)}) collective-permute-start(f32[8,64,512]{2,1,0:T(8,128)S(1)} %add.262), channel_id=1, source_target_pairs={{0,12},{1,13},{2,14},{3,15},{4,0},{5,1},{6,2},{7,3},{8,4},{9,5},{1... | collective-permute-start | bytes 3145736 | tf_op jit(solution)/shard_map/ppermute | solution.py:26
  93.5 43.3 %collective-permute-start.28 = (f32[8,64,512]{2,1,0:T(8,128)S(1)}, f32[8,64,512]{2,1,0:T(8,128)S(1)}, u32[]{:S(2)}, u32[]{:S(2)}) collective-permute-start(f32[8,64,512]{2,1,0:T(8,128)S(1)} %get-tuple-element.48), channel_id=1, source_target_pairs={{0,12},{1,13},{2,14},{3,15},{4,0},{5,1},{6,2},{7,3},{8,4},{9,5},{1... | collective-permute-start | bytes 3145736 | tf_op jit(solution)/shard_map/ppermute | solution.py:26
  98.5 38.3 %collective-permute-start.27 = (f32[8,64,512]{2,1,0:T(8,128)S(1)}, f32[8,64,512]{2,1,0:T(8,128)S(1)}, u32[]{:S(2)}, u32[]{:S(2)}) collective-permute-start(f32[8,64,512]{2,1,0:T(8,128)S(1)} %add.271), channel_id=1, source_target_pairs={{0,4},{1,5},{2,6},{3,7},{4,8},{5,9},{6,10},{7,11},{8,12},{9,13},{1... | collective-permute-start | bytes 3145736 | tf_op jit(solution)/shard_map/ppermute | solution.py:26
  98.8 20.8 %collective-permute-start.20 = (f32[4,64,512]{2,1,0:T(8,128)S(1)}, f32[4,64,512]{2,1,0:T(8,128)S(1)}, u32[]{:S(2)}, u32[]{:S(2)}) collective-permute-start(f32[4,64,512]{2,1,0:T(8,128)S(1)} %get-tuple-element.43), channel_id=1, source_target_pairs={{0,4},{1,5},{2,6},{3,7},{4,8},{5,9},{6,10},{7,11},{8,12},{9,13},{1... | collective-permute-start | bytes 1572872 | tf_op jit(solution)/shard_map/ppermute | solution.py:26
  99.7 25.5 %collective-permute-start.22 = (f32[4,64,512]{2,1,0:T(8,128)S(1)}, f32[4,64,512]{2,1,0:T(8,128)S(1)}, u32[]{:S(2)}, u32[]{:S(2)}) collective-permute-start(f32[4,64,512]{2,1,0:T(8,128)S(1)} %get-tuple-element.44), channel_id=1, source_target_pairs={{0,4},{1,5},{2,6},{3,7},{4,8},{5,9},{6,10},{7,11},{8,12},{9,13},{1... | collective-permute-start | bytes 1572872 | tf_op jit(solution)/shard_map/ppermute | solution.py:26
  125.6 20.8 %collective-permute-start.21 = (f32[2,64,512]{2,1,0:T(8,128)S(1)}, f32[2,64,512]{2,1,0:T(8,128)S(1)}, u32[]{:S(2)}, u32[]{:S(2)}) collective-permute-start(f32[2,64,512]{2,1,0:T(8,128)S(1)} %get-tuple-element.58), channel_id=1, source_target_pairs={{0,1},{1,2},{2,3},{3,0},{4,5},{5,6},{6,7},{7,4},{8,9},{9,10},{10,1... | collective-permute-start | bytes 786440 | tf_op jit(solution)/shard_map/ppermute | solution.py:26
  134.4 12.0 %collective-permute-start.23 = (f32[2,64,512]{2,1,0:T(8,128)S(1)}, f32[2,64,512]{2,1,0:T(8,128)S(1)}, u32[]{:S(2)}, u32[]{:S(2)}) collective-permute-start(f32[2,64,512]{2,1,0:T(8,128)S(1)} %get-tuple-element.54), channel_id=1, source_target_pairs={{0,2},{1,3},{2,0},{3,1},{4,6},{5,7},{6,4},{7,5},{8,10},{9,11},{10,... | collective-permute-start | bytes 786440 | tf_op jit(solution)/shard_map/ppermute | solution.py:26
  134.4 17.2 %collective-permute-start.24 = (f32[2,64,512]{2,1,0:T(8,128)S(1)}, f32[2,64,512]{2,1,0:T(8,128)S(1)}, u32[]{:S(2)}, u32[]{:S(2)}) collective-permute-start(f32[2,64,512]{2,1,0:T(8,128)S(1)} %get-tuple-element.53), channel_id=1, source_target_pairs={{0,3},{1,0},{2,1},{3,2},{4,7},{5,4},{6,5},{7,6},{8,11},{9,8},{10,9... | collective-permute-start | bytes 786440 | tf_op jit(solution)/shard_map/ppermute | solution.py:26
  137.2 14.4 %collective-permute-start.29 = (f32[2,64,512]{2,1,0:T(8,128)S(1)}, f32[2,64,512]{2,1,0:T(8,128)S(1)}, u32[]{:S(2)}, u32[]{:S(2)}) collective-permute-start(f32[2,64,512]{2,1,0:T(8,128)S(1)} %get-tuple-element.52), channel_id=1, source_target_pairs={{0,16},{1,17},{2,18},{3,19},{4,20},{5,21},{6,22},{7,23},{8,24},{9,... | collective-permute-start | bytes 786440 | tf_op jit(solution)/shard_map/ppermute | solution.py:26
  146.3 8.4 %collective-permute-start.30 = (f32[2,64,512]{2,1,0:T(8,128)S(1)}, f32[2,64,512]{2,1,0:T(8,128)S(1)}, u32[]{:S(2)}, u32[]{:S(2)}) collective-permute-start(f32[2,64,512]{2,1,0:T(8,128)S(1)} %get-tuple-element.51), channel_id=1, source_target_pairs={{0,17},{1,18},{2,19},{3,16},{4,21},{5,22},{6,23},{7,20},{8,25},{9,... | collective-permute-start | bytes 786440 | tf_op jit(solution)/shard_map/ppermute | solution.py:26
  146.3 10.9 %collective-permute-start.31 = (f32[2,64,512]{2,1,0:T(8,128)S(1)}, f32[2,64,512]{2,1,0:T(8,128)S(1)}, u32[]{:S(2)}, u32[]{:S(2)}) collective-permute-start(f32[2,64,512]{2,1,0:T(8,128)S(1)} %get-tuple-element.50), channel_id=1, source_target_pairs={{0,18},{1,19},{2,16},{3,17},{4,22},{5,23},{6,20},{7,21},{8,26},{9,... | collective-permute-start | bytes 786440 | tf_op jit(solution)/shard_map/ppermute | solution.py:26
  146.4 10.9 %collective-permute-start.32 = (f32[2,64,512]{2,1,0:T(8,128)S(1)}, f32[2,64,512]{2,1,0:T(8,128)S(1)}, u32[]{:S(2)}, u32[]{:S(2)}) collective-permute-start(f32[2,64,512]{2,1,0:T(8,128)S(1)} %get-tuple-element.49), channel_id=1, source_target_pairs={{0,19},{1,16},{2,17},{3,18},{4,23},{5,20},{6,21},{7,22},{8,27},{9,... | collective-permute-start | bytes 786440 | tf_op jit(solution)/shard_map/ppermute | solution.py:26
where the time goes:
time: 161 us; the launch traced here: 160 us
  starting transfers between devices  84 us (52%)
  waiting for transfers between devices  47.3 us (29%)
  Pallas kernels  23.6 us (15%)
  local copies, waits for them, and re-layouts  3.17 us (2%)
    ppermute x23, starting transfers between devices, move(): return lax.ppermute(value, ('c', 'y', 'z'), pairs)  58 us
    ppermute x23, waiting for transfers between devices, move(): return lax.ppermute(value, ('c', 'y', 'z'), pairs)  46.6 us
    ppermute x9, starting transfers between devices, hop(): return lax.ppermute(value, 'x', pairs)  24.6 us
    pallas_call x4, Pallas kernels, product(): pl.pallas_call(functools.partial(product_kernel, q, form, total is not No...  19.8 us
  transfers between devices with their start and end apart: 33, of which 10 were waited for; matrix products, arithmetic and copies ran while one was open for 2% of the time, Pallas kernels for 13%

commit v1 on v0

--- a/solution.py
+++ b/solution.py
@@ -244,11 +244,11 @@
 
     onward, wrap = [(0, 1), (1, 2), (2, 3)], [(0, 3)]
     both = jnp.concatenate([small[0], small[2]])
-    a1, a3 = hop(first, onward), hop(first, wrap)
-    b1, b3 = hop(both, onward), hop(both, wrap + [(1, 0)])
-    c1, c3 = hop(small[1], onward), hop(small[1], wrap)
-    a2, c2 = hop(a1, onward[1:]), hop(c1, onward[1:])
-    b2 = hop(b3, wrap + [(3, 2)])
+    a1, a3 = hop(first, onward), hop(first, wrap + [(1, 0)])
+    b1, b3 = hop(both, onward), hop(both, wrap)
+    c1, c3 = hop(small[1], onward), hop(small[1], wrap + [(1, 0)])
+    a2, c2 = hop(a3, wrap + [(3, 2)]), hop(c3, wrap + [(3, 2)])
+    b2 = hop(b1, onward[1:])
 
     wide = first.shape[0]
     low, high = [(v, 0) for v in (both, b1, b3, b2)], [(v, wide) for v in (both, b1, b3, b2)]
@@ -259,24 +259,21 @@
         tab, [(up, dict(zip(three, low))), (down, dict(zip(three, high)))], total, (0, 1), ()
     )
     rest = [((own_parts,), {3: zero[3]}), ((up_parts,), {3: low[3]}), ((down_parts,), {3: high[3]})]
+    own0, near0, far0, last0 = product(tab, [((beyond[0],), dict(zip(four, far)))] + rest, total, (0,), (8, 8, 8, 8))
+    up_far, down_near = across(far0, 1), across(last0, -1)
     own1, near1, far1, last1 = product(tab, [((beyond[1],), dict(zip(four, far)))] + rest, total, (1,), (8, 8, 8, 8))
-    up_far, down_near = across(far1, 1), across(last1, -1)
-    own0, near0, near0b, far0, last0 = product(
-        tab, [((beyond[0],), dict(zip(four, far)))] + rest, total, (0,), (8, 4, 4, 8, 8)
-    )
-    down_far = across(far0, -1)
-    up_near = across(near0, 1)
-    up_sum = across(near1 + up_far, 1)
-    up_near = [up_near, across(near0b, 1)]
-    down_sum = across(last0 + down_far, -1)
+    down_far = across(far1, -1)
+    up_near = across(near1, 1)
+    up_sum = across(near0 + up_far, 1)
+    down_sum = across(last1 + down_far, -1)
 
     found, passed = [], []
     for s in range(N):
-        part, piece = slice(2 * s, 2 * s + 2), slice(2 * (s % 2), 2 * (s % 2) + 2)
-        theirs = own1[part] + up_sum[part] + down_near[part]
-        mine = own0[part] + down_sum[part] + up_near[s // 2][piece]
+        part = slice(2 * s, 2 * s + 2)
+        mine = own0[part] + up_sum[part] + down_near[part]
+        theirs = own1[part] + down_sum[part] + up_near[part]
+        found.append(mine if s == 0 else along(mine, s))
         passed.append(along_other(theirs, s))
-        found.append(mine if s == 0 else along(mine, s))
     return join(at, found + passed)
 
 

time: 161 us -> 149 us (0.925)
  the two profiles are of different devices: /device:TPU:1 before, /device:TPU:7 now
where the time goes in v1:
time: 149 us
  starting transfers between devices  69.8 us (47%)
  waiting for transfers between devices  50.4 us (34%)
  Pallas kernels  23.6 us (16%)
  local copies, waits for them, and re-layouts  3.17 us (2%)
    ppermute x22, starting transfers between devices, move(): return lax.ppermute(value, ('c', 'y', 'z'), pairs)  55 us
    ppermute x22, waiting for transfers between devices, move(): return lax.ppermute(value, ('c', 'y', 'z'), pairs)  45.7 us
    pallas_call x4, Pallas kernels, product(): pl.pallas_call(functools.partial(product_kernel, q, form, total is not No...  19.8 us
    ppermute x9, starting transfers between devices, hop(): return lax.ppermute(value, 'x', pairs)  14.2 us
    ppermute x9, waiting for transfers between devices, hop(): return lax.ppermute(value, 'x', pairs)  4.69 us
  transfers between devices with their start and end apart: 32, of which 12 were waited for; matrix products, arithmetic and copies ran while one was open for 2% of the time, Pallas kernels for 14%

profile of v1, /device:TPU:7, one launch (start us, length us, event | category | flops | bytes accessed | tf_op | source)
XLA Modules:
  0.0 148.7 jit_solution(7659987322583711150)
XLA Ops:
  0.0 0.7 collective-permute-start.2
  0.7 1.3 collective-permute-start
  2.0 1.4 collective-permute-start.15
  3.4 0.0 collective-permute-done.2.slab_ref.refs_1_
  3.4 2.5 %collective-permute-start.16 = (f32[1024,256]{1,0:T(8,128)S(1)}, f32[1024,256]{1,0:T(8,128)}, u32[]{:S(2)}, u32[]{:S(2)}) collective-permute-start(f32[1024,256]{1,0:T(8,128)S(1)} %collective-permute-done.2.slab_ref.refs_1_), channel_id=1, source_target_pairs={{0,3},{1,0},{2,1},{3,2},{4,7},{5,4},{6,5},{7,6},{8,11},{9,8},{10,9... | collective-permute-start | bytes 3145736 | tf_op jit(solution)/shard_map/ppermute | solution.py:26
  5.9 0.1 pad_add_fusion.at_ref
  6.0 1.2 copy-done
  7.2 0.6 cut.2
  7.8 0.6 cut.3
  8.4 1.3 collective-permute-start.7
  9.7 0.1 collective-permute-start.11
  9.8 6.4 %collective-permute-done.refs_0_ = f32[1024,256]{1,0:T(8,128)} collective-permute-done((f32[1024,256]{1,0:T(8,128)}, f32[1024,256]{1,0:T(8,128)}, u32[]{:S(2)}, u32[]{:S(2)}) %collective-permute-start) | collective-permute-done | bytes 1048608 | tf_op jit(solution)/shard_map/ppermute | solution.py:26
  16.2 1.5 collective-permute-start.12
  17.7 1.2 collective-permute-start.3
  18.9 0.1 broadcast_select_fusion
  19.0 0.2 select_reduce_fusion
  19.2 0.0 collective-permute-done.7.refs_3_
  19.2 1.3 collective-permute-start.8
  20.5 0.7 collective-permute-start.10
  21.2 3.5 %collective-permute-done.3.refs_1_ = f32[256,256]{1,0:T(8,128)S(1)} collective-permute-done((f32[256,256]{1,0:T(8,128)S(1)}, f32[256,256]{1,0:T(8,128)S(1)}, u32[]{:S(2)}, u32[]{:S(2)}) %collective-permute-start.3) | collective-permute-done | bytes 262176 | tf_op jit(solution)/shard_map/ppermute | solution.py:26
  24.7 1.3 collective-permute-start.5
  26.0 4.3 %collective-permute-done.12 = f32[256,256]{1,0:T(8,128)} collective-permute-done((f32[256,256]{1,0:T(8,128)S(1)}, f32[256,256]{1,0:T(8,128)}, u32[]{:S(2)}, u32[]{:S(2)}) %collective-permute-start.12) | collective-permute-done | bytes 262176 | tf_op jit(solution)/shard_map/ppermute | solution.py:26
  30.3 1.3 collective-permute-start.4
  31.6 1.0 constant_dynamic-update-slice_fusion.1
  32.6 1.0 constant_dynamic-update-slice_fusion.refs_2_.refs_7_
  33.5 6.1 %collective-permute-start.1 = (f32[1024,256]{1,0:T(8,128)}, f32[1024,256]{1,0:T(8,128)S(1)}, u32[]{:S(2)}, u32[]{:S(2)}) collective-permute-start(f32[1024,256]{1,0:T(8,128)} %collective-permute-done.refs_0_), channel_id=1, source_target_pairs={{0,1},{1,2},{2,3},{3,0},{4,5},{5,6},{6,7},{7,4},{8,9},{9,10},{10,1... | collective-permute-start | bytes 3145736 | tf_op jit(solution)/shard_map/ppermute | solution.py:26
  39.6 1.3 collective-permute-start.13
  40.9 1.3 collective-permute-start.14
  42.2 0.0 collective-permute-done.16.refs_6_
  42.2 4.8 %collective-permute-start.24 = (f32[1024,256]{1,0:T(8,128)}, f32[1024,256]{1,0:T(8,128)S(1)}, u32[]{:S(2)}, u32[]{:S(2)}) collective-permute-start(f32[1024,256]{1,0:T(8,128)} %collective-permute-done.16.refs_6_), channel_id=1, source_target_pairs={{0,3},{1,0},{2,1},{3,2},{4,7},{5,4},{6,5},{7,6},{8,11},{9,8},{10,9... | collective-permute-start | bytes 3145736 | tf_op jit(solution)/shard_map/ppermute | solution.py:26
  47.1 3.7 %shard_map.28 = (f32[8,768,256]{2,1,0:T(8,128)S(1)}, bf16[2048,512]{1,0:T(8,128)(2,1)S(1)}) custom-call(s32[64]{0:T(128)S(1)} %broadcast_add_fusion.2.tab_ref, f32[1024,256]{1,0:T(8,128)S(1)} %copy-done.1, f32[1024,256]{1,0:T(8,128)S(1)} %collective-permute-done.2.slab_ref.refs_1_, f32[256,256]{1,0:T(8,128)S(1)} %get-tuple-element.31.refs_2_, ...), custom_call_target="tpu_custom_call" | custom-call | flops 6442450944 | bytes 12582912 | tf_op jit(solution)/shard_map/pallas_call | solution.py:172
  50.8 2.3 %collective-permute-done.13.refs_3_.refs_8_ = f32[512,256]{1,0:T(8,128)S(1)} collective-permute-done((f32[512,256]{1,0:T(8,128)S(1)}, f32[512,256]{1,0:T(8,128)S(1)}, u32[]{:S(2)}, u32[]{:S(2)}) %collective-permute-start.13) | collective-permute-done | bytes 524320 | tf_op jit(solution)/shard_map/ppermute | solution.py:46
  53.1 3.1 %collective-permute-start.9 = (f32[256,256]{1,0:T(8,128)S(1)}, f32[256,256]{1,0:T(8,128)S(1)}, u32[]{:S(2)}, u32[]{:S(2)}) collective-permute-start(f32[256,256]{1,0:T(8,128)S(1)} %collective-permute-done.8.refs_4_), channel_id=1, source_target_pairs={{0,96},{96,64},{1,97},{97,65},{2,98},{98,66},{3,99},{99,67},{4,100... | collective-permute-start | bytes 786440 | tf_op jit(solution)/shard_map/ppermute | solution.py:46
  56.2 0.0 collective-permute-done.14.refs_4_.refs_9_
  56.2 1.9 %collective-permute-start.6 = (f32[256,256]{1,0:T(8,128)S(1)}, f32[256,256]{1,0:T(8,128)S(1)}, u32[]{:S(2)}, u32[]{:S(2)}) collective-permute-start(f32[256,256]{1,0:T(8,128)S(1)} %collective-permute-done.5.refs_3_), channel_id=1, source_target_pairs={{0,96},{96,64},{1,97},{97,65},{2,98},{98,66},{3,99},{99,67},{4,100... | collective-permute-start | bytes 786440 | tf_op jit(solution)/shard_map/ppermute | solution.py:46
  58.2 1.5 collective-permute-start.17
  59.6 7.6 %shard_map.29 = (f32[8,768,256]{2,1,0:T(8,128)S(1)}, bf16[2048,512]{1,0:T(8,128)(2,1)S(1)}, bf16[2048,512]{1,0:T(8,128)(2,1)S(1)}) custom-call(s32[64]{0:T(128)S(1)} %broadcast_add_fusion.2.tab_ref, f32[1024,256]{1,0:T(8,128)} %collective-permute-done.refs_0_, f32[1024,256]{1,0:T(8,128)S(1)} %collective-permute-done.10.refs_1_, ...), custom_call_target="tpu_custom_call", output_to_operand_aliasing={{0}: (11, {})} | custom-call | flops 6442450944 | bytes 12582912 | tf_op jit(solution)/shard_map/pallas_call | solution.py:172
  67.2 0.0 collective-permute-done.9.refs_6_
  67.3 2.3 %collective-permute-done.17.refs_8_.refs_10_ = f32[512,256]{1,0:T(8,128)S(1)} collective-permute-done((f32[512,256]{1,0:T(8,128)S(1)}, f32[512,256]{1,0:T(8,128)S(1)}, u32[]{:S(2)}, u32[]{:S(2)}) %collective-permute-start.17) | collective-permute-done | bytes 524320 | tf_op jit(solution)/shard_map/ppermute | solution.py:46
  69.6 4.3 %shard_map.30 = (f32[8,64,512]{2,1,0:T(8,128)S(1)}, f32[8,64,512]{2,1,0:T(8,128)S(1)}, f32[8,64,512]{2,1,0:T(8,128)S(1)}, f32[8,64,512]{2,1,0:T(8,128)S(1)}) custom-call(s32[64]{0:T(128)S(1)} %broadcast_add_fusion.2.tab_ref, f32[1024,256]{1,0:T(8,128)S(1)} %collective-permute-done.1.refs_0_, f32[256,256]{1,0:T(8,128)S(1)} %collective-permute-done.3.refs_1_, ...), custom_call_target="tpu_custom_call" | custom-call | flops 3221225472 | bytes 12582912 | tf_op jit(solution)/shard_map/pallas_call | solution.py:172
  73.9 5.5 %collective-permute-start.18 = (f32[8,64,512]{2,1,0:T(8,128)S(1)}, f32[8,64,512]{2,1,0:T(8,128)S(1)}, u32[]{:S(2)}, u32[]{:S(2)}) collective-permute-start(f32[8,64,512]{2,1,0:T(8,128)S(1)} %get-tuple-element.41), channel_id=1, source_target_pairs={{0,4},{1,5},{2,6},{3,7},{4,8},{5,9},{6,10},{7,11},{8,12},{9,13},{1... | collective-permute-start | bytes 3145736 | tf_op jit(solution)/shard_map/ppermute | solution.py:26
  79.4 4.3 %shard_map.31 = (f32[8,64,512]{2,1,0:T(8,128)S(1)}, f32[8,64,512]{2,1,0:T(8,128)S(1)}, f32[8,64,512]{2,1,0:T(8,128)S(1)}, f32[8,64,512]{2,1,0:T(8,128)S(1)}) custom-call(s32[64]{0:T(128)S(1)} %broadcast_add_fusion.2.tab_ref, f32[1024,256]{1,0:T(8,128)S(1)} %collective-permute-done.24.refs_0_, f32[256,256]{1,0:T(8,128)S(1)} %collective-permute-done.3.refs_1_, ...), custom_call_target="tpu_custom_call" | custom-call | flops 3221225472 | bytes 12582912 | tf_op jit(solution)/shard_map/pallas_call | solution.py:172
  83.6 4.6 %collective-permute-start.25 = (f32[8,64,512]{2,1,0:T(8,128)S(1)}, f32[8,64,512]{2,1,0:T(8,128)S(1)}, u32[]{:S(2)}, u32[]{:S(2)}) collective-permute-start(f32[8,64,512]{2,1,0:T(8,128)S(1)} %get-tuple-element.45), channel_id=1, source_target_pairs={{0,12},{1,13},{2,14},{3,15},{4,0},{5,1},{6,2},{7,3},{8,4},{9,5},{1... | collective-permute-start | bytes 3145736 | tf_op jit(solution)/shard_map/ppermute | solution.py:26
  88.2 1.4 collective-permute-start.20
  89.7 6.4 %collective-permute-done.18 = f32[8,64,512]{2,1,0:T(8,128)S(1)} collective-permute-done((f32[8,64,512]{2,1,0:T(8,128)S(1)}, f32[8,64,512]{2,1,0:T(8,128)S(1)}, u32[]{:S(2)}, u32[]{:S(2)}) %collective-permute-start.18) | collective-permute-done | bytes 1048608 | tf_op jit(solution)/shard_map/ppermute | solution.py:26
  96.1 0.2 add.262
  96.3 0.1 collective-permute-start.19
  96.4 0.4 collective-permute-start.27
  96.7 3.2 %collective-permute-done.25 = f32[8,64,512]{2,1,0:T(8,128)S(1)} collective-permute-done((f32[8,64,512]{2,1,0:T(8,128)S(1)}, f32[8,64,512]{2,1,0:T(8,128)S(1)}, u32[]{:S(2)}, u32[]{:S(2)}) %collective-permute-start.25) | collective-permute-done | bytes 1048608 | tf_op jit(solution)/shard_map/ppermute | solution.py:26
  100.0 0.2 add.271
  100.2 3.2 %collective-permute-start.26 = (f32[8,64,512]{2,1,0:T(8,128)S(1)}, f32[8,64,512]{2,1,0:T(8,128)S(1)}, u32[]{:S(2)}, u32[]{:S(2)}) collective-permute-start(f32[8,64,512]{2,1,0:T(8,128)S(1)} %add.271), channel_id=1, source_target_pairs={{0,12},{1,13},{2,14},{3,15},{4,0},{5,1},{6,2},{7,3},{8,4},{9,5},{1... | collective-permute-start | bytes 3145736 | tf_op jit(solution)/shard_map/ppermute | solution.py:26
  103.4 7.8 %collective-permute-done.20 = f32[8,64,512]{2,1,0:T(8,128)S(1)} collective-permute-done((f32[8,64,512]{2,1,0:T(8,128)S(1)}, f32[8,64,512]{2,1,0:T(8,128)S(1)}, u32[]{:S(2)}, u32[]{:S(2)}) %collective-permute-start.20) | collective-permute-done | bytes 1048608 | tf_op jit(solution)/shard_map/ppermute | solution.py:26
  111.2 0.3 collective-permute-done.19
  111.5 0.3 slice_add_fusion.8
  111.9 3.6 %collective-permute-start.21 = (f32[2,64,512]{2,1,0:T(8,128)S(1)}, f32[2,64,512]{2,1,0:T(8,128)S(1)}, u32[]{:S(2)}, u32[]{:S(2)}) collective-permute-start(f32[2,64,512]{2,1,0:T(8,128)S(1)} %get-tuple-element.53), channel_id=1, source_target_pairs={{0,1},{1,2},{2,3},{3,0},{4,5},{5,6},{6,7},{7,4},{8,9},{9,10},{10,1... | collective-permute-start | bytes 786440 | tf_op jit(solution)/shard_map/ppermute | solution.py:26
  115.4 0.2 collective-permute-start.22
  115.6 2.3 %collective-permute-start.23 = (f32[2,64,512]{2,1,0:T(8,128)S(1)}, f32[2,64,512]{2,1,0:T(8,128)S(1)}, u32[]{:S(2)}, u32[]{:S(2)}) collective-permute-start(f32[2,64,512]{2,1,0:T(8,128)S(1)} %get-tuple-element.51), channel_id=1, source_target_pairs={{0,3},{1,0},{2,1},{3,2},{4,7},{5,4},{6,5},{7,6},{8,11},{9,8},{10,9... | collective-permute-start | bytes 786440 | tf_op jit(solution)/shard_map/ppermute | solution.py:26
  117.9 5.0 %collective-permute-done.27 = f32[8,64,512]{2,1,0:T(8,128)S(1)} collective-permute-done((f32[8,64,512]{2,1,0:T(8,128)S(1)}, f32[8,64,512]{2,1,0:T(8,128)S(1)}, u32[]{:S(2)}, u32[]{:S(2)}) %collective-permute-start.27) | collective-permute-done | bytes 1048608 | tf_op jit(solution)/shard_map/ppermute | solution.py:26
  122.9 0.3 slice_add_fusion
  123.2 9.9 %collective-permute-start.28 = (f32[2,64,512]{2,1,0:T(8,128)S(1)}, f32[2,64,512]{2,1,0:T(8,128)S(1)}, u32[]{:S(2)}, u32[]{:S(2)}) collective-permute-start(f32[2,64,512]{2,1,0:T(8,128)S(1)} %get-tuple-element.50), channel_id=1, source_target_pairs={{0,16},{1,17},{2,18},{3,19},{4,20},{5,21},{6,22},{7,23},{8,24},{9,... | collective-permute-start | bytes 786440 | tf_op jit(solution)/shard_map/ppermute | solution.py:26
  133.2 4.3 %collective-permute-start.31 = (f32[2,64,512]{2,1,0:T(8,128)S(1)}, f32[2,64,512]{2,1,0:T(8,128)S(1)}, u32[]{:S(2)}, u32[]{:S(2)}) collective-permute-start(f32[2,64,512]{2,1,0:T(8,128)S(1)} %get-tuple-element.47), channel_id=1, source_target_pairs={{0,19},{1,16},{2,17},{3,18},{4,23},{5,20},{6,21},{7,22},{8,27},{9,... | collective-permute-start | bytes 786440 | tf_op jit(solution)/shard_map/ppermute | solution.py:26
  137.5 4.6 %collective-permute-done.29.refs_5_ = f32[2,64,512]{2,1,0:T(8,128)S(1)} collective-permute-done((f32[2,64,512]{2,1,0:T(8,128)S(1)}, f32[2,64,512]{2,1,0:T(8,128)S(1)}, u32[]{:S(2)}, u32[]{:S(2)}) %collective-permute-start.29) | collective-permute-done | bytes 262176 | tf_op jit(solution)/shard_map/ppermute | solution.py:26
  142.1 4.0 %collective-permute-done.30.refs_6_ = f32[2,64,512]{2,1,0:T(8,128)S(1)} collective-permute-done((f32[2,64,512]{2,1,0:T(8,128)S(1)}, f32[2,64,512]{2,1,0:T(8,128)S(1)}, u32[]{:S(2)}, u32[]{:S(2)}) %collective-permute-start.30) | collective-permute-done | bytes 262176 | tf_op jit(solution)/shard_map/ppermute | solution.py:26
  146.1 2.6 %join.1 = f32[1,2,512,512]{3,2,1,0:T(8,128)} custom-call(s32[3]{0:T(128)S(1)} %pad_add_fusion.at_ref, f32[2,64,512]{2,1,0:T(8,128)S(1)} %get-tuple-element.54.refs_0_, f32[2,64,512]{2,1,0:T(8,128)S(1)} %collective-permute-done.21.refs_1_, f32[2,64,512]{2,1,0:T(8,128)S(1)} %collective-permute-done.22.refs_2_, ...), custom_call_target="tpu_custom_call" | custom-call | flops 1000000 | bytes 4194304 | tf_op jit(solution)/shard_map/join/pallas_call | solution.py:201
  (27 shorter events, 0.1 us)
Async XLA Ops:
  0.0 19.0 %copy-start.2 = (s32[16,16]{1,0:T(8,128)S(1)}, s32[16,16]{1,0:T(8,128)}, u32[]{:S(2)}) copy-start(s32[16,16]{1,0:T(8,128)} %param.3) | copy-start | bytes 3076
  0.0 3.4 %collective-permute-start.2 = (f32[1024,256]{1,0:T(8,128)}, f32[1024,256]{1,0:T(8,128)S(1)}, u32[]{:S(2)}, u32[]{:S(2)}) collective-permute-start(f32[1024,256]{1,0:T(8,128)} %refs_0_.1), channel_id=1, source_target_pairs={{0,16},{16,0},{1,17},{17,1},{2,18},{18,2},{3,19},{19,3},{4,20},{20... | collective-permute-start | bytes 3145736 | tf_op jit(solution)/shard_map/ppermute | solution.py:42
  0.7 15.5 %collective-permute-start = (f32[1024,256]{1,0:T(8,128)}, f32[1024,256]{1,0:T(8,128)}, u32[]{:S(2)}, u32[]{:S(2)}) collective-permute-start(f32[1024,256]{1,0:T(8,128)} %refs_0_.1), channel_id=1, source_target_pairs={{0,1},{1,2},{2,3},{3,0},{4,5},{5,6},{6,7},{7,4},{8,9},{9,10},{10,1... | collective-permute-start | bytes 3145736 | tf_op jit(solution)/shard_map/ppermute | solution.py:26
  2.0 15.7 %collective-permute-start.15 = (f32[1024,256]{1,0:T(8,128)}, f32[1024,256]{1,0:T(8,128)}, u32[]{:S(2)}, u32[]{:S(2)}) collective-permute-start(f32[1024,256]{1,0:T(8,128)} %refs_0_.1), channel_id=1, source_target_pairs={{0,3},{1,0},{2,1},{3,2},{4,7},{5,4},{6,5},{7,6},{8,11},{9,8},{10,9... | collective-permute-start | bytes 3145736 | tf_op jit(solution)/shard_map/ppermute | solution.py:26
  3.4 38.8 %collective-permute-start.16 = (f32[1024,256]{1,0:T(8,128)S(1)}, f32[1024,256]{1,0:T(8,128)}, u32[]{:S(2)}, u32[]{:S(2)}) collective-permute-start(f32[1024,256]{1,0:T(8,128)S(1)} %collective-permute-done.2.slab_ref.refs_1_), channel_id=1, source_target_pairs={{0,3},{1,0},{2,1},{3,2},{4,7},{5,4},{6,5},{7,6},{8,11},{9,8},{10,9... | collective-permute-start | bytes 3145736 | tf_op jit(solution)/shard_map/ppermute | solution.py:26
  6.0 1.2 copy-start
  7.2 39.9 %copy-start.1 = (f32[1024,256]{1,0:T(8,128)S(1)}, f32[1024,256]{1,0:T(8,128)}, u32[]{:S(2)}) copy-start(f32[1024,256]{1,0:T(8,128)} %refs_0_.1) | copy-start | bytes 3145732
  8.4 10.8 %collective-permute-start.7 = (f32[256,256]{1,0:T(8,128)S(1)}, f32[256,256]{1,0:T(8,128)}, u32[]{:S(2)}, u32[]{:S(2)}) collective-permute-start(f32[256,256]{1,0:T(8,128)S(1)} %get-tuple-element.31.refs_2_), channel_id=1, source_target_pairs={{0,32},{32,64},{64,96},{1,33},{33,65},{65,97},{2,34},{34,66},{66,9... | collective-permute-start | bytes 786440 | tf_op jit(solution)/shard_map/ppermute | solution.py:46
  9.7 10.8 %collective-permute-start.11 = (f32[256,256]{1,0:T(8,128)S(1)}, f32[256,256]{1,0:T(8,128)}, u32[]{:S(2)}, u32[]{:S(2)}) collective-permute-start(f32[256,256]{1,0:T(8,128)S(1)} %get-tuple-element.33), channel_id=1, source_target_pairs={{0,1},{1,2},{2,3},{3,0},{4,5},{5,6},{6,7},{7,4},{8,9},{9,10},{10,1... | collective-permute-start | bytes 786440 | tf_op jit(solution)/shard_map/ppermute | solution.py:26
  16.2 14.1 %collective-permute-start.12 = (f32[256,256]{1,0:T(8,128)S(1)}, f32[256,256]{1,0:T(8,128)}, u32[]{:S(2)}, u32[]{:S(2)}) collective-permute-start(f32[256,256]{1,0:T(8,128)S(1)} %get-tuple-element.34), channel_id=1, source_target_pairs={{0,3},{1,0},{2,1},{3,2},{4,7},{5,4},{6,5},{7,6},{8,11},{9,8},{10,9... | collective-permute-start | bytes 786440 | tf_op jit(solution)/shard_map/ppermute | solution.py:26
  17.7 7.0 %collective-permute-start.3 = (f32[256,256]{1,0:T(8,128)S(1)}, f32[256,256]{1,0:T(8,128)S(1)}, u32[]{:S(2)}, u32[]{:S(2)}) collective-permute-start(f32[256,256]{1,0:T(8,128)S(1)} %get-tuple-element.30), channel_id=1, source_target_pairs={{0,2},{1,3},{2,0},{3,1},{4,6},{5,7},{6,4},{7,5},{8,10},{9,11},{10,... | collective-permute-start | bytes 786440 | tf_op jit(solution)/shard_map/ppermute | solution.py:26
  19.2 14.4 %collective-permute-start.8 = (f32[256,256]{1,0:T(8,128)S(1)}, f32[256,256]{1,0:T(8,128)S(1)}, u32[]{:S(2)}, u32[]{:S(2)}) collective-permute-start(f32[256,256]{1,0:T(8,128)S(1)} %get-tuple-element.31.refs_2_), channel_id=1, source_target_pairs={{0,96},{32,0},{1,97},{33,1},{2,98},{34,2},{3,99},{35,3},{4,100},{3... | collective-permute-start | bytes 786440 | tf_op jit(solution)/shard_map/ppermute | solution.py:46
  20.5 37.7 %collective-permute-start.10 = (f32[1024,256]{1,0:T(8,128)S(1)}, f32[1024,256]{1,0:T(8,128)S(1)}, u32[]{:S(2)}, u32[]{:S(2)}) collective-permute-start(f32[1024,256]{1,0:T(8,128)S(1)} %collective-permute-done.2.slab_ref.refs_1_), channel_id=1, source_target_pairs={{0,1},{1,2},{2,3},{3,0},{4,5},{5,6},{6,7},{7,4},{8,9},{9,10},{10,1... | collective-permute-start | bytes 3145736 | tf_op jit(solution)/shard_map/ppermute | solution.py:26
  24.7 14.9 %collective-permute-start.5 = (f32[256,256]{1,0:T(8,128)S(1)}, f32[256,256]{1,0:T(8,128)S(1)}, u32[]{:S(2)}, u32[]{:S(2)}) collective-permute-start(f32[256,256]{1,0:T(8,128)S(1)} %collective-permute-done.3.refs_1_), channel_id=1, source_target_pairs={{0,96},{32,0},{1,97},{33,1},{2,98},{34,2},{3,99},{35,3},{4,100},{3... | collective-permute-start | bytes 786440 | tf_op jit(solution)/shard_map/ppermute | solution.py:46
  30.3 10.6 %collective-permute-start.4 = (f32[256,256]{1,0:T(8,128)S(1)}, f32[256,256]{1,0:T(8,128)S(1)}, u32[]{:S(2)}, u32[]{:S(2)}) collective-permute-start(f32[256,256]{1,0:T(8,128)S(1)} %collective-permute-done.3.refs_1_), channel_id=1, source_target_pairs={{0,32},{32,64},{64,96},{1,33},{33,65},{65,97},{2,34},{34,66},{66,9... | collective-permute-start | bytes 786440 | tf_op jit(solution)/shard_map/ppermute | solution.py:46
  33.5 33.7 %collective-permute-start.1 = (f32[1024,256]{1,0:T(8,128)}, f32[1024,256]{1,0:T(8,128)S(1)}, u32[]{:S(2)}, u32[]{:S(2)}) collective-permute-start(f32[1024,256]{1,0:T(8,128)} %collective-permute-done.refs_0_), channel_id=1, source_target_pairs={{0,1},{1,2},{2,3},{3,0},{4,5},{5,6},{6,7},{7,4},{8,9},{9,10},{10,1... | collective-permute-start | bytes 3145736 | tf_op jit(solution)/shard_map/ppermute | solution.py:26
  39.6 13.5 %collective-permute-start.13 = (f32[512,256]{1,0:T(8,128)S(1)}, f32[512,256]{1,0:T(8,128)S(1)}, u32[]{:S(2)}, u32[]{:S(2)}) collective-permute-start(f32[512,256]{1,0:T(8,128)S(1)} %constant_dynamic-update-slice_fusion.refs_2_.refs_7_), channel_id=1, source_target_pairs={{0,32},{32,64},{64,96},{1,33},{33,65},{65,97},{2,34},{34,66},{66,9... | collective-permute-start | bytes 1572872 | tf_op jit(solution)/shard_map/ppermute | solution.py:46
  40.9 15.3 %collective-permute-start.14 = (f32[512,256]{1,0:T(8,128)S(1)}, f32[512,256]{1,0:T(8,128)S(1)}, u32[]{:S(2)}, u32[]{:S(2)}) collective-permute-start(f32[512,256]{1,0:T(8,128)S(1)} %constant_dynamic-update-slice_fusion.refs_2_.refs_7_), channel_id=1, source_target_pairs={{0,96},{1,97},{2,98},{3,99},{4,100},{5,101},{6,102},{7,103},{8,104... | collective-permute-start | bytes 1572872 | tf_op jit(solution)/shard_map/ppermute | solution.py:46
  42.2 37.1 %collective-permute-start.24 = (f32[1024,256]{1,0:T(8,128)}, f32[1024,256]{1,0:T(8,128)S(1)}, u32[]{:S(2)}, u32[]{:S(2)}) collective-permute-start(f32[1024,256]{1,0:T(8,128)} %collective-permute-done.16.refs_6_), channel_id=1, source_target_pairs={{0,3},{1,0},{2,1},{3,2},{4,7},{5,4},{6,5},{7,6},{8,11},{9,8},{10,9... | collective-permute-start | bytes 3145736 | tf_op jit(solution)/shard_map/ppermute | solution.py:26
  53.1 14.1 %collective-permute-start.9 = (f32[256,256]{1,0:T(8,128)S(1)}, f32[256,256]{1,0:T(8,128)S(1)}, u32[]{:S(2)}, u32[]{:S(2)}) collective-permute-start(f32[256,256]{1,0:T(8,128)S(1)} %collective-permute-done.8.refs_4_), channel_id=1, source_target_pairs={{0,96},{96,64},{1,97},{97,65},{2,98},{98,66},{3,99},{99,67},{4,100... | collective-permute-start | bytes 786440 | tf_op jit(solution)/shard_map/ppermute | solution.py:46
  56.2 11.0 %collective-permute-start.6 = (f32[256,256]{1,0:T(8,128)S(1)}, f32[256,256]{1,0:T(8,128)S(1)}, u32[]{:S(2)}, u32[]{:S(2)}) collective-permute-start(f32[256,256]{1,0:T(8,128)S(1)} %collective-permute-done.5.refs_3_), channel_id=1, source_target_pairs={{0,96},{96,64},{1,97},{97,65},{2,98},{98,66},{3,99},{99,67},{4,100... | collective-permute-start | bytes 786440 | tf_op jit(solution)/shard_map/ppermute | solution.py:46
  58.2 11.5 %collective-permute-start.17 = (f32[512,256]{1,0:T(8,128)S(1)}, f32[512,256]{1,0:T(8,128)S(1)}, u32[]{:S(2)}, u32[]{:S(2)}) collective-permute-start(f32[512,256]{1,0:T(8,128)S(1)} %collective-permute-done.13.refs_3_.refs_8_), channel_id=1, source_target_pairs={{32,64},{64,96},{33,65},{65,97},{34,66},{66,98},{35,67},{67,99},{3... | collective-permute-start | bytes 1572872 | tf_op jit(solution)/shard_map/ppermute | solution.py:46
  73.9 22.2 %collective-permute-start.18 = (f32[8,64,512]{2,1,0:T(8,128)S(1)}, f32[8,64,512]{2,1,0:T(8,128)S(1)}, u32[]{:S(2)}, u32[]{:S(2)}) collective-permute-start(f32[8,64,512]{2,1,0:T(8,128)S(1)} %get-tuple-element.41), channel_id=1, source_target_pairs={{0,4},{1,5},{2,6},{3,7},{4,8},{5,9},{6,10},{7,11},{8,12},{9,13},{1... | collective-permute-start | bytes 3145736 | tf_op jit(solution)/shard_map/ppermute | solution.py:26
  83.6 16.3 %collective-permute-start.25 = (f32[8,64,512]{2,1,0:T(8,128)S(1)}, f32[8,64,512]{2,1,0:T(8,128)S(1)}, u32[]{:S(2)}, u32[]{:S(2)}) collective-permute-start(f32[8,64,512]{2,1,0:T(8,128)S(1)} %get-tuple-element.45), channel_id=1, source_target_pairs={{0,12},{1,13},{2,14},{3,15},{4,0},{5,1},{6,2},{7,3},{8,4},{9,5},{1... | collective-permute-start | bytes 3145736 | tf_op jit(solution)/shard_map/ppermute | solution.py:26
  88.2 23.0 %collective-permute-start.20 = (f32[8,64,512]{2,1,0:T(8,128)S(1)}, f32[8,64,512]{2,1,0:T(8,128)S(1)}, u32[]{:S(2)}, u32[]{:S(2)}) collective-permute-start(f32[8,64,512]{2,1,0:T(8,128)S(1)} %get-tuple-element.42), channel_id=1, source_target_pairs={{0,12},{1,13},{2,14},{3,15},{4,0},{5,1},{6,2},{7,3},{8,4},{9,5},{1... | collective-permute-start | bytes 3145736 | tf_op jit(solution)/shard_map/ppermute | solution.py:26
  96.3 15.2 %collective-permute-start.19 = (f32[8,64,512]{2,1,0:T(8,128)S(1)}, f32[8,64,512]{2,1,0:T(8,128)S(1)}, u32[]{:S(2)}, u32[]{:S(2)}) collective-permute-start(f32[8,64,512]{2,1,0:T(8,128)S(1)} %add.262), channel_id=1, source_target_pairs={{0,4},{1,5},{2,6},{3,7},{4,8},{5,9},{6,10},{7,11},{8,12},{9,13},{1... | collective-permute-start | bytes 3145736 | tf_op jit(solution)/shard_map/ppermute | solution.py:26
  96.4 26.5 %collective-permute-start.27 = (f32[8,64,512]{2,1,0:T(8,128)S(1)}, f32[8,64,512]{2,1,0:T(8,128)S(1)}, u32[]{:S(2)}, u32[]{:S(2)}) collective-permute-start(f32[8,64,512]{2,1,0:T(8,128)S(1)} %get-tuple-element.46), channel_id=1, source_target_pairs={{0,4},{1,5},{2,6},{3,7},{4,8},{5,9},{6,10},{7,11},{8,12},{9,13},{1... | collective-permute-start | bytes 3145736 | tf_op jit(solution)/shard_map/ppermute | solution.py:26
  100.2 22.7 %collective-permute-start.26 = (f32[8,64,512]{2,1,0:T(8,128)S(1)}, f32[8,64,512]{2,1,0:T(8,128)S(1)}, u32[]{:S(2)}, u32[]{:S(2)}) collective-permute-start(f32[8,64,512]{2,1,0:T(8,128)S(1)} %add.271), channel_id=1, source_target_pairs={{0,12},{1,13},{2,14},{3,15},{4,0},{5,1},{6,2},{7,3},{8,4},{9,5},{1... | collective-permute-start | bytes 3145736 | tf_op jit(solution)/shard_map/ppermute | solution.py:26
  111.9 21.3 %collective-permute-start.21 = (f32[2,64,512]{2,1,0:T(8,128)S(1)}, f32[2,64,512]{2,1,0:T(8,128)S(1)}, u32[]{:S(2)}, u32[]{:S(2)}) collective-permute-start(f32[2,64,512]{2,1,0:T(8,128)S(1)} %get-tuple-element.53), channel_id=1, source_target_pairs={{0,1},{1,2},{2,3},{3,0},{4,5},{5,6},{6,7},{7,4},{8,9},{9,10},{10,1... | collective-permute-start | bytes 786440 | tf_op jit(solution)/shard_map/ppermute | solution.py:26
  115.4 17.7 %collective-permute-start.22 = (f32[2,64,512]{2,1,0:T(8,128)S(1)}, f32[2,64,512]{2,1,0:T(8,128)S(1)}, u32[]{:S(2)}, u32[]{:S(2)}) collective-permute-start(f32[2,64,512]{2,1,0:T(8,128)S(1)} %get-tuple-element.52), channel_id=1, source_target_pairs={{0,2},{1,3},{2,0},{3,1},{4,6},{5,7},{6,4},{7,5},{8,10},{9,11},{10,... | collective-permute-start | bytes 786440 | tf_op jit(solution)/shard_map/ppermute | solution.py:26
  115.6 21.9 %collective-permute-start.23 = (f32[2,64,512]{2,1,0:T(8,128)S(1)}, f32[2,64,512]{2,1,0:T(8,128)S(1)}, u32[]{:S(2)}, u32[]{:S(2)}) collective-permute-start(f32[2,64,512]{2,1,0:T(8,128)S(1)} %get-tuple-element.51), channel_id=1, source_target_pairs={{0,3},{1,0},{2,1},{3,2},{4,7},{5,4},{6,5},{7,6},{8,11},{9,8},{10,9... | collective-permute-start | bytes 786440 | tf_op jit(solution)/shard_map/ppermute | solution.py:26
  123.2 14.3 %collective-permute-start.28 = (f32[2,64,512]{2,1,0:T(8,128)S(1)}, f32[2,64,512]{2,1,0:T(8,128)S(1)}, u32[]{:S(2)}, u32[]{:S(2)}) collective-permute-start(f32[2,64,512]{2,1,0:T(8,128)S(1)} %get-tuple-element.50), channel_id=1, source_target_pairs={{0,16},{1,17},{2,18},{3,19},{4,20},{5,21},{6,22},{7,23},{8,24},{9,... | collective-permute-start | bytes 786440 | tf_op jit(solution)/shard_map/ppermute | solution.py:26
  133.2 9.0 %collective-permute-start.29 = (f32[2,64,512]{2,1,0:T(8,128)S(1)}, f32[2,64,512]{2,1,0:T(8,128)S(1)}, u32[]{:S(2)}, u32[]{:S(2)}) collective-permute-start(f32[2,64,512]{2,1,0:T(8,128)S(1)} %get-tuple-element.49), channel_id=1, source_target_pairs={{0,17},{1,18},{2,19},{3,16},{4,21},{5,22},{6,23},{7,20},{8,25},{9,... | collective-permute-start | bytes 786440 | tf_op jit(solution)/shard_map/ppermute | solution.py:26
  133.2 13.0 %collective-permute-start.30 = (f32[2,64,512]{2,1,0:T(8,128)S(1)}, f32[2,64,512]{2,1,0:T(8,128)S(1)}, u32[]{:S(2)}, u32[]{:S(2)}) collective-permute-start(f32[2,64,512]{2,1,0:T(8,128)S(1)} %get-tuple-element.48), channel_id=1, source_target_pairs={{0,18},{1,19},{2,16},{3,17},{4,22},{5,23},{6,20},{7,21},{8,26},{9,... | collective-permute-start | bytes 786440 | tf_op jit(solution)/shard_map/ppermute | solution.py:26
  133.2 13.0 %collective-permute-start.31 = (f32[2,64,512]{2,1,0:T(8,128)S(1)}, f32[2,64,512]{2,1,0:T(8,128)S(1)}, u32[]{:S(2)}, u32[]{:S(2)}) collective-permute-start(f32[2,64,512]{2,1,0:T(8,128)S(1)} %get-tuple-element.47), channel_id=1, source_target_pairs={{0,19},{1,16},{2,17},{3,18},{4,23},{5,20},{6,21},{7,22},{8,27},{9,... | collective-permute-start | bytes 786440 | tf_op jit(solution)/shard_map/ppermute | solution.py:26

commit v2 on v1

--- a/solution.py
+++ b/solution.py
@@ -244,15 +244,15 @@
 
     onward, wrap = [(0, 1), (1, 2), (2, 3)], [(0, 3)]
     both = jnp.concatenate([small[0], small[2]])
-    a1, a3 = hop(first, onward), hop(first, wrap + [(1, 0)])
+    a1, a3 = hop(first, onward), hop(first, wrap)
     b1, b3 = hop(both, onward), hop(both, wrap)
-    c1, c3 = hop(small[1], onward), hop(small[1], wrap + [(1, 0)])
-    a2, c2 = hop(a3, wrap + [(3, 2)]), hop(c3, wrap + [(3, 2)])
+    c1, c3 = hop(small[1], onward), hop(small[1], wrap)
+    d2 = hop(jnp.concatenate([first, small[1]]), [(0, 2), (1, 3)])
     b2 = hop(b1, onward[1:])
 
     wide = first.shape[0]
     low, high = [(v, 0) for v in (both, b1, b3, b2)], [(v, wide) for v in (both, b1, b3, b2)]
-    zero, far = [(v, 0) for v in (first, a1, a3, a2)], [(v, 0) for v in (small[1], c1, c3, c2)]
+    zero, far = [(first, 0), (a1, 0), (a3, 0), (d2, 0)], [(small[1], 0), (c1, 0), (c3, 0), (d2, wide)]
     three, four = range(3), range(4)
     total, own_parts = product(tab, [((panel, other), dict(zip(three, zero)))], None, (0, 1), ())
     total, up_parts, down_parts = product(

time: 149 us -> 153 us (1.027)
  the two profiles are of different devices: /device:TPU:7 before, /device:TPU:1 now
where the time goes in v2:
time: 153 us; the launch traced here: 152 us
  starting transfers between devices  74.1 us (48%)
  waiting for transfers between devices  50 us (33%)
  Pallas kernels  23.2 us (15%)
  local copies, waits for them, and re-layouts  3.17 us (2%)
    ppermute x22, starting transfers between devices, move(): return lax.ppermute(value, ('c', 'y', 'z'), pairs)  52.2 us
    ppermute x22, waiting for transfers between devices, move(): return lax.ppermute(value, ('c', 'y', 'z'), pairs)  43.2 us
    ppermute x8, starting transfers between devices, hop(): return lax.ppermute(value, 'x', pairs)  20.5 us
    pallas_call x4, Pallas kernels, product(): pl.pallas_call(functools.partial(product_kernel, q, form, total is not No...  19.4 us
    ppermute x8, waiting for transfers between devices, hop(): return lax.ppermute(value, 'x', pairs)  6.8 us
  transfers between devices with their start and end apart: 31, of which 9 were waited for; matrix products, arithmetic and copies ran while one was open for 2% of the time, Pallas kernels for 14%

profile of v2, /device:TPU:1, one launch (start us, length us, event | category | flops | bytes accessed | tf_op | source)
XLA Modules:
  0.0 152.3 jit_solution(14863806928439226895)
XLA Ops:
  0.0 1.4 collective-permute-start.2
  1.4 1.4 collective-permute-start
  2.8 1.4 collective-permute-start.14
  4.2 0.0 collective-permute-done.2.slab_ref.refs_1_
  4.3 2.5 %collective-permute-start.15 = (f32[1024,256]{1,0:T(8,128)S(1)}, f32[1024,256]{1,0:T(8,128)}, u32[]{:S(2)}, u32[]{:S(2)}) collective-permute-start(f32[1024,256]{1,0:T(8,128)S(1)} %collective-permute-done.2.slab_ref.refs_1_), channel_id=1, source_target_pairs={{0,3},{1,0},{2,1},{3,2},{4,7},{5,4},{6,5},{7,6},{8,11},{9,8},{10,9... | collective-permute-start | bytes 3145736 | tf_op jit(solution)/shard_map/ppermute | solution.py:26
  6.7 0.1 pad_add_fusion.at_ref
  6.8 1.2 copy-done
  8.0 0.6 cut.2
  8.6 0.6 cut.3
  9.2 0.1 collective-permute-start.10
  9.3 2.7 %collective-permute-start.11 = (f32[256,256]{1,0:T(8,128)S(1)}, f32[256,256]{1,0:T(8,128)}, u32[]{:S(2)}, u32[]{:S(2)}) collective-permute-start(f32[256,256]{1,0:T(8,128)S(1)} %get-tuple-element.34), channel_id=1, source_target_pairs={{0,3},{1,0},{2,1},{3,2},{4,7},{5,4},{6,5},{7,6},{8,11},{9,8},{10,9... | collective-permute-start | bytes 786440 | tf_op jit(solution)/shard_map/ppermute | solution.py:26
  12.0 5.1 %collective-permute-done.refs_0_ = f32[1024,256]{1,0:T(8,128)} collective-permute-done((f32[1024,256]{1,0:T(8,128)}, f32[1024,256]{1,0:T(8,128)}, u32[]{:S(2)}, u32[]{:S(2)}) %collective-permute-start) | collective-permute-done | bytes 1048608 | tf_op jit(solution)/shard_map/ppermute | solution.py:26
  17.0 1.6 %collective-permute-start.3 = (f32[256,256]{1,0:T(8,128)S(1)}, f32[256,256]{1,0:T(8,128)S(1)}, u32[]{:S(2)}, u32[]{:S(2)}) collective-permute-start(f32[256,256]{1,0:T(8,128)S(1)} %get-tuple-element.30), channel_id=1, source_target_pairs={{0,2},{1,3},{2,0},{3,1},{4,6},{5,7},{6,4},{7,5},{8,10},{9,11},{10,... | collective-permute-start | bytes 786440 | tf_op jit(solution)/shard_map/ppermute | solution.py:26
  18.7 0.1 broadcast_select_fusion
  18.8 0.2 select_reduce_fusion
  19.0 0.0 collective-permute-done.14.refs_5_
  19.0 3.1 %collective-permute-start.7 = (f32[256,256]{1,0:T(8,128)S(1)}, f32[256,256]{1,0:T(8,128)S(1)}, u32[]{:S(2)}, u32[]{:S(2)}) collective-permute-start(f32[256,256]{1,0:T(8,128)S(1)} %get-tuple-element.31.refs_2_), channel_id=1, source_target_pairs={{0,32},{32,64},{64,96},{1,33},{33,65},{65,97},{2,34},{34,66},{66,9... | collective-permute-start | bytes 786440 | tf_op jit(solution)/shard_map/ppermute | solution.py:46
  22.1 0.0 collective-permute-done.10
  22.1 2.6 %collective-permute-start.8 = (f32[256,256]{1,0:T(8,128)S(1)}, f32[256,256]{1,0:T(8,128)S(1)}, u32[]{:S(2)}, u32[]{:S(2)}) collective-permute-start(f32[256,256]{1,0:T(8,128)S(1)} %get-tuple-element.31.refs_2_), channel_id=1, source_target_pairs={{0,96},{1,97},{2,98},{3,99},{4,100},{5,101},{6,102},{7,103},{8,104... | collective-permute-start | bytes 786440 | tf_op jit(solution)/shard_map/ppermute | solution.py:46
  24.7 6.4 %collective-permute-done.11 = f32[256,256]{1,0:T(8,128)} collective-permute-done((f32[256,256]{1,0:T(8,128)S(1)}, f32[256,256]{1,0:T(8,128)}, u32[]{:S(2)}, u32[]{:S(2)}) %collective-permute-start.11) | collective-permute-done | bytes 262176 | tf_op jit(solution)/shard_map/ppermute | solution.py:26
  31.1 1.3 collective-permute-start.9
  32.4 0.0 collective-permute-done.3.refs_1_
  32.4 3.1 %collective-permute-start.4 = (f32[256,256]{1,0:T(8,128)S(1)}, f32[256,256]{1,0:T(8,128)S(1)}, u32[]{:S(2)}, u32[]{:S(2)}) collective-permute-start(f32[256,256]{1,0:T(8,128)S(1)} %collective-permute-done.3.refs_1_), channel_id=1, source_target_pairs={{0,32},{32,64},{64,96},{1,33},{33,65},{65,97},{2,34},{34,66},{66,9... | collective-permute-start | bytes 786440 | tf_op jit(solution)/shard_map/ppermute | solution.py:46
  35.5 1.0 constant_dynamic-update-slice_fusion.1
  36.5 1.0 constant_dynamic-update-slice_fusion.refs_2_.refs_7_
  37.5 0.0 collective-permute-done.7.refs_3_
  37.5 3.2 %collective-permute-start.1 = (f32[1024,256]{1,0:T(8,128)}, f32[1024,256]{1,0:T(8,128)S(1)}, u32[]{:S(2)}, u32[]{:S(2)}) collective-permute-start(f32[1024,256]{1,0:T(8,128)} %collective-permute-done.refs_0_), channel_id=1, source_target_pairs={{0,1},{1,2},{2,3},{3,0},{4,5},{5,6},{6,7},{7,4},{8,9},{9,10},{10,1... | collective-permute-start | bytes 3145736 | tf_op jit(solution)/shard_map/ppermute | solution.py:26
  40.7 3.1 %collective-permute-start.12 = (f32[512,256]{1,0:T(8,128)S(1)}, f32[512,256]{1,0:T(8,128)S(1)}, u32[]{:S(2)}, u32[]{:S(2)}) collective-permute-start(f32[512,256]{1,0:T(8,128)S(1)} %constant_dynamic-update-slice_fusion.refs_2_.refs_7_), channel_id=1, source_target_pairs={{0,32},{32,64},{64,96},{1,33},{33,65},{65,97},{2,34},{34,66},{66,9... | collective-permute-start | bytes 1572872 | tf_op jit(solution)/shard_map/ppermute | solution.py:46
  43.8 1.3 collective-permute-start.13
  45.2 0.0 collective-permute-done.15.refs_6_
  45.2 3.8 %collective-permute-start.23 = (f32[1024,256]{1,0:T(8,128)}, f32[1024,256]{1,0:T(8,128)S(1)}, u32[]{:S(2)}, u32[]{:S(2)}) collective-permute-start(f32[1024,256]{1,0:T(8,128)} %collective-permute-done.15.refs_6_), channel_id=1, source_target_pairs={{0,3},{1,0},{2,1},{3,2},{4,7},{5,4},{6,5},{7,6},{8,11},{9,8},{10,9... | collective-permute-start | bytes 3145736 | tf_op jit(solution)/shard_map/ppermute | solution.py:26
  48.9 3.3 %shard_map.28 = (f32[8,768,256]{2,1,0:T(8,128)S(1)}, bf16[2048,512]{1,0:T(8,128)(2,1)S(1)}) custom-call(s32[64]{0:T(128)S(1)} %broadcast_add_fusion.2.tab_ref, f32[1024,256]{1,0:T(8,128)S(1)} %copy-done.1, f32[1024,256]{1,0:T(8,128)S(1)} %collective-permute-done.2.slab_ref.refs_1_, f32[256,256]{1,0:T(8,128)S(1)} %get-tuple-element.31.refs_2_, ...), custom_call_target="tpu_custom_call" | custom-call | flops 6442450944 | bytes 12582912 | tf_op jit(solution)/shard_map/pallas_call | solution.py:172
  52.3 0.0 collective-permute-done.12.refs_3_.refs_8_
  52.3 5.1 %collective-permute-start.6 = (f32[512,256]{1,0:T(8,128)S(1)}, f32[512,256]{1,0:T(8,128)S(1)}, u32[]{:S(2)}, u32[]{:S(2)}) collective-permute-start(f32[512,256]{1,0:T(8,128)S(1)} %pad_maximum_fusion), channel_id=1, source_target_pairs={{0,64},{32,96},{1,65},{33,97},{2,66},{34,98},{3,67},{35,99},{4,68}... | collective-permute-start | bytes 1572872 | tf_op jit(solution)/shard_map/ppermute | solution.py:46
  57.3 0.0 collective-permute-done.13.refs_4_.refs_9_
  57.4 1.3 collective-permute-start.5
  58.7 0.9 collective-permute-start.16
  59.6 7.6 %shard_map.29 = (f32[8,768,256]{2,1,0:T(8,128)S(1)}, bf16[2048,512]{1,0:T(8,128)(2,1)S(1)}, bf16[2048,512]{1,0:T(8,128)(2,1)S(1)}) custom-call(s32[64]{0:T(128)S(1)} %broadcast_add_fusion.2.tab_ref, f32[1024,256]{1,0:T(8,128)} %collective-permute-done.refs_0_, f32[1024,256]{1,0:T(8,128)S(1)} %collective-permute-done.9.refs_1_, ...), custom_call_target="tpu_custom_call", output_to_operand_aliasing={{0}: (11, {})} | custom-call | flops 6442450944 | bytes 12582912 | tf_op jit(solution)/shard_map/pallas_call | solution.py:172
  67.2 6.8 %collective-permute-done.5.refs_3_ = f32[256,256]{1,0:T(8,128)S(1)} collective-permute-done((f32[256,256]{1,0:T(8,128)S(1)}, f32[256,256]{1,0:T(8,128)S(1)}, u32[]{:S(2)}, u32[]{:S(2)}) %collective-permute-start.5) | collective-permute-done | bytes 262176 | tf_op jit(solution)/shard_map/ppermute | solution.py:46
  74.0 4.3 %shard_map.30 = (f32[8,64,512]{2,1,0:T(8,128)S(1)}, f32[8,64,512]{2,1,0:T(8,128)S(1)}, f32[8,64,512]{2,1,0:T(8,128)S(1)}, f32[8,64,512]{2,1,0:T(8,128)S(1)}) custom-call(s32[64]{0:T(128)S(1)} %broadcast_add_fusion.2.tab_ref, f32[1024,256]{1,0:T(8,128)S(1)} %collective-permute-done.1.refs_0_, f32[256,256]{1,0:T(8,128)S(1)} %collective-permute-done.3.refs_1_, ...), custom_call_target="tpu_custom_call" | custom-call | flops 3221225472 | bytes 12582912 | tf_op jit(solution)/shard_map/pallas_call | solution.py:172
  78.3 2.2 %collective-permute-start.17 = (f32[8,64,512]{2,1,0:T(8,128)S(1)}, f32[8,64,512]{2,1,0:T(8,128)S(1)}, u32[]{:S(2)}, u32[]{:S(2)}) collective-permute-start(f32[8,64,512]{2,1,0:T(8,128)S(1)} %get-tuple-element.41), channel_id=1, source_target_pairs={{0,4},{1,5},{2,6},{3,7},{4,8},{5,9},{6,10},{7,11},{8,12},{9,13},{1... | collective-permute-start | bytes 3145736 | tf_op jit(solution)/shard_map/ppermute | solution.py:26
  80.5 4.3 %shard_map.31 = (f32[8,64,512]{2,1,0:T(8,128)S(1)}, f32[8,64,512]{2,1,0:T(8,128)S(1)}, f32[8,64,512]{2,1,0:T(8,128)S(1)}, f32[8,64,512]{2,1,0:T(8,128)S(1)}) custom-call(s32[64]{0:T(128)S(1)} %broadcast_add_fusion.2.tab_ref, f32[1024,256]{1,0:T(8,128)S(1)} %collective-permute-done.23.refs_0_, f32[256,256]{1,0:T(8,128)S(1)} %collective-permute-done.3.refs_1_, ...), custom_call_target="tpu_custom_call" | custom-call | flops 3221225472 | bytes 12582912 | tf_op jit(solution)/shard_map/pallas_call | solution.py:172
  84.8 4.7 %collective-permute-start.24 = (f32[8,64,512]{2,1,0:T(8,128)S(1)}, f32[8,64,512]{2,1,0:T(8,128)S(1)}, u32[]{:S(2)}, u32[]{:S(2)}) collective-permute-start(f32[8,64,512]{2,1,0:T(8,128)S(1)} %get-tuple-element.45), channel_id=1, source_target_pairs={{0,12},{1,13},{2,14},{3,15},{4,0},{5,1},{6,2},{7,3},{8,4},{9,5},{1... | collective-permute-start | bytes 3145736 | tf_op jit(solution)/shard_map/ppermute | solution.py:26
  89.5 1.4 collective-permute-start.19
  91.0 6.7 %collective-permute-done.17 = f32[8,64,512]{2,1,0:T(8,128)S(1)} collective-permute-done((f32[8,64,512]{2,1,0:T(8,128)S(1)}, f32[8,64,512]{2,1,0:T(8,128)S(1)}, u32[]{:S(2)}, u32[]{:S(2)}) %collective-permute-start.17) | collective-permute-done | bytes 1048608 | tf_op jit(solution)/shard_map/ppermute | solution.py:26
  97.6 0.2 add.262
  97.8 0.1 collective-permute-start.18
  97.9 0.3 collective-permute-start.26
  98.2 3.0 %collective-permute-done.24 = f32[8,64,512]{2,1,0:T(8,128)S(1)} collective-permute-done((f32[8,64,512]{2,1,0:T(8,128)S(1)}, f32[8,64,512]{2,1,0:T(8,128)S(1)}, u32[]{:S(2)}, u32[]{:S(2)}) %collective-permute-start.24) | collective-permute-done | bytes 1048608 | tf_op jit(solution)/shard_map/ppermute | solution.py:26
  101.3 0.2 add.271
  101.5 3.2 %collective-permute-start.25 = (f32[8,64,512]{2,1,0:T(8,128)S(1)}, f32[8,64,512]{2,1,0:T(8,128)S(1)}, u32[]{:S(2)}, u32[]{:S(2)}) collective-permute-start(f32[8,64,512]{2,1,0:T(8,128)S(1)} %add.271), channel_id=1, source_target_pairs={{0,12},{1,13},{2,14},{3,15},{4,0},{5,1},{6,2},{7,3},{8,4},{9,5},{1... | collective-permute-start | bytes 3145736 | tf_op jit(solution)/shard_map/ppermute | solution.py:26
  104.7 7.8 %collective-permute-done.19 = f32[8,64,512]{2,1,0:T(8,128)S(1)} collective-permute-done((f32[8,64,512]{2,1,0:T(8,128)S(1)}, f32[8,64,512]{2,1,0:T(8,128)S(1)}, u32[]{:S(2)}, u32[]{:S(2)}) %collective-permute-start.19) | collective-permute-done | bytes 1048608 | tf_op jit(solution)/shard_map/ppermute | solution.py:26
  112.5 0.6 collective-permute-done.18
  113.1 0.3 slice_add_fusion.8
  113.4 1.6 %collective-permute-start.20 = (f32[2,64,512]{2,1,0:T(8,128)S(1)}, f32[2,64,512]{2,1,0:T(8,128)S(1)}, u32[]{:S(2)}, u32[]{:S(2)}) collective-permute-start(f32[2,64,512]{2,1,0:T(8,128)S(1)} %get-tuple-element.53), channel_id=1, source_target_pairs={{0,1},{1,2},{2,3},{3,0},{4,5},{5,6},{6,7},{7,4},{8,9},{9,10},{10,1... | collective-permute-start | bytes 786440 | tf_op jit(solution)/shard_map/ppermute | solution.py:26
  115.0 1.7 %collective-permute-start.21 = (f32[2,64,512]{2,1,0:T(8,128)S(1)}, f32[2,64,512]{2,1,0:T(8,128)S(1)}, u32[]{:S(2)}, u32[]{:S(2)}) collective-permute-start(f32[2,64,512]{2,1,0:T(8,128)S(1)} %get-tuple-element.52), channel_id=1, source_target_pairs={{0,2},{1,3},{2,0},{3,1},{4,6},{5,7},{6,4},{7,5},{8,10},{9,11},{10,... | collective-permute-start | bytes 786440 | tf_op jit(solution)/shard_map/ppermute | solution.py:26
  116.6 2.0 %collective-permute-start.22 = (f32[2,64,512]{2,1,0:T(8,128)S(1)}, f32[2,64,512]{2,1,0:T(8,128)S(1)}, u32[]{:S(2)}, u32[]{:S(2)}) collective-permute-start(f32[2,64,512]{2,1,0:T(8,128)S(1)} %get-tuple-element.51), channel_id=1, source_target_pairs={{0,3},{1,0},{2,1},{3,2},{4,7},{5,4},{6,5},{7,6},{8,11},{9,8},{10,9... | collective-permute-start | bytes 786440 | tf_op jit(solution)/shard_map/ppermute | solution.py:26
  118.6 5.7 %collective-permute-done.26 = f32[8,64,512]{2,1,0:T(8,128)S(1)} collective-permute-done((f32[8,64,512]{2,1,0:T(8,128)S(1)}, f32[8,64,512]{2,1,0:T(8,128)S(1)}, u32[]{:S(2)}, u32[]{:S(2)}) %collective-permute-start.26) | collective-permute-done | bytes 1048608 | tf_op jit(solution)/shard_map/ppermute | solution.py:26
  124.3 0.3 slice_add_fusion
  124.7 15.2 %collective-permute-start.27 = (f32[2,64,512]{2,1,0:T(8,128)S(1)}, f32[2,64,512]{2,1,0:T(8,128)S(1)}, u32[]{:S(2)}, u32[]{:S(2)}) collective-permute-start(f32[2,64,512]{2,1,0:T(8,128)S(1)} %get-tuple-element.50), channel_id=1, source_target_pairs={{0,16},{1,17},{2,18},{3,19},{4,20},{5,21},{6,22},{7,23},{8,24},{9,... | collective-permute-start | bytes 786440 | tf_op jit(solution)/shard_map/ppermute | solution.py:26
  139.9 1.7 %collective-permute-start.28 = (f32[2,64,512]{2,1,0:T(8,128)S(1)}, f32[2,64,512]{2,1,0:T(8,128)S(1)}, u32[]{:S(2)}, u32[]{:S(2)}) collective-permute-start(f32[2,64,512]{2,1,0:T(8,128)S(1)} %get-tuple-element.49), channel_id=1, source_target_pairs={{0,17},{1,18},{2,19},{3,16},{4,21},{5,22},{6,23},{7,20},{8,25},{9,... | collective-permute-start | bytes 786440 | tf_op jit(solution)/shard_map/ppermute | solution.py:26
  141.6 0.2 collective-permute-start.29
  141.8 7.9 %collective-permute-done.28.refs_5_ = f32[2,64,512]{2,1,0:T(8,128)S(1)} collective-permute-done((f32[2,64,512]{2,1,0:T(8,128)S(1)}, f32[2,64,512]{2,1,0:T(8,128)S(1)}, u32[]{:S(2)}, u32[]{:S(2)}) %collective-permute-start.28) | collective-permute-done | bytes 262176 | tf_op jit(solution)/shard_map/ppermute | solution.py:26
  149.7 2.6 %join.1 = f32[1,2,512,512]{3,2,1,0:T(8,128)} custom-call(s32[3]{0:T(128)S(1)} %pad_add_fusion.at_ref, f32[2,64,512]{2,1,0:T(8,128)S(1)} %get-tuple-element.54.refs_0_, f32[2,64,512]{2,1,0:T(8,128)S(1)} %collective-permute-done.20.refs_1_, f32[2,64,512]{2,1,0:T(8,128)S(1)} %collective-permute-done.21.refs_2_, ...), custom_call_target="tpu_custom_call" | custom-call | flops 1000000 | bytes 4194304 | tf_op jit(solution)/shard_map/join/pallas_call | solution.py:201
  (26 shorter events, 0.1 us)
Async XLA Ops:
  0.0 18.8 %copy-start.2 = (s32[16,16]{1,0:T(8,128)S(1)}, s32[16,16]{1,0:T(8,128)}, u32[]{:S(2)}) copy-start(s32[16,16]{1,0:T(8,128)} %param.3) | copy-start | bytes 3076
  0.0 4.2 %collective-permute-start.2 = (f32[1024,256]{1,0:T(8,128)}, f32[1024,256]{1,0:T(8,128)S(1)}, u32[]{:S(2)}, u32[]{:S(2)}) collective-permute-start(f32[1024,256]{1,0:T(8,128)} %refs_0_.1), channel_id=1, source_target_pairs={{0,16},{16,0},{1,17},{17,1},{2,18},{18,2},{3,19},{19,3},{4,20},{20... | collective-permute-start | bytes 3145736 | tf_op jit(solution)/shard_map/ppermute | solution.py:42
  1.4 15.6 %collective-permute-start = (f32[1024,256]{1,0:T(8,128)}, f32[1024,256]{1,0:T(8,128)}, u32[]{:S(2)}, u32[]{:S(2)}) collective-permute-start(f32[1024,256]{1,0:T(8,128)} %refs_0_.1), channel_id=1, source_target_pairs={{0,1},{1,2},{2,3},{3,0},{4,5},{5,6},{6,7},{7,4},{8,9},{9,10},{10,1... | collective-permute-start | bytes 3145736 | tf_op jit(solution)/shard_map/ppermute | solution.py:26
  2.8 16.2 %collective-permute-start.14 = (f32[1024,256]{1,0:T(8,128)}, f32[1024,256]{1,0:T(8,128)}, u32[]{:S(2)}, u32[]{:S(2)}) collective-permute-start(f32[1024,256]{1,0:T(8,128)} %refs_0_.1), channel_id=1, source_target_pairs={{0,3},{1,0},{2,1},{3,2},{4,7},{5,4},{6,5},{7,6},{8,11},{9,8},{10,9... | collective-permute-start | bytes 3145736 | tf_op jit(solution)/shard_map/ppermute | solution.py:26
  4.3 40.9 %collective-permute-start.15 = (f32[1024,256]{1,0:T(8,128)S(1)}, f32[1024,256]{1,0:T(8,128)}, u32[]{:S(2)}, u32[]{:S(2)}) collective-permute-start(f32[1024,256]{1,0:T(8,128)S(1)} %collective-permute-done.2.slab_ref.refs_1_), channel_id=1, source_target_pairs={{0,3},{1,0},{2,1},{3,2},{4,7},{5,4},{6,5},{7,6},{8,11},{9,8},{10,9... | collective-permute-start | bytes 3145736 | tf_op jit(solution)/shard_map/ppermute | solution.py:26
  6.8 1.2 copy-start
  8.0 40.9 %copy-start.1 = (f32[1024,256]{1,0:T(8,128)S(1)}, f32[1024,256]{1,0:T(8,128)}, u32[]{:S(2)}) copy-start(f32[1024,256]{1,0:T(8,128)} %refs_0_.1) | copy-start | bytes 3145732
  9.2 12.9 %collective-permute-start.10 = (f32[256,256]{1,0:T(8,128)S(1)}, f32[256,256]{1,0:T(8,128)}, u32[]{:S(2)}, u32[]{:S(2)}) collective-permute-start(f32[256,256]{1,0:T(8,128)S(1)} %get-tuple-element.33), channel_id=1, source_target_pairs={{0,1},{1,2},{2,3},{3,0},{4,5},{5,6},{6,7},{7,4},{8,9},{9,10},{10,1... | collective-permute-start | bytes 786440 | tf_op jit(solution)/shard_map/ppermute | solution.py:26
  9.3 21.8 %collective-permute-start.11 = (f32[256,256]{1,0:T(8,128)S(1)}, f32[256,256]{1,0:T(8,128)}, u32[]{:S(2)}, u32[]{:S(2)}) collective-permute-start(f32[256,256]{1,0:T(8,128)S(1)} %get-tuple-element.34), channel_id=1, source_target_pairs={{0,3},{1,0},{2,1},{3,2},{4,7},{5,4},{6,5},{7,6},{8,11},{9,8},{10,9... | collective-permute-start | bytes 786440 | tf_op jit(solution)/shard_map/ppermute | solution.py:26
  17.0 15.4 %collective-permute-start.3 = (f32[256,256]{1,0:T(8,128)S(1)}, f32[256,256]{1,0:T(8,128)S(1)}, u32[]{:S(2)}, u32[]{:S(2)}) collective-permute-start(f32[256,256]{1,0:T(8,128)S(1)} %get-tuple-element.30), channel_id=1, source_target_pairs={{0,2},{1,3},{2,0},{3,1},{4,6},{5,7},{6,4},{7,5},{8,10},{9,11},{10,... | collective-permute-start | bytes 786440 | tf_op jit(solution)/shard_map/ppermute | solution.py:26
  19.0 18.5 %collective-permute-start.7 = (f32[256,256]{1,0:T(8,128)S(1)}, f32[256,256]{1,0:T(8,128)S(1)}, u32[]{:S(2)}, u32[]{:S(2)}) collective-permute-start(f32[256,256]{1,0:T(8,128)S(1)} %get-tuple-element.31.refs_2_), channel_id=1, source_target_pairs={{0,32},{32,64},{64,96},{1,33},{33,65},{65,97},{2,34},{34,66},{66,9... | collective-permute-start | bytes 786440 | tf_op jit(solution)/shard_map/ppermute | solution.py:46
  22.1 18.6 %collective-permute-start.8 = (f32[256,256]{1,0:T(8,128)S(1)}, f32[256,256]{1,0:T(8,128)S(1)}, u32[]{:S(2)}, u32[]{:S(2)}) collective-permute-start(f32[256,256]{1,0:T(8,128)S(1)} %get-tuple-element.31.refs_2_), channel_id=1, source_target_pairs={{0,96},{1,97},{2,98},{3,99},{4,100},{5,101},{6,102},{7,103},{8,104... | collective-permute-start | bytes 786440 | tf_op jit(solution)/shard_map/ppermute | solution.py:46
  31.1 27.6 %collective-permute-start.9 = (f32[1024,256]{1,0:T(8,128)S(1)}, f32[1024,256]{1,0:T(8,128)S(1)}, u32[]{:S(2)}, u32[]{:S(2)}) collective-permute-start(f32[1024,256]{1,0:T(8,128)S(1)} %collective-permute-done.2.slab_ref.refs_1_), channel_id=1, source_target_pairs={{0,1},{1,2},{2,3},{3,0},{4,5},{5,6},{6,7},{7,4},{8,9},{9,10},{10,1... | collective-permute-start | bytes 3145736 | tf_op jit(solution)/shard_map/ppermute | solution.py:26
  32.4 11.4 %collective-permute-start.4 = (f32[256,256]{1,0:T(8,128)S(1)}, f32[256,256]{1,0:T(8,128)S(1)}, u32[]{:S(2)}, u32[]{:S(2)}) collective-permute-start(f32[256,256]{1,0:T(8,128)S(1)} %collective-permute-done.3.refs_1_), channel_id=1, source_target_pairs={{0,32},{32,64},{64,96},{1,33},{33,65},{65,97},{2,34},{34,66},{66,9... | collective-permute-start | bytes 786440 | tf_op jit(solution)/shard_map/ppermute | solution.py:46
  37.5 36.5 %collective-permute-start.1 = (f32[1024,256]{1,0:T(8,128)}, f32[1024,256]{1,0:T(8,128)S(1)}, u32[]{:S(2)}, u32[]{:S(2)}) collective-permute-start(f32[1024,256]{1,0:T(8,128)} %collective-permute-done.refs_0_), channel_id=1, source_target_pairs={{0,1},{1,2},{2,3},{3,0},{4,5},{5,6},{6,7},{7,4},{8,9},{9,10},{10,1... | collective-permute-start | bytes 3145736 | tf_op jit(solution)/shard_map/ppermute | solution.py:26
  40.7 11.6 %collective-permute-start.12 = (f32[512,256]{1,0:T(8,128)S(1)}, f32[512,256]{1,0:T(8,128)S(1)}, u32[]{:S(2)}, u32[]{:S(2)}) collective-permute-start(f32[512,256]{1,0:T(8,128)S(1)} %constant_dynamic-update-slice_fusion.refs_2_.refs_7_), channel_id=1, source_target_pairs={{0,32},{32,64},{64,96},{1,33},{33,65},{65,97},{2,34},{34,66},{66,9... | collective-permute-start | bytes 1572872 | tf_op jit(solution)/shard_map/ppermute | solution.py:46
  43.8 13.5 %collective-permute-start.13 = (f32[512,256]{1,0:T(8,128)S(1)}, f32[512,256]{1,0:T(8,128)S(1)}, u32[]{:S(2)}, u32[]{:S(2)}) collective-permute-start(f32[512,256]{1,0:T(8,128)S(1)} %constant_dynamic-update-slice_fusion.refs_2_.refs_7_), channel_id=1, source_target_pairs={{0,96},{1,97},{2,98},{3,99},{4,100},{5,101},{6,102},{7,103},{8,104... | collective-permute-start | bytes 1572872 | tf_op jit(solution)/shard_map/ppermute | solution.py:46
  45.2 35.3 %collective-permute-start.23 = (f32[1024,256]{1,0:T(8,128)}, f32[1024,256]{1,0:T(8,128)S(1)}, u32[]{:S(2)}, u32[]{:S(2)}) collective-permute-start(f32[1024,256]{1,0:T(8,128)} %collective-permute-done.15.refs_6_), channel_id=1, source_target_pairs={{0,3},{1,0},{2,1},{3,2},{4,7},{5,4},{6,5},{7,6},{8,11},{9,8},{10,9... | collective-permute-start | bytes 3145736 | tf_op jit(solution)/shard_map/ppermute | solution.py:26
  52.3 21.7 %collective-permute-start.6 = (f32[512,256]{1,0:T(8,128)S(1)}, f32[512,256]{1,0:T(8,128)S(1)}, u32[]{:S(2)}, u32[]{:S(2)}) collective-permute-start(f32[512,256]{1,0:T(8,128)S(1)} %pad_maximum_fusion), channel_id=1, source_target_pairs={{0,64},{32,96},{1,65},{33,97},{2,66},{34,98},{3,67},{35,99},{4,68}... | collective-permute-start | bytes 1572872 | tf_op jit(solution)/shard_map/ppermute | solution.py:46
  57.4 16.6 %collective-permute-start.5 = (f32[256,256]{1,0:T(8,128)S(1)}, f32[256,256]{1,0:T(8,128)S(1)}, u32[]{:S(2)}, u32[]{:S(2)}) collective-permute-start(f32[256,256]{1,0:T(8,128)S(1)} %collective-permute-done.3.refs_1_), channel_id=1, source_target_pairs={{0,96},{1,97},{2,98},{3,99},{4,100},{5,101},{6,102},{7,103},{8,104... | collective-permute-start | bytes 786440 | tf_op jit(solution)/shard_map/ppermute | solution.py:46
  58.7 15.3 %collective-permute-start.16 = (f32[512,256]{1,0:T(8,128)S(1)}, f32[512,256]{1,0:T(8,128)S(1)}, u32[]{:S(2)}, u32[]{:S(2)}) collective-permute-start(f32[512,256]{1,0:T(8,128)S(1)} %collective-permute-done.12.refs_3_.refs_8_), channel_id=1, source_target_pairs={{32,64},{64,96},{33,65},{65,97},{34,66},{66,98},{35,67},{67,99},{3... | collective-permute-start | bytes 1572872 | tf_op jit(solution)/shard_map/ppermute | solution.py:46
  78.3 19.4 %collective-permute-start.17 = (f32[8,64,512]{2,1,0:T(8,128)S(1)}, f32[8,64,512]{2,1,0:T(8,128)S(1)}, u32[]{:S(2)}, u32[]{:S(2)}) collective-permute-start(f32[8,64,512]{2,1,0:T(8,128)S(1)} %get-tuple-element.41), channel_id=1, source_target_pairs={{0,4},{1,5},{2,6},{3,7},{4,8},{5,9},{6,10},{7,11},{8,12},{9,13},{1... | collective-permute-start | bytes 3145736 | tf_op jit(solution)/shard_map/ppermute | solution.py:26
  84.8 16.5 %collective-permute-start.24 = (f32[8,64,512]{2,1,0:T(8,128)S(1)}, f32[8,64,512]{2,1,0:T(8,128)S(1)}, u32[]{:S(2)}, u32[]{:S(2)}) collective-permute-start(f32[8,64,512]{2,1,0:T(8,128)S(1)} %get-tuple-element.45), channel_id=1, source_target_pairs={{0,12},{1,13},{2,14},{3,15},{4,0},{5,1},{6,2},{7,3},{8,4},{9,5},{1... | collective-permute-start | bytes 3145736 | tf_op jit(solution)/shard_map/ppermute | solution.py:26
  89.5 23.0 %collective-permute-start.19 = (f32[8,64,512]{2,1,0:T(8,128)S(1)}, f32[8,64,512]{2,1,0:T(8,128)S(1)}, u32[]{:S(2)}, u32[]{:S(2)}) collective-permute-start(f32[8,64,512]{2,1,0:T(8,128)S(1)} %get-tuple-element.42), channel_id=1, source_target_pairs={{0,12},{1,13},{2,14},{3,15},{4,0},{5,1},{6,2},{7,3},{8,4},{9,5},{1... | collective-permute-start | bytes 3145736 | tf_op jit(solution)/shard_map/ppermute | solution.py:26
  97.8 15.2 %collective-permute-start.18 = (f32[8,64,512]{2,1,0:T(8,128)S(1)}, f32[8,64,512]{2,1,0:T(8,128)S(1)}, u32[]{:S(2)}, u32[]{:S(2)}) collective-permute-start(f32[8,64,512]{2,1,0:T(8,128)S(1)} %add.262), channel_id=1, source_target_pairs={{0,4},{1,5},{2,6},{3,7},{4,8},{5,9},{6,10},{7,11},{8,12},{9,13},{1... | collective-permute-start | bytes 3145736 | tf_op jit(solution)/shard_map/ppermute | solution.py:26
  97.9 26.4 %collective-permute-start.26 = (f32[8,64,512]{2,1,0:T(8,128)S(1)}, f32[8,64,512]{2,1,0:T(8,128)S(1)}, u32[]{:S(2)}, u32[]{:S(2)}) collective-permute-start(f32[8,64,512]{2,1,0:T(8,128)S(1)} %get-tuple-element.46), channel_id=1, source_target_pairs={{0,4},{1,5},{2,6},{3,7},{4,8},{5,9},{6,10},{7,11},{8,12},{9,13},{1... | collective-permute-start | bytes 3145736 | tf_op jit(solution)/shard_map/ppermute | solution.py:26
  101.5 22.8 %collective-permute-start.25 = (f32[8,64,512]{2,1,0:T(8,128)S(1)}, f32[8,64,512]{2,1,0:T(8,128)S(1)}, u32[]{:S(2)}, u32[]{:S(2)}) collective-permute-start(f32[8,64,512]{2,1,0:T(8,128)S(1)} %add.271), channel_id=1, source_target_pairs={{0,12},{1,13},{2,14},{3,15},{4,0},{5,1},{6,2},{7,3},{8,4},{9,5},{1... | collective-permute-start | bytes 3145736 | tf_op jit(solution)/shard_map/ppermute | solution.py:26
  113.4 28.2 %collective-permute-start.20 = (f32[2,64,512]{2,1,0:T(8,128)S(1)}, f32[2,64,512]{2,1,0:T(8,128)S(1)}, u32[]{:S(2)}, u32[]{:S(2)}) collective-permute-start(f32[2,64,512]{2,1,0:T(8,128)S(1)} %get-tuple-element.53), channel_id=1, source_target_pairs={{0,1},{1,2},{2,3},{3,0},{4,5},{5,6},{6,7},{7,4},{8,9},{9,10},{10,1... | collective-permute-start | bytes 786440 | tf_op jit(solution)/shard_map/ppermute | solution.py:26
  115.0 26.8 %collective-permute-start.21 = (f32[2,64,512]{2,1,0:T(8,128)S(1)}, f32[2,64,512]{2,1,0:T(8,128)S(1)}, u32[]{:S(2)}, u32[]{:S(2)}) collective-permute-start(f32[2,64,512]{2,1,0:T(8,128)S(1)} %get-tuple-element.52), channel_id=1, source_target_pairs={{0,2},{1,3},{2,0},{3,1},{4,6},{5,7},{6,4},{7,5},{8,10},{9,11},{10,... | collective-permute-start | bytes 786440 | tf_op jit(solution)/shard_map/ppermute | solution.py:26
  116.6 25.1 %collective-permute-start.22 = (f32[2,64,512]{2,1,0:T(8,128)S(1)}, f32[2,64,512]{2,1,0:T(8,128)S(1)}, u32[]{:S(2)}, u32[]{:S(2)}) collective-permute-start(f32[2,64,512]{2,1,0:T(8,128)S(1)} %get-tuple-element.51), channel_id=1, source_target_pairs={{0,3},{1,0},{2,1},{3,2},{4,7},{5,4},{6,5},{7,6},{8,11},{9,8},{10,9... | collective-permute-start | bytes 786440 | tf_op jit(solution)/shard_map/ppermute | solution.py:26
  124.7 17.1 %collective-permute-start.27 = (f32[2,64,512]{2,1,0:T(8,128)S(1)}, f32[2,64,512]{2,1,0:T(8,128)S(1)}, u32[]{:S(2)}, u32[]{:S(2)}) collective-permute-start(f32[2,64,512]{2,1,0:T(8,128)S(1)} %get-tuple-element.50), channel_id=1, source_target_pairs={{0,16},{1,17},{2,18},{3,19},{4,20},{5,21},{6,22},{7,23},{8,24},{9,... | collective-permute-start | bytes 786440 | tf_op jit(solution)/shard_map/ppermute | solution.py:26
  139.9 9.8 %collective-permute-start.28 = (f32[2,64,512]{2,1,0:T(8,128)S(1)}, f32[2,64,512]{2,1,0:T(8,128)S(1)}, u32[]{:S(2)}, u32[]{:S(2)}) collective-permute-start(f32[2,64,512]{2,1,0:T(8,128)S(1)} %get-tuple-element.49), channel_id=1, source_target_pairs={{0,17},{1,18},{2,19},{3,16},{4,21},{5,22},{6,23},{7,20},{8,25},{9,... | collective-permute-start | bytes 786440 | tf_op jit(solution)/shard_map/ppermute | solution.py:26
  141.6 8.1 %collective-permute-start.29 = (f32[2,64,512]{2,1,0:T(8,128)S(1)}, f32[2,64,512]{2,1,0:T(8,128)S(1)}, u32[]{:S(2)}, u32[]{:S(2)}) collective-permute-start(f32[2,64,512]{2,1,0:T(8,128)S(1)} %get-tuple-element.48), channel_id=1, source_target_pairs={{0,18},{1,19},{2,16},{3,17},{4,22},{5,23},{6,20},{7,21},{8,26},{9,... | collective-permute-start | bytes 786440 | tf_op jit(solution)/shard_map/ppermute | solution.py:26
  141.8 7.9 %collective-permute-start.30 = (f32[2,64,512]{2,1,0:T(8,128)S(1)}, f32[2,64,512]{2,1,0:T(8,128)S(1)}, u32[]{:S(2)}, u32[]{:S(2)}) collective-permute-start(f32[2,64,512]{2,1,0:T(8,128)S(1)} %get-tuple-element.47), channel_id=1, source_target_pairs={{0,19},{1,16},{2,17},{3,18},{4,23},{5,20},{6,21},{7,22},{8,27},{9,... | collective-permute-start | bytes 786440 | tf_op jit(solution)/shard_map/ppermute | solution.py:26

commit v3 on v2

--- a/solution.py
+++ b/solution.py
@@ -245,14 +245,14 @@
     onward, wrap = [(0, 1), (1, 2), (2, 3)], [(0, 3)]
     both = jnp.concatenate([small[0], small[2]])
     a1, a3 = hop(first, onward), hop(first, wrap)
-    b1, b3 = hop(both, onward), hop(both, wrap)
+    b1, b3 = hop(both, onward), hop(both, wrap + [(1, 0)])
     c1, c3 = hop(small[1], onward), hop(small[1], wrap)
-    d2 = hop(jnp.concatenate([first, small[1]]), [(0, 2), (1, 3)])
-    b2 = hop(b1, onward[1:])
+    a2, c2 = hop(a1, onward[1:]), hop(c1, onward[1:])
+    b2 = hop(b3, wrap + [(3, 2)])
 
     wide = first.shape[0]
     low, high = [(v, 0) for v in (both, b1, b3, b2)], [(v, wide) for v in (both, b1, b3, b2)]
-    zero, far = [(first, 0), (a1, 0), (a3, 0), (d2, 0)], [(small[1], 0), (c1, 0), (c3, 0), (d2, wide)]
+    zero, far = [(v, 0) for v in (first, a1, a3, a2)], [(v, 0) for v in (small[1], c1, c3, c2)]
     three, four = range(3), range(4)
     total, own_parts = product(tab, [((panel, other), dict(zip(three, zero)))], None, (0, 1), ())
     total, up_parts, down_parts = product(

time: 153 us -> 150 us (0.980)
  waiting for transfers between devices: 50 us -> 36.1 us
  starting transfers between devices: 74.1 us -> 84.5 us
    ppermute x22, waiting for transfers between devices: 43.2 us -> 35.4 us  [move(): return lax.ppermute(value, ('c', 'y', 'z'), pairs)]
    ppermute x22, starting transfers between devices: 52.2 us -> 58.5 us  [move(): return lax.ppermute(value, ('c', 'y', 'z'), pairs)]
    ppermute x8 -> x9, waiting for transfers between devices: 6.8 us -> 0.7 us  [hop(): return lax.ppermute(value, 'x', pairs)]
    ppermute x8 -> x9, starting transfers between devices: 20.5 us -> 24.6 us  [hop(): return lax.ppermute(value, 'x', pairs)]
  transfers between devices with their start and end apart: 31 -> 32, of which waited for: 9 -> 10; matrix products, arithmetic and copies ran while one was open for 2% -> 2% of each run, Pallas kernels for 14% -> 14%
where the time goes in v3:
time: 150 us; the launch traced here: 149 us
  starting transfers between devices  84.5 us (56%)
  waiting for transfers between devices  36.1 us (24%)
  Pallas kernels  23.6 us (16%)
  local copies, waits for them, and re-layouts  3.17 us (2%)
    ppermute x22, starting transfers between devices, move(): return lax.ppermute(value, ('c', 'y', 'z'), pairs)  58.5 us
    ppermute x22, waiting for transfers between devices, move(): return lax.ppermute(value, ('c', 'y', 'z'), pairs)  35.4 us
    ppermute x9, starting transfers between devices, hop(): return lax.ppermute(value, 'x', pairs)  24.6 us
    pallas_call x4, Pallas kernels, product(): pl.pallas_call(functools.partial(product_kernel, q, form, total is not No...  19.8 us
  transfers between devices with their start and end apart: 32, of which 10 were waited for; matrix products, arithmetic and copies ran while one was open for 2% of the time, Pallas kernels for 14%

profile of v3, /device:TPU:1, one launch (start us, length us, event | category | flops | bytes accessed | tf_op | source)
XLA Modules:
  0.0 149.2 jit_solution(13182946609971569130)
XLA Ops:
  0.0 1.4 collective-permute-start.2
  1.4 1.4 collective-permute-start
  2.8 1.4 collective-permute-start.15
  4.2 0.0 collective-permute-done.2.slab_ref.refs_1_
  4.3 2.5 %collective-permute-start.16 = (f32[1024,256]{1,0:T(8,128)S(1)}, f32[1024,256]{1,0:T(8,128)}, u32[]{:S(2)}, u32[]{:S(2)}) collective-permute-start(f32[1024,256]{1,0:T(8,128)S(1)} %collective-permute-done.2.slab_ref.refs_1_), channel_id=1, source_target_pairs={{0,3},{1,0},{2,1},{3,2},{4,7},{5,4},{6,5},{7,6},{8,11},{9,8},{10,9... | collective-permute-start | bytes 3145736 | tf_op jit(solution)/shard_map/ppermute | solution.py:26
  6.7 0.1 pad_add_fusion.at_ref
  6.8 1.2 copy-done
  8.0 0.6 cut.2
  8.6 0.6 cut.3
  9.2 3.8 %collective-permute-start.7 = (f32[256,256]{1,0:T(8,128)S(1)}, f32[256,256]{1,0:T(8,128)}, u32[]{:S(2)}, u32[]{:S(2)}) collective-permute-start(f32[256,256]{1,0:T(8,128)S(1)} %get-tuple-element.31.refs_2_), channel_id=1, source_target_pairs={{0,32},{32,64},{64,96},{1,33},{33,65},{65,97},{2,34},{34,66},{66,9... | collective-permute-start | bytes 786440 | tf_op jit(solution)/shard_map/ppermute | solution.py:46
  13.1 0.0 collective-permute-start.11
  13.1 4.0 %collective-permute-done.refs_0_ = f32[1024,256]{1,0:T(8,128)} collective-permute-done((f32[1024,256]{1,0:T(8,128)}, f32[1024,256]{1,0:T(8,128)}, u32[]{:S(2)}, u32[]{:S(2)}) %collective-permute-start) | collective-permute-done | bytes 1048608 | tf_op jit(solution)/shard_map/ppermute | solution.py:26
  17.0 1.5 collective-permute-start.12
  18.5 1.2 collective-permute-start.3
  19.7 0.1 broadcast_select_fusion
  19.8 0.2 select_reduce_fusion
  20.0 0.0 collective-permute-done.7.refs_3_
  20.0 4.4 %collective-permute-start.8 = (f32[256,256]{1,0:T(8,128)S(1)}, f32[256,256]{1,0:T(8,128)S(1)}, u32[]{:S(2)}, u32[]{:S(2)}) collective-permute-start(f32[256,256]{1,0:T(8,128)S(1)} %get-tuple-element.31.refs_2_), channel_id=1, source_target_pairs={{0,96},{1,97},{2,98},{3,99},{4,100},{5,101},{6,102},{7,103},{8,104... | collective-permute-start | bytes 786440 | tf_op jit(solution)/shard_map/ppermute | solution.py:46
  24.4 0.0 collective-permute-done.11
  24.4 0.7 collective-permute-start.10
  25.1 0.4 collective-permute-done.3.refs_1_
  25.5 3.1 %collective-permute-start.4 = (f32[256,256]{1,0:T(8,128)S(1)}, f32[256,256]{1,0:T(8,128)S(1)}, u32[]{:S(2)}, u32[]{:S(2)}) collective-permute-start(f32[256,256]{1,0:T(8,128)S(1)} %collective-permute-done.3.refs_1_), channel_id=1, source_target_pairs={{0,32},{32,64},{64,96},{1,33},{33,65},{65,97},{2,34},{34,66},{66,9... | collective-permute-start | bytes 786440 | tf_op jit(solution)/shard_map/ppermute | solution.py:46
  28.6 2.5 %collective-permute-done.12 = f32[256,256]{1,0:T(8,128)} collective-permute-done((f32[256,256]{1,0:T(8,128)S(1)}, f32[256,256]{1,0:T(8,128)}, u32[]{:S(2)}, u32[]{:S(2)}) %collective-permute-start.12) | collective-permute-done | bytes 262176 | tf_op jit(solution)/shard_map/ppermute | solution.py:26
  31.1 4.4 %collective-permute-start.5 = (f32[256,256]{1,0:T(8,128)S(1)}, f32[256,256]{1,0:T(8,128)S(1)}, u32[]{:S(2)}, u32[]{:S(2)}) collective-permute-start(f32[256,256]{1,0:T(8,128)S(1)} %collective-permute-done.3.refs_1_), channel_id=1, source_target_pairs={{0,96},{1,97},{2,98},{3,99},{4,100},{5,101},{6,102},{7,103},{8,104... | collective-permute-start | bytes 786440 | tf_op jit(solution)/shard_map/ppermute | solution.py:46
  35.5 1.0 constant_dynamic-update-slice_fusion.1
  36.5 1.0 constant_dynamic-update-slice_fusion.refs_2_.refs_7_
  37.4 0.0 collective-permute-done.8.refs_4_
  37.5 6.1 %collective-permute-start.1 = (f32[1024,256]{1,0:T(8,128)}, f32[1024,256]{1,0:T(8,128)S(1)}, u32[]{:S(2)}, u32[]{:S(2)}) collective-permute-start(f32[1024,256]{1,0:T(8,128)} %collective-permute-done.refs_0_), channel_id=1, source_target_pairs={{0,1},{1,2},{2,3},{3,0},{4,5},{5,6},{6,7},{7,4},{8,9},{9,10},{10,1... | collective-permute-start | bytes 3145736 | tf_op jit(solution)/shard_map/ppermute | solution.py:26
  43.6 0.0 collective-permute-done.4.refs_2_
  43.6 1.3 collective-permute-start.13
  44.9 0.0 collective-permute-done.5.refs_3_
  44.9 1.9 %collective-permute-start.14 = (f32[512,256]{1,0:T(8,128)S(1)}, f32[512,256]{1,0:T(8,128)S(1)}, u32[]{:S(2)}, u32[]{:S(2)}) collective-permute-start(f32[512,256]{1,0:T(8,128)S(1)} %constant_dynamic-update-slice_fusion.refs_2_.refs_7_), channel_id=1, source_target_pairs={{0,96},{32,0},{1,97},{33,1},{2,98},{34,2},{3,99},{35,3},{4,100},{3... | collective-permute-start | bytes 1572872 | tf_op jit(solution)/shard_map/ppermute | solution.py:46
  46.8 0.0 collective-permute-done.16.refs_6_
  46.8 5.4 %collective-permute-start.24 = (f32[1024,256]{1,0:T(8,128)}, f32[1024,256]{1,0:T(8,128)S(1)}, u32[]{:S(2)}, u32[]{:S(2)}) collective-permute-start(f32[1024,256]{1,0:T(8,128)} %collective-permute-done.16.refs_6_), channel_id=1, source_target_pairs={{0,3},{1,0},{2,1},{3,2},{4,7},{5,4},{6,5},{7,6},{8,11},{9,8},{10,9... | collective-permute-start | bytes 3145736 | tf_op jit(solution)/shard_map/ppermute | solution.py:26
  52.2 3.7 %shard_map.28 = (f32[8,768,256]{2,1,0:T(8,128)S(1)}, bf16[2048,512]{1,0:T(8,128)(2,1)S(1)}) custom-call(s32[64]{0:T(128)S(1)} %broadcast_add_fusion.2.tab_ref, f32[1024,256]{1,0:T(8,128)S(1)} %copy-done.1, f32[1024,256]{1,0:T(8,128)S(1)} %collective-permute-done.2.slab_ref.refs_1_, f32[256,256]{1,0:T(8,128)S(1)} %get-tuple-element.31.refs_2_, ...), custom_call_target="tpu_custom_call" | custom-call | flops 6442450944 | bytes 12582912 | tf_op jit(solution)/shard_map/pallas_call | solution.py:172
  55.9 0.7 collective-permute-start.9
  56.6 0.7 collective-permute-done.14.refs_4_.refs_9_
  57.3 0.7 collective-permute-start.6
  58.0 4.2 %collective-permute-start.17 = (f32[512,256]{1,0:T(8,128)S(1)}, f32[512,256]{1,0:T(8,128)S(1)}, u32[]{:S(2)}, u32[]{:S(2)}) collective-permute-start(f32[512,256]{1,0:T(8,128)S(1)} %collective-permute-done.14.refs_4_.refs_9_), channel_id=1, source_target_pairs={{0,96},{96,64},{1,97},{97,65},{2,98},{98,66},{3,99},{99,67},{4,100... | collective-permute-start | bytes 1572872 | tf_op jit(solution)/shard_map/ppermute | solution.py:46
  62.2 7.6 %shard_map.29 = (f32[8,768,256]{2,1,0:T(8,128)S(1)}, bf16[2048,512]{1,0:T(8,128)(2,1)S(1)}, bf16[2048,512]{1,0:T(8,128)(2,1)S(1)}) custom-call(s32[64]{0:T(128)S(1)} %broadcast_add_fusion.2.tab_ref, f32[1024,256]{1,0:T(8,128)} %collective-permute-done.refs_0_, f32[1024,256]{1,0:T(8,128)S(1)} %collective-permute-done.10.refs_1_, ...), custom_call_target="tpu_custom_call", output_to_operand_aliasing={{0}: (11, {})} | custom-call | flops 6442450944 | bytes 12582912 | tf_op jit(solution)/shard_map/pallas_call | solution.py:172
  69.9 4.3 %shard_map.30 = (f32[8,64,512]{2,1,0:T(8,128)S(1)}, f32[8,64,512]{2,1,0:T(8,128)S(1)}, f32[8,64,512]{2,1,0:T(8,128)S(1)}, f32[8,64,512]{2,1,0:T(8,128)S(1)}) custom-call(s32[64]{0:T(128)S(1)} %broadcast_add_fusion.2.tab_ref, f32[1024,256]{1,0:T(8,128)S(1)} %collective-permute-done.1.refs_0_, f32[256,256]{1,0:T(8,128)S(1)} %collective-permute-done.3.refs_1_, ...), custom_call_target="tpu_custom_call" | custom-call | flops 3221225472 | bytes 12582912 | tf_op jit(solution)/shard_map/pallas_call | solution.py:172
  74.1 0.1 collective-permute-start.18
  74.2 4.3 %shard_map.31 = (f32[8,64,512]{2,1,0:T(8,128)S(1)}, f32[8,64,512]{2,1,0:T(8,128)S(1)}, f32[8,64,512]{2,1,0:T(8,128)S(1)}, f32[8,64,512]{2,1,0:T(8,128)S(1)}) custom-call(s32[64]{0:T(128)S(1)} %broadcast_add_fusion.2.tab_ref, f32[1024,256]{1,0:T(8,128)S(1)} %collective-permute-done.24.refs_0_, f32[256,256]{1,0:T(8,128)S(1)} %collective-permute-done.3.refs_1_, ...), custom_call_target="tpu_custom_call" | custom-call | flops 3221225472 | bytes 12582912 | tf_op jit(solution)/shard_map/pallas_call | solution.py:172
  78.5 4.0 %collective-permute-start.25 = (f32[8,64,512]{2,1,0:T(8,128)S(1)}, f32[8,64,512]{2,1,0:T(8,128)S(1)}, u32[]{:S(2)}, u32[]{:S(2)}) collective-permute-start(f32[8,64,512]{2,1,0:T(8,128)S(1)} %get-tuple-element.45), channel_id=1, source_target_pairs={{0,12},{1,13},{2,14},{3,15},{4,0},{5,1},{6,2},{7,3},{8,4},{9,5},{1... | collective-permute-start | bytes 3145736 | tf_op jit(solution)/shard_map/ppermute | solution.py:26
  82.5 3.4 %collective-permute-start.20 = (f32[8,64,512]{2,1,0:T(8,128)S(1)}, f32[8,64,512]{2,1,0:T(8,128)S(1)}, u32[]{:S(2)}, u32[]{:S(2)}) collective-permute-start(f32[8,64,512]{2,1,0:T(8,128)S(1)} %get-tuple-element.42), channel_id=1, source_target_pairs={{0,12},{1,13},{2,14},{3,15},{4,0},{5,1},{6,2},{7,3},{8,4},{9,5},{1... | collective-permute-start | bytes 3145736 | tf_op jit(solution)/shard_map/ppermute | solution.py:26
  85.9 4.7 %collective-permute-done.18 = f32[8,64,512]{2,1,0:T(8,128)S(1)} collective-permute-done((f32[8,64,512]{2,1,0:T(8,128)S(1)}, f32[8,64,512]{2,1,0:T(8,128)S(1)}, u32[]{:S(2)}, u32[]{:S(2)}) %collective-permute-start.18) | collective-permute-done | bytes 1048608 | tf_op jit(solution)/shard_map/ppermute | solution.py:26
  90.6 0.2 add.262
  90.8 2.1 %collective-permute-start.19 = (f32[8,64,512]{2,1,0:T(8,128)S(1)}, f32[8,64,512]{2,1,0:T(8,128)S(1)}, u32[]{:S(2)}, u32[]{:S(2)}) collective-permute-start(f32[8,64,512]{2,1,0:T(8,128)S(1)} %add.262), channel_id=1, source_target_pairs={{0,4},{1,5},{2,6},{3,7},{4,8},{5,9},{6,10},{7,11},{8,12},{9,13},{1... | collective-permute-start | bytes 3145736 | tf_op jit(solution)/shard_map/ppermute | solution.py:26
  92.9 2.2 %collective-permute-start.27 = (f32[8,64,512]{2,1,0:T(8,128)S(1)}, f32[8,64,512]{2,1,0:T(8,128)S(1)}, u32[]{:S(2)}, u32[]{:S(2)}) collective-permute-start(f32[8,64,512]{2,1,0:T(8,128)S(1)} %get-tuple-element.46), channel_id=1, source_target_pairs={{0,4},{1,5},{2,6},{3,7},{4,8},{5,9},{6,10},{7,11},{8,12},{9,13},{1... | collective-permute-start | bytes 3145736 | tf_op jit(solution)/shard_map/ppermute | solution.py:26
  95.1 2.6 %collective-permute-done.25 = f32[8,64,512]{2,1,0:T(8,128)S(1)} collective-permute-done((f32[8,64,512]{2,1,0:T(8,128)S(1)}, f32[8,64,512]{2,1,0:T(8,128)S(1)}, u32[]{:S(2)}, u32[]{:S(2)}) %collective-permute-start.25) | collective-permute-done | bytes 1048608 | tf_op jit(solution)/shard_map/ppermute | solution.py:26
  97.7 0.2 add.271
  97.9 0.1 collective-permute-start.26
  98.0 10.9 %collective-permute-done.20 = f32[8,64,512]{2,1,0:T(8,128)S(1)} collective-permute-done((f32[8,64,512]{2,1,0:T(8,128)S(1)}, f32[8,64,512]{2,1,0:T(8,128)S(1)}, u32[]{:S(2)}, u32[]{:S(2)}) %collective-permute-start.20) | collective-permute-done | bytes 1048608 | tf_op jit(solution)/shard_map/ppermute | solution.py:26
  109.0 0.3 slice_add_fusion.8
  109.3 6.6 %collective-permute-start.21 = (f32[2,64,512]{2,1,0:T(8,128)S(1)}, f32[2,64,512]{2,1,0:T(8,128)S(1)}, u32[]{:S(2)}, u32[]{:S(2)}) collective-permute-start(f32[2,64,512]{2,1,0:T(8,128)S(1)} %get-tuple-element.53), channel_id=1, source_target_pairs={{0,1},{1,2},{2,3},{3,0},{4,5},{5,6},{6,7},{7,4},{8,9},{9,10},{10,1... | collective-permute-start | bytes 786440 | tf_op jit(solution)/shard_map/ppermute | solution.py:26
  115.9 1.1 collective-permute-start.22
  117.0 1.4 collective-permute-start.23
  118.4 1.8 %collective-permute-done.26 = f32[8,64,512]{2,1,0:T(8,128)S(1)} collective-permute-done((f32[8,64,512]{2,1,0:T(8,128)S(1)}, f32[8,64,512]{2,1,0:T(8,128)S(1)}, u32[]{:S(2)}, u32[]{:S(2)}) %collective-permute-start.26) | collective-permute-done | bytes 1048608 | tf_op jit(solution)/shard_map/ppermute | solution.py:26
  120.2 0.3 slice_add_fusion
  120.5 14.3 %collective-permute-start.28 = (f32[2,64,512]{2,1,0:T(8,128)S(1)}, f32[2,64,512]{2,1,0:T(8,128)S(1)}, u32[]{:S(2)}, u32[]{:S(2)}) collective-permute-start(f32[2,64,512]{2,1,0:T(8,128)S(1)} %get-tuple-element.50), channel_id=1, source_target_pairs={{0,16},{1,17},{2,18},{3,19},{4,20},{5,21},{6,22},{7,23},{8,24},{9,... | collective-permute-start | bytes 786440 | tf_op jit(solution)/shard_map/ppermute | solution.py:26
  134.9 3.2 %collective-permute-start.31 = (f32[2,64,512]{2,1,0:T(8,128)S(1)}, f32[2,64,512]{2,1,0:T(8,128)S(1)}, u32[]{:S(2)}, u32[]{:S(2)}) collective-permute-start(f32[2,64,512]{2,1,0:T(8,128)S(1)} %get-tuple-element.47), channel_id=1, source_target_pairs={{0,19},{1,16},{2,17},{3,18},{4,23},{5,20},{6,21},{7,22},{8,27},{9,... | collective-permute-start | bytes 786440 | tf_op jit(solution)/shard_map/ppermute | solution.py:26
  138.1 4.5 %collective-permute-done.29.refs_5_ = f32[2,64,512]{2,1,0:T(8,128)S(1)} collective-permute-done((f32[2,64,512]{2,1,0:T(8,128)S(1)}, f32[2,64,512]{2,1,0:T(8,128)S(1)}, u32[]{:S(2)}, u32[]{:S(2)}) %collective-permute-start.29) | collective-permute-done | bytes 262176 | tf_op jit(solution)/shard_map/ppermute | solution.py:26
  142.6 4.0 %collective-permute-done.30.refs_6_ = f32[2,64,512]{2,1,0:T(8,128)S(1)} collective-permute-done((f32[2,64,512]{2,1,0:T(8,128)S(1)}, f32[2,64,512]{2,1,0:T(8,128)S(1)}, u32[]{:S(2)}, u32[]{:S(2)}) %collective-permute-start.30) | collective-permute-done | bytes 262176 | tf_op jit(solution)/shard_map/ppermute | solution.py:26
  146.6 2.6 %join.1 = f32[1,2,512,512]{3,2,1,0:T(8,128)} custom-call(s32[3]{0:T(128)S(1)} %pad_add_fusion.at_ref, f32[2,64,512]{2,1,0:T(8,128)S(1)} %get-tuple-element.54.refs_0_, f32[2,64,512]{2,1,0:T(8,128)S(1)} %collective-permute-done.21.refs_1_, f32[2,64,512]{2,1,0:T(8,128)S(1)} %collective-permute-done.22.refs_2_, ...), custom_call_target="tpu_custom_call" | custom-call | flops 1000000 | bytes 4194304 | tf_op jit(solution)/shard_map/join/pallas_call | solution.py:201
  (27 shorter events, 0.1 us)
Async XLA Ops:
  0.0 19.8 %copy-start.2 = (s32[16,16]{1,0:T(8,128)S(1)}, s32[16,16]{1,0:T(8,128)}, u32[]{:S(2)}) copy-start(s32[16,16]{1,0:T(8,128)} %param.3) | copy-start | bytes 3076
  0.0 4.2 %collective-permute-start.2 = (f32[1024,256]{1,0:T(8,128)}, f32[1024,256]{1,0:T(8,128)S(1)}, u32[]{:S(2)}, u32[]{:S(2)}) collective-permute-start(f32[1024,256]{1,0:T(8,128)} %refs_0_.1), channel_id=1, source_target_pairs={{0,16},{16,0},{1,17},{17,1},{2,18},{18,2},{3,19},{19,3},{4,20},{20... | collective-permute-start | bytes 3145736 | tf_op jit(solution)/shard_map/ppermute | solution.py:42
  1.4 15.6 %collective-permute-start = (f32[1024,256]{1,0:T(8,128)}, f32[1024,256]{1,0:T(8,128)}, u32[]{:S(2)}, u32[]{:S(2)}) collective-permute-start(f32[1024,256]{1,0:T(8,128)} %refs_0_.1), channel_id=1, source_target_pairs={{0,1},{1,2},{2,3},{3,0},{4,5},{5,6},{6,7},{7,4},{8,9},{9,10},{10,1... | collective-permute-start | bytes 3145736 | tf_op jit(solution)/shard_map/ppermute | solution.py:26
  2.8 15.7 %collective-permute-start.15 = (f32[1024,256]{1,0:T(8,128)}, f32[1024,256]{1,0:T(8,128)}, u32[]{:S(2)}, u32[]{:S(2)}) collective-permute-start(f32[1024,256]{1,0:T(8,128)} %refs_0_.1), channel_id=1, source_target_pairs={{0,3},{1,0},{2,1},{3,2},{4,7},{5,4},{6,5},{7,6},{8,11},{9,8},{10,9... | collective-permute-start | bytes 3145736 | tf_op jit(solution)/shard_map/ppermute | solution.py:26
  4.3 42.6 %collective-permute-start.16 = (f32[1024,256]{1,0:T(8,128)S(1)}, f32[1024,256]{1,0:T(8,128)}, u32[]{:S(2)}, u32[]{:S(2)}) collective-permute-start(f32[1024,256]{1,0:T(8,128)S(1)} %collective-permute-done.2.slab_ref.refs_1_), channel_id=1, source_target_pairs={{0,3},{1,0},{2,1},{3,2},{4,7},{5,4},{6,5},{7,6},{8,11},{9,8},{10,9... | collective-permute-start | bytes 3145736 | tf_op jit(solution)/shard_map/ppermute | solution.py:26
  6.8 1.2 copy-start
  8.0 44.2 %copy-start.1 = (f32[1024,256]{1,0:T(8,128)S(1)}, f32[1024,256]{1,0:T(8,128)}, u32[]{:S(2)}) copy-start(f32[1024,256]{1,0:T(8,128)} %refs_0_.1) | copy-start | bytes 3145732
  9.2 10.8 %collective-permute-start.7 = (f32[256,256]{1,0:T(8,128)S(1)}, f32[256,256]{1,0:T(8,128)}, u32[]{:S(2)}, u32[]{:S(2)}) collective-permute-start(f32[256,256]{1,0:T(8,128)S(1)} %get-tuple-element.31.refs_2_), channel_id=1, source_target_pairs={{0,32},{32,64},{64,96},{1,33},{33,65},{65,97},{2,34},{34,66},{66,9... | collective-permute-start | bytes 786440 | tf_op jit(solution)/shard_map/ppermute | solution.py:46
  13.1 11.3 %collective-permute-start.11 = (f32[256,256]{1,0:T(8,128)S(1)}, f32[256,256]{1,0:T(8,128)}, u32[]{:S(2)}, u32[]{:S(2)}) collective-permute-start(f32[256,256]{1,0:T(8,128)S(1)} %get-tuple-element.33), channel_id=1, source_target_pairs={{0,1},{1,2},{2,3},{3,0},{4,5},{5,6},{6,7},{7,4},{8,9},{9,10},{10,1... | collective-permute-start | bytes 786440 | tf_op jit(solution)/shard_map/ppermute | solution.py:26
  17.0 14.1 %collective-permute-start.12 = (f32[256,256]{1,0:T(8,128)S(1)}, f32[256,256]{1,0:T(8,128)}, u32[]{:S(2)}, u32[]{:S(2)}) collective-permute-start(f32[256,256]{1,0:T(8,128)S(1)} %get-tuple-element.34), channel_id=1, source_target_pairs={{0,3},{1,0},{2,1},{3,2},{4,7},{5,4},{6,5},{7,6},{8,11},{9,8},{10,9... | collective-permute-start | bytes 786440 | tf_op jit(solution)/shard_map/ppermute | solution.py:26
  18.5 7.0 %collective-permute-start.3 = (f32[256,256]{1,0:T(8,128)S(1)}, f32[256,256]{1,0:T(8,128)S(1)}, u32[]{:S(2)}, u32[]{:S(2)}) collective-permute-start(f32[256,256]{1,0:T(8,128)S(1)} %get-tuple-element.30), channel_id=1, source_target_pairs={{0,2},{1,3},{2,0},{3,1},{4,6},{5,7},{6,4},{7,5},{8,10},{9,11},{10,... | collective-permute-start | bytes 786440 | tf_op jit(solution)/shard_map/ppermute | solution.py:26
  20.0 17.5 %collective-permute-start.8 = (f32[256,256]{1,0:T(8,128)S(1)}, f32[256,256]{1,0:T(8,128)S(1)}, u32[]{:S(2)}, u32[]{:S(2)}) collective-permute-start(f32[256,256]{1,0:T(8,128)S(1)} %get-tuple-element.31.refs_2_), channel_id=1, source_target_pairs={{0,96},{1,97},{2,98},{3,99},{4,100},{5,101},{6,102},{7,103},{8,104... | collective-permute-start | bytes 786440 | tf_op jit(solution)/shard_map/ppermute | solution.py:46
  24.4 33.5 %collective-permute-start.10 = (f32[1024,256]{1,0:T(8,128)S(1)}, f32[1024,256]{1,0:T(8,128)S(1)}, u32[]{:S(2)}, u32[]{:S(2)}) collective-permute-start(f32[1024,256]{1,0:T(8,128)S(1)} %collective-permute-done.2.slab_ref.refs_1_), channel_id=1, source_target_pairs={{0,1},{1,2},{2,3},{3,0},{4,5},{5,6},{6,7},{7,4},{8,9},{9,10},{10,1... | collective-permute-start | bytes 3145736 | tf_op jit(solution)/shard_map/ppermute | solution.py:26
  25.5 18.0 %collective-permute-start.4 = (f32[256,256]{1,0:T(8,128)S(1)}, f32[256,256]{1,0:T(8,128)S(1)}, u32[]{:S(2)}, u32[]{:S(2)}) collective-permute-start(f32[256,256]{1,0:T(8,128)S(1)} %collective-permute-done.3.refs_1_), channel_id=1, source_target_pairs={{0,32},{32,64},{64,96},{1,33},{33,65},{65,97},{2,34},{34,66},{66,9... | collective-permute-start | bytes 786440 | tf_op jit(solution)/shard_map/ppermute | solution.py:46
  31.1 13.8 %collective-permute-start.5 = (f32[256,256]{1,0:T(8,128)S(1)}, f32[256,256]{1,0:T(8,128)S(1)}, u32[]{:S(2)}, u32[]{:S(2)}) collective-permute-start(f32[256,256]{1,0:T(8,128)S(1)} %collective-permute-done.3.refs_1_), channel_id=1, source_target_pairs={{0,96},{1,97},{2,98},{3,99},{4,100},{5,101},{6,102},{7,103},{8,104... | collective-permute-start | bytes 786440 | tf_op jit(solution)/shard_map/ppermute | solution.py:46
  37.5 32.4 %collective-permute-start.1 = (f32[1024,256]{1,0:T(8,128)}, f32[1024,256]{1,0:T(8,128)S(1)}, u32[]{:S(2)}, u32[]{:S(2)}) collective-permute-start(f32[1024,256]{1,0:T(8,128)} %collective-permute-done.refs_0_), channel_id=1, source_target_pairs={{0,1},{1,2},{2,3},{3,0},{4,5},{5,6},{6,7},{7,4},{8,9},{9,10},{10,1... | collective-permute-start | bytes 3145736 | tf_op jit(solution)/shard_map/ppermute | solution.py:26
  43.6 12.3 %collective-permute-start.13 = (f32[512,256]{1,0:T(8,128)S(1)}, f32[512,256]{1,0:T(8,128)S(1)}, u32[]{:S(2)}, u32[]{:S(2)}) collective-permute-start(f32[512,256]{1,0:T(8,128)S(1)} %constant_dynamic-update-slice_fusion.refs_2_.refs_7_), channel_id=1, source_target_pairs={{0,32},{32,64},{64,96},{1,33},{33,65},{65,97},{2,34},{34,66},{66,9... | collective-permute-start | bytes 1572872 | tf_op jit(solution)/shard_map/ppermute | solution.py:46
  44.9 12.4 %collective-permute-start.14 = (f32[512,256]{1,0:T(8,128)S(1)}, f32[512,256]{1,0:T(8,128)S(1)}, u32[]{:S(2)}, u32[]{:S(2)}) collective-permute-start(f32[512,256]{1,0:T(8,128)S(1)} %constant_dynamic-update-slice_fusion.refs_2_.refs_7_), channel_id=1, source_target_pairs={{0,96},{32,0},{1,97},{33,1},{2,98},{34,2},{3,99},{35,3},{4,100},{3... | collective-permute-start | bytes 1572872 | tf_op jit(solution)/shard_map/ppermute | solution.py:46
  46.8 27.4 %collective-permute-start.24 = (f32[1024,256]{1,0:T(8,128)}, f32[1024,256]{1,0:T(8,128)S(1)}, u32[]{:S(2)}, u32[]{:S(2)}) collective-permute-start(f32[1024,256]{1,0:T(8,128)} %collective-permute-done.16.refs_6_), channel_id=1, source_target_pairs={{0,3},{1,0},{2,1},{3,2},{4,7},{5,4},{6,5},{7,6},{8,11},{9,8},{10,9... | collective-permute-start | bytes 3145736 | tf_op jit(solution)/shard_map/ppermute | solution.py:26
  55.9 13.9 %collective-permute-start.9 = (f32[256,256]{1,0:T(8,128)}, f32[256,256]{1,0:T(8,128)S(1)}, u32[]{:S(2)}, u32[]{:S(2)}) collective-permute-start(f32[256,256]{1,0:T(8,128)} %collective-permute-done.7.refs_3_), channel_id=1, source_target_pairs={{32,64},{64,96},{33,65},{65,97},{34,66},{66,98},{35,67},{67,99},{3... | collective-permute-start | bytes 786440 | tf_op jit(solution)/shard_map/ppermute | solution.py:46
  57.3 12.6 %collective-permute-start.6 = (f32[256,256]{1,0:T(8,128)S(1)}, f32[256,256]{1,0:T(8,128)S(1)}, u32[]{:S(2)}, u32[]{:S(2)}) collective-permute-start(f32[256,256]{1,0:T(8,128)S(1)} %collective-permute-done.4.refs_2_), channel_id=1, source_target_pairs={{32,64},{64,96},{33,65},{65,97},{34,66},{66,98},{35,67},{67,99},{3... | collective-permute-start | bytes 786440 | tf_op jit(solution)/shard_map/ppermute | solution.py:46
  58.0 11.9 %collective-permute-start.17 = (f32[512,256]{1,0:T(8,128)S(1)}, f32[512,256]{1,0:T(8,128)S(1)}, u32[]{:S(2)}, u32[]{:S(2)}) collective-permute-start(f32[512,256]{1,0:T(8,128)S(1)} %collective-permute-done.14.refs_4_.refs_9_), channel_id=1, source_target_pairs={{0,96},{96,64},{1,97},{97,65},{2,98},{98,66},{3,99},{99,67},{4,100... | collective-permute-start | bytes 1572872 | tf_op jit(solution)/shard_map/ppermute | solution.py:46
  74.1 16.5 %collective-permute-start.18 = (f32[8,64,512]{2,1,0:T(8,128)S(1)}, f32[8,64,512]{2,1,0:T(8,128)S(1)}, u32[]{:S(2)}, u32[]{:S(2)}) collective-permute-start(f32[8,64,512]{2,1,0:T(8,128)S(1)} %get-tuple-element.41), channel_id=1, source_target_pairs={{0,4},{1,5},{2,6},{3,7},{4,8},{5,9},{6,10},{7,11},{8,12},{9,13},{1... | collective-permute-start | bytes 3145736 | tf_op jit(solution)/shard_map/ppermute | solution.py:26
  78.5 19.2 %collective-permute-start.25 = (f32[8,64,512]{2,1,0:T(8,128)S(1)}, f32[8,64,512]{2,1,0:T(8,128)S(1)}, u32[]{:S(2)}, u32[]{:S(2)}) collective-permute-start(f32[8,64,512]{2,1,0:T(8,128)S(1)} %get-tuple-element.45), channel_id=1, source_target_pairs={{0,12},{1,13},{2,14},{3,15},{4,0},{5,1},{6,2},{7,3},{8,4},{9,5},{1... | collective-permute-start | bytes 3145736 | tf_op jit(solution)/shard_map/ppermute | solution.py:26
  82.5 26.5 %collective-permute-start.20 = (f32[8,64,512]{2,1,0:T(8,128)S(1)}, f32[8,64,512]{2,1,0:T(8,128)S(1)}, u32[]{:S(2)}, u32[]{:S(2)}) collective-permute-start(f32[8,64,512]{2,1,0:T(8,128)S(1)} %get-tuple-element.42), channel_id=1, source_target_pairs={{0,12},{1,13},{2,14},{3,15},{4,0},{5,1},{6,2},{7,3},{8,4},{9,5},{1... | collective-permute-start | bytes 3145736 | tf_op jit(solution)/shard_map/ppermute | solution.py:26
  90.8 18.2 %collective-permute-start.19 = (f32[8,64,512]{2,1,0:T(8,128)S(1)}, f32[8,64,512]{2,1,0:T(8,128)S(1)}, u32[]{:S(2)}, u32[]{:S(2)}) collective-permute-start(f32[8,64,512]{2,1,0:T(8,128)S(1)} %add.262), channel_id=1, source_target_pairs={{0,4},{1,5},{2,6},{3,7},{4,8},{5,9},{6,10},{7,11},{8,12},{9,13},{1... | collective-permute-start | bytes 3145736 | tf_op jit(solution)/shard_map/ppermute | solution.py:26
  92.9 25.5 %collective-permute-start.27 = (f32[8,64,512]{2,1,0:T(8,128)S(1)}, f32[8,64,512]{2,1,0:T(8,128)S(1)}, u32[]{:S(2)}, u32[]{:S(2)}) collective-permute-start(f32[8,64,512]{2,1,0:T(8,128)S(1)} %get-tuple-element.46), channel_id=1, source_target_pairs={{0,4},{1,5},{2,6},{3,7},{4,8},{5,9},{6,10},{7,11},{8,12},{9,13},{1... | collective-permute-start | bytes 3145736 | tf_op jit(solution)/shard_map/ppermute | solution.py:26
  97.9 22.3 %collective-permute-start.26 = (f32[8,64,512]{2,1,0:T(8,128)S(1)}, f32[8,64,512]{2,1,0:T(8,128)S(1)}, u32[]{:S(2)}, u32[]{:S(2)}) collective-permute-start(f32[8,64,512]{2,1,0:T(8,128)S(1)} %add.271), channel_id=1, source_target_pairs={{0,12},{1,13},{2,14},{3,15},{4,0},{5,1},{6,2},{7,3},{8,4},{9,5},{1... | collective-permute-start | bytes 3145736 | tf_op jit(solution)/shard_map/ppermute | solution.py:26
  109.3 25.5 %collective-permute-start.21 = (f32[2,64,512]{2,1,0:T(8,128)S(1)}, f32[2,64,512]{2,1,0:T(8,128)S(1)}, u32[]{:S(2)}, u32[]{:S(2)}) collective-permute-start(f32[2,64,512]{2,1,0:T(8,128)S(1)} %get-tuple-element.53), channel_id=1, source_target_pairs={{0,1},{1,2},{2,3},{3,0},{4,5},{5,6},{6,7},{7,4},{8,9},{9,10},{10,1... | collective-permute-start | bytes 786440 | tf_op jit(solution)/shard_map/ppermute | solution.py:26
  115.9 19.0 %collective-permute-start.22 = (f32[2,64,512]{2,1,0:T(8,128)S(1)}, f32[2,64,512]{2,1,0:T(8,128)S(1)}, u32[]{:S(2)}, u32[]{:S(2)}) collective-permute-start(f32[2,64,512]{2,1,0:T(8,128)S(1)} %get-tuple-element.52), channel_id=1, source_target_pairs={{0,2},{1,3},{2,0},{3,1},{4,6},{5,7},{6,4},{7,5},{8,10},{9,11},{10,... | collective-permute-start | bytes 786440 | tf_op jit(solution)/shard_map/ppermute | solution.py:26
  117.0 21.1 %collective-permute-start.23 = (f32[2,64,512]{2,1,0:T(8,128)S(1)}, f32[2,64,512]{2,1,0:T(8,128)S(1)}, u32[]{:S(2)}, u32[]{:S(2)}) collective-permute-start(f32[2,64,512]{2,1,0:T(8,128)S(1)} %get-tuple-element.51), channel_id=1, source_target_pairs={{0,3},{1,0},{2,1},{3,2},{4,7},{5,4},{6,5},{7,6},{8,11},{9,8},{10,9... | collective-permute-start | bytes 786440 | tf_op jit(solution)/shard_map/ppermute | solution.py:26
  120.5 17.6 %collective-permute-start.28 = (f32[2,64,512]{2,1,0:T(8,128)S(1)}, f32[2,64,512]{2,1,0:T(8,128)S(1)}, u32[]{:S(2)}, u32[]{:S(2)}) collective-permute-start(f32[2,64,512]{2,1,0:T(8,128)S(1)} %get-tuple-element.50), channel_id=1, source_target_pairs={{0,16},{1,17},{2,18},{3,19},{4,20},{5,21},{6,22},{7,23},{8,24},{9,... | collective-permute-start | bytes 786440 | tf_op jit(solution)/shard_map/ppermute | solution.py:26
  134.8 7.8 %collective-permute-start.29 = (f32[2,64,512]{2,1,0:T(8,128)S(1)}, f32[2,64,512]{2,1,0:T(8,128)S(1)}, u32[]{:S(2)}, u32[]{:S(2)}) collective-permute-start(f32[2,64,512]{2,1,0:T(8,128)S(1)} %get-tuple-element.49), channel_id=1, source_target_pairs={{0,17},{1,18},{2,19},{3,16},{4,21},{5,22},{6,23},{7,20},{8,25},{9,... | collective-permute-start | bytes 786440 | tf_op jit(solution)/shard_map/ppermute | solution.py:26
  134.8 11.8 %collective-permute-start.30 = (f32[2,64,512]{2,1,0:T(8,128)S(1)}, f32[2,64,512]{2,1,0:T(8,128)S(1)}, u32[]{:S(2)}, u32[]{:S(2)}) collective-permute-start(f32[2,64,512]{2,1,0:T(8,128)S(1)} %get-tuple-element.48), channel_id=1, source_target_pairs={{0,18},{1,19},{2,16},{3,17},{4,22},{5,23},{6,20},{7,21},{8,26},{9,... | collective-permute-start | bytes 786440 | tf_op jit(solution)/shard_map/ppermute | solution.py:26
  134.9 11.7 %collective-permute-start.31 = (f32[2,64,512]{2,1,0:T(8,128)S(1)}, f32[2,64,512]{2,1,0:T(8,128)S(1)}, u32[]{:S(2)}, u32[]{:S(2)}) collective-permute-start(f32[2,64,512]{2,1,0:T(8,128)S(1)} %get-tuple-element.47), channel_id=1, source_target_pairs={{0,19},{1,16},{2,17},{3,18},{4,23},{5,20},{6,21},{7,22},{8,27},{9,... | collective-permute-start | bytes 786440 | tf_op jit(solution)/shard_map/ppermute | solution.py:26

commit v4 on v3

--- a/solution.py
+++ b/solution.py
@@ -185,25 +185,27 @@
 
 def join_kernel(q, at_ref, *refs):
     pieces, out_ref, held = refs[:8], refs[8], refs[9]
+    wide = held.shape[1]
+    slot, columns = pl.program_id(0), pl.ds(pl.multiple_of(pl.program_id(1) * wide, wide), wide)
     for index in range(8):
         kind = at_ref[0] if index < N else 1 - at_ref[0]
         mine = at_ref[1] if index < N else at_ref[2]
         part = lax.rem(mine + N - index % N, N)
         start = pl.multiple_of((kind * N + part) * q, q)
-        for slot in range(2):
-            held[slot, pl.ds(start, q), :] = pieces[index][slot]
-    for slot in range(2):
-        out_ref[0, slot] = held[slot].T
+        held[pl.ds(start, q), :] = pieces[index][slot, :, columns]
+    out_ref[0, 0] = held[...].T
 
 
 def join(at, pieces):
     _, q, half = pieces[0].shape
+    wide = half // 2
     return pl.pallas_call(
         functools.partial(join_kernel, q),
+        grid=(2, 2),
         out_shape=jax.ShapeDtypeStruct((1, 2, half, half), jnp.float32),
         in_specs=specs(SMEM, 1) + specs(VMEM, 8),
-        out_specs=pl.BlockSpec(memory_space=VMEM),
-        scratch_shapes=[VMEM((2, half, half), jnp.float32)],
+        out_specs=pl.BlockSpec((1, 1, wide, half), lambda slot, block: (0, slot, block, 0)),
+        scratch_shapes=[VMEM((half, wide), jnp.float32)],
         compiler_params=pltpu.CompilerParams(vmem_limit_bytes=GRANT),
         cost_estimate=pl.CostEstimate(flops=10**6, bytes_accessed=16 * half * half, transcendentals=0),
         name="join",
@@ -261,17 +263,20 @@
     rest = [((own_parts,), {3: zero[3]}), ((up_parts,), {3: low[3]}), ((down_parts,), {3: high[3]})]
     own0, near0, far0, last0 = product(tab, [((beyond[0],), dict(zip(four, far)))] + rest, total, (0,), (8, 8, 8, 8))
     up_far, down_near = across(far0, 1), across(last0, -1)
-    own1, near1, far1, last1 = product(tab, [((beyond[1],), dict(zip(four, far)))] + rest, total, (1,), (8, 8, 8, 8))
+    own1, near1, near1b, far1, last1 = product(
+        tab, [((beyond[1],), dict(zip(four, far)))] + rest, total, (1,), (8, 4, 4, 8, 8)
+    )
     down_far = across(far1, -1)
     up_near = across(near1, 1)
     up_sum = across(near0 + up_far, 1)
+    up_near = [up_near, across(near1b, 1)]
     down_sum = across(last1 + down_far, -1)
 
     found, passed = [], []
     for s in range(N):
-        part = slice(2 * s, 2 * s + 2)
+        part, piece = slice(2 * s, 2 * s + 2), slice(2 * (s % 2), 2 * (s % 2) + 2)
         mine = own0[part] + up_sum[part] + down_near[part]
-        theirs = own1[part] + down_sum[part] + up_near[part]
+        theirs = own1[part] + down_sum[part] + up_near[s // 2][piece]
         found.append(mine if s == 0 else along(mine, s))
         passed.append(along_other(theirs, s))
     return join(at, found + passed)

time: 150 us -> 150 us (level)
  starting transfers between devices: 84.5 us -> 86.5 us
  waiting for transfers between devices: 36.1 us -> 34.2 us
    ppermute x22 -> x23, waiting for transfers between devices: 35.4 us -> 33.5 us  [move(): return lax.ppermute(value, ('c', 'y', 'z'), pairs)]
    ppermute x22 -> x23, starting transfers between devices: 58.5 us -> 60.5 us  [move(): return lax.ppermute(value, ('c', 'y', 'z'), pairs)]
  transfers between devices with their start and end apart: 32 -> 33, of which waited for: 10 -> 10; matrix products, arithmetic and copies ran while one was open for 2% -> 2% of each run, Pallas kernels for 14% -> 14%
where the time goes in v4:
time: 150 us; the launch traced here: 149 us
  starting transfers between devices  86.5 us (58%)
  waiting for transfers between devices  34.2 us (23%)
  Pallas kernels  23.9 us (16%)
  local copies, waits for them, and re-layouts  3.17 us (2%)
    ppermute x23, starting transfers between devices, move(): return lax.ppermute(value, ('c', 'y', 'z'), pairs)  60.5 us
    ppermute x23, waiting for transfers between devices, move(): return lax.ppermute(value, ('c', 'y', 'z'), pairs)  33.5 us
    ppermute x9, starting transfers between devices, hop(): return lax.ppermute(value, 'x', pairs)  24.6 us
    pallas_call x4, Pallas kernels, product(): pl.pallas_call(functools.partial(product_kernel, q, form, total is not No...  19.8 us
  transfers between devices with their start and end apart: 33, of which 10 were waited for; matrix products, arithmetic and copies ran while one was open for 2% of the time, Pallas kernels for 14%

profile of v4, /device:TPU:1, one launch (start us, length us, event | category | flops | bytes accessed | tf_op | source)
XLA Modules:
  0.0 149.5 jit_solution(5613692289739176102)
XLA Ops:
  0.0 1.4 collective-permute-start.2
  1.4 1.4 collective-permute-start
  2.8 1.4 collective-permute-start.15
  4.2 0.0 collective-permute-done.2.slab_ref.refs_1_
  4.3 2.5 %collective-permute-start.16 = (f32[1024,256]{1,0:T(8,128)S(1)}, f32[1024,256]{1,0:T(8,128)}, u32[]{:S(2)}, u32[]{:S(2)}) collective-permute-start(f32[1024,256]{1,0:T(8,128)S(1)} %collective-permute-done.2.slab_ref.refs_1_), channel_id=1, source_target_pairs={{0,3},{1,0},{2,1},{3,2},{4,7},{5,4},{6,5},{7,6},{8,11},{9,8},{10,9... | collective-permute-start | bytes 3145736 | tf_op jit(solution)/shard_map/ppermute | solution.py:26
  6.7 0.1 pad_add_fusion.at_ref
  6.8 1.2 copy-done
  8.0 0.6 cut.2
  8.6 0.6 cut.3
  9.2 3.9 %collective-permute-start.7 = (f32[256,256]{1,0:T(8,128)S(1)}, f32[256,256]{1,0:T(8,128)}, u32[]{:S(2)}, u32[]{:S(2)}) collective-permute-start(f32[256,256]{1,0:T(8,128)S(1)} %get-tuple-element.32.refs_2_), channel_id=1, source_target_pairs={{0,32},{32,64},{64,96},{1,33},{33,65},{65,97},{2,34},{34,66},{66,9... | collective-permute-start | bytes 786440 | tf_op jit(solution)/shard_map/ppermute | solution.py:46
  13.1 3.9 %collective-permute-done.refs_0_ = f32[1024,256]{1,0:T(8,128)} collective-permute-done((f32[1024,256]{1,0:T(8,128)}, f32[1024,256]{1,0:T(8,128)}, u32[]{:S(2)}, u32[]{:S(2)}) %collective-permute-start) | collective-permute-done | bytes 1048608 | tf_op jit(solution)/shard_map/ppermute | solution.py:26
  17.0 1.5 collective-permute-start.12
  18.5 1.2 collective-permute-start.3
  19.7 0.1 broadcast_select_fusion
  19.8 0.2 select_reduce_fusion
  20.0 0.0 collective-permute-done.7.refs_3_
  20.0 4.4 %collective-permute-start.8 = (f32[256,256]{1,0:T(8,128)S(1)}, f32[256,256]{1,0:T(8,128)S(1)}, u32[]{:S(2)}, u32[]{:S(2)}) collective-permute-start(f32[256,256]{1,0:T(8,128)S(1)} %get-tuple-element.32.refs_2_), channel_id=1, source_target_pairs={{0,96},{1,97},{2,98},{3,99},{4,100},{5,101},{6,102},{7,103},{8,104... | collective-permute-start | bytes 786440 | tf_op jit(solution)/shard_map/ppermute | solution.py:46
  24.4 0.0 collective-permute-done.11
  24.4 0.7 collective-permute-start.10
  25.1 0.4 collective-permute-done.3.refs_1_
  25.5 3.1 %collective-permute-start.4 = (f32[256,256]{1,0:T(8,128)S(1)}, f32[256,256]{1,0:T(8,128)S(1)}, u32[]{:S(2)}, u32[]{:S(2)}) collective-permute-start(f32[256,256]{1,0:T(8,128)S(1)} %collective-permute-done.3.refs_1_), channel_id=1, source_target_pairs={{0,32},{32,64},{64,96},{1,33},{33,65},{65,97},{2,34},{34,66},{66,9... | collective-permute-start | bytes 786440 | tf_op jit(solution)/shard_map/ppermute | solution.py:46
  28.6 2.5 %collective-permute-done.12 = f32[256,256]{1,0:T(8,128)} collective-permute-done((f32[256,256]{1,0:T(8,128)S(1)}, f32[256,256]{1,0:T(8,128)}, u32[]{:S(2)}, u32[]{:S(2)}) %collective-permute-start.12) | collective-permute-done | bytes 262176 | tf_op jit(solution)/shard_map/ppermute | solution.py:26
  31.1 4.4 %collective-permute-start.5 = (f32[256,256]{1,0:T(8,128)S(1)}, f32[256,256]{1,0:T(8,128)S(1)}, u32[]{:S(2)}, u32[]{:S(2)}) collective-permute-start(f32[256,256]{1,0:T(8,128)S(1)} %collective-permute-done.3.refs_1_), channel_id=1, source_target_pairs={{0,96},{1,97},{2,98},{3,99},{4,100},{5,101},{6,102},{7,103},{8,104... | collective-permute-start | bytes 786440 | tf_op jit(solution)/shard_map/ppermute | solution.py:46
  35.5 1.0 constant_dynamic-update-slice_fusion.1
  36.5 1.0 constant_dynamic-update-slice_fusion.refs_2_.refs_7_
  37.4 0.0 collective-permute-done.8.refs_4_
  37.5 6.1 %collective-permute-start.1 = (f32[1024,256]{1,0:T(8,128)}, f32[1024,256]{1,0:T(8,128)S(1)}, u32[]{:S(2)}, u32[]{:S(2)}) collective-permute-start(f32[1024,256]{1,0:T(8,128)} %collective-permute-done.refs_0_), channel_id=1, source_target_pairs={{0,1},{1,2},{2,3},{3,0},{4,5},{5,6},{6,7},{7,4},{8,9},{9,10},{10,1... | collective-permute-start | bytes 3145736 | tf_op jit(solution)/shard_map/ppermute | solution.py:26
  43.6 0.0 collective-permute-done.4.refs_2_
  43.6 1.3 collective-permute-start.13
  44.9 0.0 collective-permute-done.5.refs_3_
  44.9 1.9 %collective-permute-start.14 = (f32[512,256]{1,0:T(8,128)S(1)}, f32[512,256]{1,0:T(8,128)S(1)}, u32[]{:S(2)}, u32[]{:S(2)}) collective-permute-start(f32[512,256]{1,0:T(8,128)S(1)} %constant_dynamic-update-slice_fusion.refs_2_.refs_7_), channel_id=1, source_target_pairs={{0,96},{32,0},{1,97},{33,1},{2,98},{34,2},{3,99},{35,3},{4,100},{3... | collective-permute-start | bytes 1572872 | tf_op jit(solution)/shard_map/ppermute | solution.py:46
  46.8 0.0 collective-permute-done.16.refs_6_
  46.8 5.4 %collective-permute-start.24 = (f32[1024,256]{1,0:T(8,128)}, f32[1024,256]{1,0:T(8,128)S(1)}, u32[]{:S(2)}, u32[]{:S(2)}) collective-permute-start(f32[1024,256]{1,0:T(8,128)} %collective-permute-done.16.refs_6_), channel_id=1, source_target_pairs={{0,3},{1,0},{2,1},{3,2},{4,7},{5,4},{6,5},{7,6},{8,11},{9,8},{10,9... | collective-permute-start | bytes 3145736 | tf_op jit(solution)/shard_map/ppermute | solution.py:26
  52.2 3.7 %shard_map.28 = (f32[8,768,256]{2,1,0:T(8,128)S(1)}, bf16[2048,512]{1,0:T(8,128)(2,1)S(1)}) custom-call(s32[64]{0:T(128)S(1)} %broadcast_add_fusion.2.tab_ref, f32[1024,256]{1,0:T(8,128)S(1)} %copy-done.1, f32[1024,256]{1,0:T(8,128)S(1)} %collective-permute-done.2.slab_ref.refs_1_, f32[256,256]{1,0:T(8,128)S(1)} %get-tuple-element.32.refs_2_, ...), custom_call_target="tpu_custom_call" | custom-call | flops 6442450944 | bytes 12582912 | tf_op jit(solution)/shard_map/pallas_call | solution.py:172
  55.9 0.7 collective-permute-start.9
  56.6 0.7 collective-permute-done.14.refs_4_.refs_9_
  57.3 0.7 collective-permute-start.6
  58.0 4.2 %collective-permute-start.17 = (f32[512,256]{1,0:T(8,128)S(1)}, f32[512,256]{1,0:T(8,128)S(1)}, u32[]{:S(2)}, u32[]{:S(2)}) collective-permute-start(f32[512,256]{1,0:T(8,128)S(1)} %collective-permute-done.14.refs_4_.refs_9_), channel_id=1, source_target_pairs={{0,96},{96,64},{1,97},{97,65},{2,98},{98,66},{3,99},{99,67},{4,100... | collective-permute-start | bytes 1572872 | tf_op jit(solution)/shard_map/ppermute | solution.py:46
  62.2 7.6 %shard_map.29 = (f32[8,768,256]{2,1,0:T(8,128)S(1)}, bf16[2048,512]{1,0:T(8,128)(2,1)S(1)}, bf16[2048,512]{1,0:T(8,128)(2,1)S(1)}) custom-call(s32[64]{0:T(128)S(1)} %broadcast_add_fusion.2.tab_ref, f32[1024,256]{1,0:T(8,128)} %collective-permute-done.refs_0_, f32[1024,256]{1,0:T(8,128)S(1)} %collective-permute-done.10.refs_1_, ...), custom_call_target="tpu_custom_call", output_to_operand_aliasing={{0}: (11, {})} | custom-call | flops 6442450944 | bytes 12582912 | tf_op jit(solution)/shard_map/pallas_call | solution.py:172
  69.9 4.3 %shard_map.30 = (f32[8,64,512]{2,1,0:T(8,128)S(1)}, f32[8,64,512]{2,1,0:T(8,128)S(1)}, f32[8,64,512]{2,1,0:T(8,128)S(1)}, f32[8,64,512]{2,1,0:T(8,128)S(1)}) custom-call(s32[64]{0:T(128)S(1)} %broadcast_add_fusion.2.tab_ref, f32[1024,256]{1,0:T(8,128)S(1)} %collective-permute-done.1.refs_0_, f32[256,256]{1,0:T(8,128)S(1)} %collective-permute-done.3.refs_1_, ...), custom_call_target="tpu_custom_call" | custom-call | flops 3221225472 | bytes 12582912 | tf_op jit(solution)/shard_map/pallas_call | solution.py:172
  74.1 0.1 collective-permute-start.18
  74.2 4.3 %shard_map.31 = (f32[8,64,512]{2,1,0:T(8,128)S(1)}, f32[4,64,512]{2,1,0:T(8,128)S(1)}, f32[4,64,512]{2,1,0:T(8,128)S(1)}, f32[8,64,512]{2,1,0:T(8,128)S(1)}, f32[8,64,512]{2,1,0:T(8,128)S(1)}) custom-call(s32[64]{0:T(128)S(1)} %broadcast_add_fusion.2.tab_ref, f32[1024,256]{1,0:T(8,128)S(1)} %collective-permute-done.24.refs_0_, ...), custom_call_target="tpu_custom_call" | custom-call | flops 3221225472 | bytes 12582912 | tf_op jit(solution)/shard_map/pallas_call | solution.py:172
  78.5 4.0 %collective-permute-start.25 = (f32[8,64,512]{2,1,0:T(8,128)S(1)}, f32[8,64,512]{2,1,0:T(8,128)S(1)}, u32[]{:S(2)}, u32[]{:S(2)}) collective-permute-start(f32[8,64,512]{2,1,0:T(8,128)S(1)} %get-tuple-element.46), channel_id=1, source_target_pairs={{0,12},{1,13},{2,14},{3,15},{4,0},{5,1},{6,2},{7,3},{8,4},{9,5},{1... | collective-permute-start | bytes 3145736 | tf_op jit(solution)/shard_map/ppermute | solution.py:26
  82.5 3.4 %collective-permute-start.20 = (f32[8,64,512]{2,1,0:T(8,128)S(1)}, f32[8,64,512]{2,1,0:T(8,128)S(1)}, u32[]{:S(2)}, u32[]{:S(2)}) collective-permute-start(f32[8,64,512]{2,1,0:T(8,128)S(1)} %get-tuple-element.43), channel_id=1, source_target_pairs={{0,12},{1,13},{2,14},{3,15},{4,0},{5,1},{6,2},{7,3},{8,4},{9,5},{1... | collective-permute-start | bytes 3145736 | tf_op jit(solution)/shard_map/ppermute | solution.py:26
  85.9 4.7 %collective-permute-done.18 = f32[8,64,512]{2,1,0:T(8,128)S(1)} collective-permute-done((f32[8,64,512]{2,1,0:T(8,128)S(1)}, f32[8,64,512]{2,1,0:T(8,128)S(1)}, u32[]{:S(2)}, u32[]{:S(2)}) %collective-permute-start.18) | collective-permute-done | bytes 1048608 | tf_op jit(solution)/shard_map/ppermute | solution.py:26
  90.6 0.2 add.262
  90.8 2.1 %collective-permute-start.19 = (f32[8,64,512]{2,1,0:T(8,128)S(1)}, f32[8,64,512]{2,1,0:T(8,128)S(1)}, u32[]{:S(2)}, u32[]{:S(2)}) collective-permute-start(f32[8,64,512]{2,1,0:T(8,128)S(1)} %add.262), channel_id=1, source_target_pairs={{0,4},{1,5},{2,6},{3,7},{4,8},{5,9},{6,10},{7,11},{8,12},{9,13},{1... | collective-permute-start | bytes 3145736 | tf_op jit(solution)/shard_map/ppermute | solution.py:26
  92.9 4.8 %collective-permute-done.25 = f32[8,64,512]{2,1,0:T(8,128)S(1)} collective-permute-done((f32[8,64,512]{2,1,0:T(8,128)S(1)}, f32[8,64,512]{2,1,0:T(8,128)S(1)}, u32[]{:S(2)}, u32[]{:S(2)}) %collective-permute-start.25) | collective-permute-done | bytes 1048608 | tf_op jit(solution)/shard_map/ppermute | solution.py:26
  97.7 0.2 add.271
  97.9 0.3 collective-permute-start.26
  98.2 1.5 %collective-permute-start.27 = (f32[4,64,512]{2,1,0:T(8,128)S(1)}, f32[4,64,512]{2,1,0:T(8,128)S(1)}, u32[]{:S(2)}, u32[]{:S(2)}) collective-permute-start(f32[4,64,512]{2,1,0:T(8,128)S(1)} %get-tuple-element.47), channel_id=1, source_target_pairs={{0,4},{1,5},{2,6},{3,7},{4,8},{5,9},{6,10},{7,11},{8,12},{9,13},{1... | collective-permute-start | bytes 1572872 | tf_op jit(solution)/shard_map/ppermute | solution.py:26
  99.8 1.4 collective-permute-start.30
  101.1 7.8 %collective-permute-done.20 = f32[8,64,512]{2,1,0:T(8,128)S(1)} collective-permute-done((f32[8,64,512]{2,1,0:T(8,128)S(1)}, f32[8,64,512]{2,1,0:T(8,128)S(1)}, u32[]{:S(2)}, u32[]{:S(2)}) %collective-permute-start.20) | collective-permute-done | bytes 1048608 | tf_op jit(solution)/shard_map/ppermute | solution.py:26
  108.9 0.3 slice_add_fusion.8
  109.3 6.6 %collective-permute-start.21 = (f32[2,64,512]{2,1,0:T(8,128)S(1)}, f32[2,64,512]{2,1,0:T(8,128)S(1)}, u32[]{:S(2)}, u32[]{:S(2)}) collective-permute-start(f32[2,64,512]{2,1,0:T(8,128)S(1)} %get-tuple-element.51), channel_id=1, source_target_pairs={{0,1},{1,2},{2,3},{3,0},{4,5},{5,6},{6,7},{7,4},{8,9},{9,10},{10,1... | collective-permute-start | bytes 786440 | tf_op jit(solution)/shard_map/ppermute | solution.py:26
  115.9 1.1 collective-permute-start.22
  117.0 2.4 %collective-permute-start.23 = (f32[2,64,512]{2,1,0:T(8,128)S(1)}, f32[2,64,512]{2,1,0:T(8,128)S(1)}, u32[]{:S(2)}, u32[]{:S(2)}) collective-permute-start(f32[2,64,512]{2,1,0:T(8,128)S(1)} %get-tuple-element.49), channel_id=1, source_target_pairs={{0,3},{1,0},{2,1},{3,2},{4,7},{5,4},{6,5},{7,6},{8,11},{9,8},{10,9... | collective-permute-start | bytes 786440 | tf_op jit(solution)/shard_map/ppermute | solution.py:26
  119.4 0.8 collective-permute-done.26
  120.2 0.3 slice_add_fusion
  120.5 14.3 %collective-permute-start.28 = (f32[2,64,512]{2,1,0:T(8,128)S(1)}, f32[2,64,512]{2,1,0:T(8,128)S(1)}, u32[]{:S(2)}, u32[]{:S(2)}) collective-permute-start(f32[2,64,512]{2,1,0:T(8,128)S(1)} %get-tuple-element.57), channel_id=1, source_target_pairs={{0,16},{1,17},{2,18},{3,19},{4,20},{5,21},{6,22},{7,23},{8,24},{9,... | collective-permute-start | bytes 786440 | tf_op jit(solution)/shard_map/ppermute | solution.py:26
  134.8 3.3 %collective-permute-start.32 = (f32[2,64,512]{2,1,0:T(8,128)S(1)}, f32[2,64,512]{2,1,0:T(8,128)S(1)}, u32[]{:S(2)}, u32[]{:S(2)}) collective-permute-start(f32[2,64,512]{2,1,0:T(8,128)S(1)} %get-tuple-element.53), channel_id=1, source_target_pairs={{0,19},{1,16},{2,17},{3,18},{4,23},{5,20},{6,21},{7,22},{8,27},{9,... | collective-permute-start | bytes 786440 | tf_op jit(solution)/shard_map/ppermute | solution.py:26
  138.1 4.5 %collective-permute-done.29.refs_5_ = f32[2,64,512]{2,1,0:T(8,128)S(1)} collective-permute-done((f32[2,64,512]{2,1,0:T(8,128)S(1)}, f32[2,64,512]{2,1,0:T(8,128)S(1)}, u32[]{:S(2)}, u32[]{:S(2)}) %collective-permute-start.29) | collective-permute-done | bytes 262176 | tf_op jit(solution)/shard_map/ppermute | solution.py:26
  142.6 4.0 %collective-permute-done.31.refs_6_ = f32[2,64,512]{2,1,0:T(8,128)S(1)} collective-permute-done((f32[2,64,512]{2,1,0:T(8,128)S(1)}, f32[2,64,512]{2,1,0:T(8,128)S(1)}, u32[]{:S(2)}, u32[]{:S(2)}) %collective-permute-start.31) | collective-permute-done | bytes 262176 | tf_op jit(solution)/shard_map/ppermute | solution.py:26
  146.6 2.9 %join.1 = f32[1,2,512,512]{3,2,1,0:T(8,128)} custom-call(s32[3]{0:T(128)S(1)} %pad_add_fusion.at_ref, f32[2,64,512]{2,1,0:T(8,128)S(1)} %get-tuple-element.52.refs_0_, f32[2,64,512]{2,1,0:T(8,128)S(1)} %collective-permute-done.21.refs_1_, f32[2,64,512]{2,1,0:T(8,128)S(1)} %collective-permute-done.22.refs_2_, ...), custom_call_target="tpu_custom_call" | custom-call | flops 1000000 | bytes 4194304 | tf_op jit(solution)/shard_map/join/pallas_call | solution.py:202
  (29 shorter events, 0.1 us)
Async XLA Ops:
  0.0 19.8 %copy-start.2 = (s32[16,16]{1,0:T(8,128)S(1)}, s32[16,16]{1,0:T(8,128)}, u32[]{:S(2)}) copy-start(s32[16,16]{1,0:T(8,128)} %param.3) | copy-start | bytes 3076
  0.0 4.2 %collective-permute-start.2 = (f32[1024,256]{1,0:T(8,128)}, f32[1024,256]{1,0:T(8,128)S(1)}, u32[]{:S(2)}, u32[]{:S(2)}) collective-permute-start(f32[1024,256]{1,0:T(8,128)} %refs_0_.1), channel_id=1, source_target_pairs={{0,16},{16,0},{1,17},{17,1},{2,18},{18,2},{3,19},{19,3},{4,20},{20... | collective-permute-start | bytes 3145736 | tf_op jit(solution)/shard_map/ppermute | solution.py:42
  1.4 15.6 %collective-permute-start = (f32[1024,256]{1,0:T(8,128)}, f32[1024,256]{1,0:T(8,128)}, u32[]{:S(2)}, u32[]{:S(2)}) collective-permute-start(f32[1024,256]{1,0:T(8,128)} %refs_0_.1), channel_id=1, source_target_pairs={{0,1},{1,2},{2,3},{3,0},{4,5},{5,6},{6,7},{7,4},{8,9},{9,10},{10,1... | collective-permute-start | bytes 3145736 | tf_op jit(solution)/shard_map/ppermute | solution.py:26
  2.8 15.7 %collective-permute-start.15 = (f32[1024,256]{1,0:T(8,128)}, f32[1024,256]{1,0:T(8,128)}, u32[]{:S(2)}, u32[]{:S(2)}) collective-permute-start(f32[1024,256]{1,0:T(8,128)} %refs_0_.1), channel_id=1, source_target_pairs={{0,3},{1,0},{2,1},{3,2},{4,7},{5,4},{6,5},{7,6},{8,11},{9,8},{10,9... | collective-permute-start | bytes 3145736 | tf_op jit(solution)/shard_map/ppermute | solution.py:26
  4.3 42.6 %collective-permute-start.16 = (f32[1024,256]{1,0:T(8,128)S(1)}, f32[1024,256]{1,0:T(8,128)}, u32[]{:S(2)}, u32[]{:S(2)}) collective-permute-start(f32[1024,256]{1,0:T(8,128)S(1)} %collective-permute-done.2.slab_ref.refs_1_), channel_id=1, source_target_pairs={{0,3},{1,0},{2,1},{3,2},{4,7},{5,4},{6,5},{7,6},{8,11},{9,8},{10,9... | collective-permute-start | bytes 3145736 | tf_op jit(solution)/shard_map/ppermute | solution.py:26
  6.8 1.2 copy-start
  8.0 44.2 %copy-start.1 = (f32[1024,256]{1,0:T(8,128)S(1)}, f32[1024,256]{1,0:T(8,128)}, u32[]{:S(2)}) copy-start(f32[1024,256]{1,0:T(8,128)} %refs_0_.1) | copy-start | bytes 3145732
  9.2 10.8 %collective-permute-start.7 = (f32[256,256]{1,0:T(8,128)S(1)}, f32[256,256]{1,0:T(8,128)}, u32[]{:S(2)}, u32[]{:S(2)}) collective-permute-start(f32[256,256]{1,0:T(8,128)S(1)} %get-tuple-element.32.refs_2_), channel_id=1, source_target_pairs={{0,32},{32,64},{64,96},{1,33},{33,65},{65,97},{2,34},{34,66},{66,9... | collective-permute-start | bytes 786440 | tf_op jit(solution)/shard_map/ppermute | solution.py:46
  13.1 11.3 %collective-permute-start.11 = (f32[256,256]{1,0:T(8,128)S(1)}, f32[256,256]{1,0:T(8,128)}, u32[]{:S(2)}, u32[]{:S(2)}) collective-permute-start(f32[256,256]{1,0:T(8,128)S(1)} %get-tuple-element.34), channel_id=1, source_target_pairs={{0,1},{1,2},{2,3},{3,0},{4,5},{5,6},{6,7},{7,4},{8,9},{9,10},{10,1... | collective-permute-start | bytes 786440 | tf_op jit(solution)/shard_map/ppermute | solution.py:26
  17.0 14.1 %collective-permute-start.12 = (f32[256,256]{1,0:T(8,128)S(1)}, f32[256,256]{1,0:T(8,128)}, u32[]{:S(2)}, u32[]{:S(2)}) collective-permute-start(f32[256,256]{1,0:T(8,128)S(1)} %get-tuple-element.35), channel_id=1, source_target_pairs={{0,3},{1,0},{2,1},{3,2},{4,7},{5,4},{6,5},{7,6},{8,11},{9,8},{10,9... | collective-permute-start | bytes 786440 | tf_op jit(solution)/shard_map/ppermute | solution.py:26
  18.5 7.0 %collective-permute-start.3 = (f32[256,256]{1,0:T(8,128)S(1)}, f32[256,256]{1,0:T(8,128)S(1)}, u32[]{:S(2)}, u32[]{:S(2)}) collective-permute-start(f32[256,256]{1,0:T(8,128)S(1)} %get-tuple-element.31), channel_id=1, source_target_pairs={{0,2},{1,3},{2,0},{3,1},{4,6},{5,7},{6,4},{7,5},{8,10},{9,11},{10,... | collective-permute-start | bytes 786440 | tf_op jit(solution)/shard_map/ppermute | solution.py:26
  20.0 17.5 %collective-permute-start.8 = (f32[256,256]{1,0:T(8,128)S(1)}, f32[256,256]{1,0:T(8,128)S(1)}, u32[]{:S(2)}, u32[]{:S(2)}) collective-permute-start(f32[256,256]{1,0:T(8,128)S(1)} %get-tuple-element.32.refs_2_), channel_id=1, source_target_pairs={{0,96},{1,97},{2,98},{3,99},{4,100},{5,101},{6,102},{7,103},{8,104... | collective-permute-start | bytes 786440 | tf_op jit(solution)/shard_map/ppermute | solution.py:46
  24.4 33.5 %collective-permute-start.10 = (f32[1024,256]{1,0:T(8,128)S(1)}, f32[1024,256]{1,0:T(8,128)S(1)}, u32[]{:S(2)}, u32[]{:S(2)}) collective-permute-start(f32[1024,256]{1,0:T(8,128)S(1)} %collective-permute-done.2.slab_ref.refs_1_), channel_id=1, source_target_pairs={{0,1},{1,2},{2,3},{3,0},{4,5},{5,6},{6,7},{7,4},{8,9},{9,10},{10,1... | collective-permute-start | bytes 3145736 | tf_op jit(solution)/shard_map/ppermute | solution.py:26
  25.5 18.0 %collective-permute-start.4 = (f32[256,256]{1,0:T(8,128)S(1)}, f32[256,256]{1,0:T(8,128)S(1)}, u32[]{:S(2)}, u32[]{:S(2)}) collective-permute-start(f32[256,256]{1,0:T(8,128)S(1)} %collective-permute-done.3.refs_1_), channel_id=1, source_target_pairs={{0,32},{32,64},{64,96},{1,33},{33,65},{65,97},{2,34},{34,66},{66,9... | collective-permute-start | bytes 786440 | tf_op jit(solution)/shard_map/ppermute | solution.py:46
  31.1 13.8 %collective-permute-start.5 = (f32[256,256]{1,0:T(8,128)S(1)}, f32[256,256]{1,0:T(8,128)S(1)}, u32[]{:S(2)}, u32[]{:S(2)}) collective-permute-start(f32[256,256]{1,0:T(8,128)S(1)} %collective-permute-done.3.refs_1_), channel_id=1, source_target_pairs={{0,96},{1,97},{2,98},{3,99},{4,100},{5,101},{6,102},{7,103},{8,104... | collective-permute-start | bytes 786440 | tf_op jit(solution)/shard_map/ppermute | solution.py:46
  37.5 32.4 %collective-permute-start.1 = (f32[1024,256]{1,0:T(8,128)}, f32[1024,256]{1,0:T(8,128)S(1)}, u32[]{:S(2)}, u32[]{:S(2)}) collective-permute-start(f32[1024,256]{1,0:T(8,128)} %collective-permute-done.refs_0_), channel_id=1, source_target_pairs={{0,1},{1,2},{2,3},{3,0},{4,5},{5,6},{6,7},{7,4},{8,9},{9,10},{10,1... | collective-permute-start | bytes 3145736 | tf_op jit(solution)/shard_map/ppermute | solution.py:26
  43.6 12.3 %collective-permute-start.13 = (f32[512,256]{1,0:T(8,128)S(1)}, f32[512,256]{1,0:T(8,128)S(1)}, u32[]{:S(2)}, u32[]{:S(2)}) collective-permute-start(f32[512,256]{1,0:T(8,128)S(1)} %constant_dynamic-update-slice_fusion.refs_2_.refs_7_), channel_id=1, source_target_pairs={{0,32},{32,64},{64,96},{1,33},{33,65},{65,97},{2,34},{34,66},{66,9... | collective-permute-start | bytes 1572872 | tf_op jit(solution)/shard_map/ppermute | solution.py:46
  44.9 12.4 %collective-permute-start.14 = (f32[512,256]{1,0:T(8,128)S(1)}, f32[512,256]{1,0:T(8,128)S(1)}, u32[]{:S(2)}, u32[]{:S(2)}) collective-permute-start(f32[512,256]{1,0:T(8,128)S(1)} %constant_dynamic-update-slice_fusion.refs_2_.refs_7_), channel_id=1, source_target_pairs={{0,96},{32,0},{1,97},{33,1},{2,98},{34,2},{3,99},{35,3},{4,100},{3... | collective-permute-start | bytes 1572872 | tf_op jit(solution)/shard_map/ppermute | solution.py:46
  46.8 27.4 %collective-permute-start.24 = (f32[1024,256]{1,0:T(8,128)}, f32[1024,256]{1,0:T(8,128)S(1)}, u32[]{:S(2)}, u32[]{:S(2)}) collective-permute-start(f32[1024,256]{1,0:T(8,128)} %collective-permute-done.16.refs_6_), channel_id=1, source_target_pairs={{0,3},{1,0},{2,1},{3,2},{4,7},{5,4},{6,5},{7,6},{8,11},{9,8},{10,9... | collective-permute-start | bytes 3145736 | tf_op jit(solution)/shard_map/ppermute | solution.py:26
  55.9 13.9 %collective-permute-start.9 = (f32[256,256]{1,0:T(8,128)}, f32[256,256]{1,0:T(8,128)S(1)}, u32[]{:S(2)}, u32[]{:S(2)}) collective-permute-start(f32[256,256]{1,0:T(8,128)} %collective-permute-done.7.refs_3_), channel_id=1, source_target_pairs={{32,64},{64,96},{33,65},{65,97},{34,66},{66,98},{35,67},{67,99},{3... | collective-permute-start | bytes 786440 | tf_op jit(solution)/shard_map/ppermute | solution.py:46
  57.3 12.6 %collective-permute-start.6 = (f32[256,256]{1,0:T(8,128)S(1)}, f32[256,256]{1,0:T(8,128)S(1)}, u32[]{:S(2)}, u32[]{:S(2)}) collective-permute-start(f32[256,256]{1,0:T(8,128)S(1)} %collective-permute-done.4.refs_2_), channel_id=1, source_target_pairs={{32,64},{64,96},{33,65},{65,97},{34,66},{66,98},{35,67},{67,99},{3... | collective-permute-start | bytes 786440 | tf_op jit(solution)/shard_map/ppermute | solution.py:46
  58.0 11.9 %collective-permute-start.17 = (f32[512,256]{1,0:T(8,128)S(1)}, f32[512,256]{1,0:T(8,128)S(1)}, u32[]{:S(2)}, u32[]{:S(2)}) collective-permute-start(f32[512,256]{1,0:T(8,128)S(1)} %collective-permute-done.14.refs_4_.refs_9_), channel_id=1, source_target_pairs={{0,96},{96,64},{1,97},{97,65},{2,98},{98,66},{3,99},{99,67},{4,100... | collective-permute-start | bytes 1572872 | tf_op jit(solution)/shard_map/ppermute | solution.py:46
  74.1 16.5 %collective-permute-start.18 = (f32[8,64,512]{2,1,0:T(8,128)S(1)}, f32[8,64,512]{2,1,0:T(8,128)S(1)}, u32[]{:S(2)}, u32[]{:S(2)}) collective-permute-start(f32[8,64,512]{2,1,0:T(8,128)S(1)} %get-tuple-element.42), channel_id=1, source_target_pairs={{0,4},{1,5},{2,6},{3,7},{4,8},{5,9},{6,10},{7,11},{8,12},{9,13},{1... | collective-permute-start | bytes 3145736 | tf_op jit(solution)/shard_map/ppermute | solution.py:26
  78.5 19.2 %collective-permute-start.25 = (f32[8,64,512]{2,1,0:T(8,128)S(1)}, f32[8,64,512]{2,1,0:T(8,128)S(1)}, u32[]{:S(2)}, u32[]{:S(2)}) collective-permute-start(f32[8,64,512]{2,1,0:T(8,128)S(1)} %get-tuple-element.46), channel_id=1, source_target_pairs={{0,12},{1,13},{2,14},{3,15},{4,0},{5,1},{6,2},{7,3},{8,4},{9,5},{1... | collective-permute-start | bytes 3145736 | tf_op jit(solution)/shard_map/ppermute | solution.py:26
  82.5 26.5 %collective-permute-start.20 = (f32[8,64,512]{2,1,0:T(8,128)S(1)}, f32[8,64,512]{2,1,0:T(8,128)S(1)}, u32[]{:S(2)}, u32[]{:S(2)}) collective-permute-start(f32[8,64,512]{2,1,0:T(8,128)S(1)} %get-tuple-element.43), channel_id=1, source_target_pairs={{0,12},{1,13},{2,14},{3,15},{4,0},{5,1},{6,2},{7,3},{8,4},{9,5},{1... | collective-permute-start | bytes 3145736 | tf_op jit(solution)/shard_map/ppermute | solution.py:26
  90.8 18.1 %collective-permute-start.19 = (f32[8,64,512]{2,1,0:T(8,128)S(1)}, f32[8,64,512]{2,1,0:T(8,128)S(1)}, u32[]{:S(2)}, u32[]{:S(2)}) collective-permute-start(f32[8,64,512]{2,1,0:T(8,128)S(1)} %add.262), channel_id=1, source_target_pairs={{0,4},{1,5},{2,6},{3,7},{4,8},{5,9},{6,10},{7,11},{8,12},{9,13},{1... | collective-permute-start | bytes 3145736 | tf_op jit(solution)/shard_map/ppermute | solution.py:26
  97.9 22.3 %collective-permute-start.26 = (f32[8,64,512]{2,1,0:T(8,128)S(1)}, f32[8,64,512]{2,1,0:T(8,128)S(1)}, u32[]{:S(2)}, u32[]{:S(2)}) collective-permute-start(f32[8,64,512]{2,1,0:T(8,128)S(1)} %add.271), channel_id=1, source_target_pairs={{0,12},{1,13},{2,14},{3,15},{4,0},{5,1},{6,2},{7,3},{8,4},{9,5},{1... | collective-permute-start | bytes 3145736 | tf_op jit(solution)/shard_map/ppermute | solution.py:26
  98.2 18.7 %collective-permute-start.27 = (f32[4,64,512]{2,1,0:T(8,128)S(1)}, f32[4,64,512]{2,1,0:T(8,128)S(1)}, u32[]{:S(2)}, u32[]{:S(2)}) collective-permute-start(f32[4,64,512]{2,1,0:T(8,128)S(1)} %get-tuple-element.47), channel_id=1, source_target_pairs={{0,4},{1,5},{2,6},{3,7},{4,8},{5,9},{6,10},{7,11},{8,12},{9,13},{1... | collective-permute-start | bytes 1572872 | tf_op jit(solution)/shard_map/ppermute | solution.py:26
  99.8 19.6 %collective-permute-start.30 = (f32[4,64,512]{2,1,0:T(8,128)S(1)}, f32[4,64,512]{2,1,0:T(8,128)S(1)}, u32[]{:S(2)}, u32[]{:S(2)}) collective-permute-start(f32[4,64,512]{2,1,0:T(8,128)S(1)} %get-tuple-element.48), channel_id=1, source_target_pairs={{0,4},{1,5},{2,6},{3,7},{4,8},{5,9},{6,10},{7,11},{8,12},{9,13},{1... | collective-permute-start | bytes 1572872 | tf_op jit(solution)/shard_map/ppermute | solution.py:26
  109.3 25.5 %collective-permute-start.21 = (f32[2,64,512]{2,1,0:T(8,128)S(1)}, f32[2,64,512]{2,1,0:T(8,128)S(1)}, u32[]{:S(2)}, u32[]{:S(2)}) collective-permute-start(f32[2,64,512]{2,1,0:T(8,128)S(1)} %get-tuple-element.51), channel_id=1, source_target_pairs={{0,1},{1,2},{2,3},{3,0},{4,5},{5,6},{6,7},{7,4},{8,9},{9,10},{10,1... | collective-permute-start | bytes 786440 | tf_op jit(solution)/shard_map/ppermute | solution.py:26
  115.9 19.0 %collective-permute-start.22 = (f32[2,64,512]{2,1,0:T(8,128)S(1)}, f32[2,64,512]{2,1,0:T(8,128)S(1)}, u32[]{:S(2)}, u32[]{:S(2)}) collective-permute-start(f32[2,64,512]{2,1,0:T(8,128)S(1)} %get-tuple-element.50), channel_id=1, source_target_pairs={{0,2},{1,3},{2,0},{3,1},{4,6},{5,7},{6,4},{7,5},{8,10},{9,11},{10,... | collective-permute-start | bytes 786440 | tf_op jit(solution)/shard_map/ppermute | solution.py:26
  117.0 21.2 %collective-permute-start.23 = (f32[2,64,512]{2,1,0:T(8,128)S(1)}, f32[2,64,512]{2,1,0:T(8,128)S(1)}, u32[]{:S(2)}, u32[]{:S(2)}) collective-permute-start(f32[2,64,512]{2,1,0:T(8,128)S(1)} %get-tuple-element.49), channel_id=1, source_target_pairs={{0,3},{1,0},{2,1},{3,2},{4,7},{5,4},{6,5},{7,6},{8,11},{9,8},{10,9... | collective-permute-start | bytes 786440 | tf_op jit(solution)/shard_map/ppermute | solution.py:26
  120.5 17.6 %collective-permute-start.28 = (f32[2,64,512]{2,1,0:T(8,128)S(1)}, f32[2,64,512]{2,1,0:T(8,128)S(1)}, u32[]{:S(2)}, u32[]{:S(2)}) collective-permute-start(f32[2,64,512]{2,1,0:T(8,128)S(1)} %get-tuple-element.57), channel_id=1, source_target_pairs={{0,16},{1,17},{2,18},{3,19},{4,20},{5,21},{6,22},{7,23},{8,24},{9,... | collective-permute-start | bytes 786440 | tf_op jit(solution)/shard_map/ppermute | solution.py:26
  134.8 7.8 %collective-permute-start.29 = (f32[2,64,512]{2,1,0:T(8,128)S(1)}, f32[2,64,512]{2,1,0:T(8,128)S(1)}, u32[]{:S(2)}, u32[]{:S(2)}) collective-permute-start(f32[2,64,512]{2,1,0:T(8,128)S(1)} %get-tuple-element.58), channel_id=1, source_target_pairs={{0,17},{1,18},{2,19},{3,16},{4,21},{5,22},{6,23},{7,20},{8,25},{9,... | collective-permute-start | bytes 786440 | tf_op jit(solution)/shard_map/ppermute | solution.py:26
  134.8 11.8 %collective-permute-start.31 = (f32[2,64,512]{2,1,0:T(8,128)S(1)}, f32[2,64,512]{2,1,0:T(8,128)S(1)}, u32[]{:S(2)}, u32[]{:S(2)}) collective-permute-start(f32[2,64,512]{2,1,0:T(8,128)S(1)} %get-tuple-element.54), channel_id=1, source_target_pairs={{0,18},{1,19},{2,16},{3,17},{4,22},{5,23},{6,20},{7,21},{8,26},{9,... | collective-permute-start | bytes 786440 | tf_op jit(solution)/shard_map/ppermute | solution.py:26
  134.8 11.7 %collective-permute-start.32 = (f32[2,64,512]{2,1,0:T(8,128)S(1)}, f32[2,64,512]{2,1,0:T(8,128)S(1)}, u32[]{:S(2)}, u32[]{:S(2)}) collective-permute-start(f32[2,64,512]{2,1,0:T(8,128)S(1)} %get-tuple-element.53), channel_id=1, source_target_pairs={{0,19},{1,16},{2,17},{3,18},{4,23},{5,20},{6,21},{7,22},{8,27},{9,... | collective-permute-start | bytes 786440 | tf_op jit(solution)/shard_map/ppermute | solution.py:26

commit v5 on v3

--- a/solution.py
+++ b/solution.py
@@ -261,17 +261,20 @@
     rest = [((own_parts,), {3: zero[3]}), ((up_parts,), {3: low[3]}), ((down_parts,), {3: high[3]})]
     own0, near0, far0, last0 = product(tab, [((beyond[0],), dict(zip(four, far)))] + rest, total, (0,), (8, 8, 8, 8))
     up_far, down_near = across(far0, 1), across(last0, -1)
-    own1, near1, far1, last1 = product(tab, [((beyond[1],), dict(zip(four, far)))] + rest, total, (1,), (8, 8, 8, 8))
+    own1, near1, near1b, far1, last1 = product(
+        tab, [((beyond[1],), dict(zip(four, far)))] + rest, total, (1,), (8, 4, 4, 8, 8)
+    )
     down_far = across(far1, -1)
     up_near = across(near1, 1)
     up_sum = across(near0 + up_far, 1)
+    up_near = [up_near, across(near1b, 1)]
     down_sum = across(last1 + down_far, -1)
 
     found, passed = [], []
     for s in range(N):
-        part = slice(2 * s, 2 * s + 2)
+        part, piece = slice(2 * s, 2 * s + 2), slice(2 * (s % 2), 2 * (s % 2) + 2)
         mine = own0[part] + up_sum[part] + down_near[part]
-        theirs = own1[part] + down_sum[part] + up_near[part]
+        theirs = own1[part] + down_sum[part] + up_near[s // 2][piece]
         found.append(mine if s == 0 else along(mine, s))
         passed.append(along_other(theirs, s))
     return join(at, found + passed)

time: 150 us -> 150 us (level)
  starting transfers between devices: 84.5 us -> 86.5 us
  waiting for transfers between devices: 36.1 us -> 34.2 us
    ppermute x22 -> x23, waiting for transfers between devices: 35.4 us -> 33.5 us  [move(): return lax.ppermute(value, ('c', 'y', 'z'), pairs)]
    ppermute x22 -> x23, starting transfers between devices: 58.5 us -> 60.5 us  [move(): return lax.ppermute(value, ('c', 'y', 'z'), pairs)]
  transfers between devices with their start and end apart: 32 -> 33, of which waited for: 10 -> 10; matrix products, arithmetic and copies ran while one was open for 2% -> 2% of each run, Pallas kernels for 14% -> 14%
where the time goes in v5:
time: 150 us; the launch traced here: 149 us
  starting transfers between devices  86.5 us (58%)
  waiting for transfers between devices  34.2 us (23%)
  Pallas kernels  23.6 us (16%)
  local copies, waits for them, and re-layouts  3.17 us (2%)
    ppermute x23, starting transfers between devices, move(): return lax.ppermute(value, ('c', 'y', 'z'), pairs)  60.5 us
    ppermute x23, waiting for transfers between devices, move(): return lax.ppermute(value, ('c', 'y', 'z'), pairs)  33.5 us
    ppermute x9, starting transfers between devices, hop(): return lax.ppermute(value, 'x', pairs)  24.6 us
    pallas_call x4, Pallas kernels, product(): pl.pallas_call(functools.partial(product_kernel, q, form, total is not No...  19.8 us
  transfers between devices with their start and end apart: 33, of which 10 were waited for; matrix products, arithmetic and copies ran while one was open for 2% of the time, Pallas kernels for 14%

profile of v5, /device:TPU:1, one launch (start us, length us, event | category | flops | bytes accessed | tf_op | source)
XLA Modules:
  0.0 149.2 jit_solution(234273068075598113)
XLA Ops:
  0.0 1.4 collective-permute-start.2
  1.4 1.4 collective-permute-start
  2.8 1.4 collective-permute-start.15
  4.2 0.0 collective-permute-done.2.slab_ref.refs_1_
  4.3 2.5 %collective-permute-start.16 = (f32[1024,256]{1,0:T(8,128)S(1)}, f32[1024,256]{1,0:T(8,128)}, u32[]{:S(2)}, u32[]{:S(2)}) collective-permute-start(f32[1024,256]{1,0:T(8,128)S(1)} %collective-permute-done.2.slab_ref.refs_1_), channel_id=1, source_target_pairs={{0,3},{1,0},{2,1},{3,2},{4,7},{5,4},{6,5},{7,6},{8,11},{9,8},{10,9... | collective-permute-start | bytes 3145736 | tf_op jit(solution)/shard_map/ppermute | solution.py:26
  6.7 0.1 pad_add_fusion.at_ref
  6.8 1.2 copy-done
  8.0 0.6 cut.2
  8.6 0.6 cut.3
  9.2 3.9 %collective-permute-start.7 = (f32[256,256]{1,0:T(8,128)S(1)}, f32[256,256]{1,0:T(8,128)}, u32[]{:S(2)}, u32[]{:S(2)}) collective-permute-start(f32[256,256]{1,0:T(8,128)S(1)} %get-tuple-element.32.refs_2_), channel_id=1, source_target_pairs={{0,32},{32,64},{64,96},{1,33},{33,65},{65,97},{2,34},{34,66},{66,9... | collective-permute-start | bytes 786440 | tf_op jit(solution)/shard_map/ppermute | solution.py:46
  13.1 3.9 %collective-permute-done.refs_0_ = f32[1024,256]{1,0:T(8,128)} collective-permute-done((f32[1024,256]{1,0:T(8,128)}, f32[1024,256]{1,0:T(8,128)}, u32[]{:S(2)}, u32[]{:S(2)}) %collective-permute-start) | collective-permute-done | bytes 1048608 | tf_op jit(solution)/shard_map/ppermute | solution.py:26
  17.0 1.5 collective-permute-start.12
  18.5 1.2 collective-permute-start.3
  19.7 0.1 broadcast_select_fusion
  19.8 0.2 select_reduce_fusion
  20.0 0.0 collective-permute-done.7.refs_3_
  20.0 4.4 %collective-permute-start.8 = (f32[256,256]{1,0:T(8,128)S(1)}, f32[256,256]{1,0:T(8,128)S(1)}, u32[]{:S(2)}, u32[]{:S(2)}) collective-permute-start(f32[256,256]{1,0:T(8,128)S(1)} %get-tuple-element.32.refs_2_), channel_id=1, source_target_pairs={{0,96},{1,97},{2,98},{3,99},{4,100},{5,101},{6,102},{7,103},{8,104... | collective-permute-start | bytes 786440 | tf_op jit(solution)/shard_map/ppermute | solution.py:46
  24.4 0.0 collective-permute-done.11
  24.4 0.7 collective-permute-start.10
  25.1 0.4 collective-permute-done.3.refs_1_
  25.5 3.1 %collective-permute-start.4 = (f32[256,256]{1,0:T(8,128)S(1)}, f32[256,256]{1,0:T(8,128)S(1)}, u32[]{:S(2)}, u32[]{:S(2)}) collective-permute-start(f32[256,256]{1,0:T(8,128)S(1)} %collective-permute-done.3.refs_1_), channel_id=1, source_target_pairs={{0,32},{32,64},{64,96},{1,33},{33,65},{65,97},{2,34},{34,66},{66,9... | collective-permute-start | bytes 786440 | tf_op jit(solution)/shard_map/ppermute | solution.py:46
  28.6 2.5 %collective-permute-done.12 = f32[256,256]{1,0:T(8,128)} collective-permute-done((f32[256,256]{1,0:T(8,128)S(1)}, f32[256,256]{1,0:T(8,128)}, u32[]{:S(2)}, u32[]{:S(2)}) %collective-permute-start.12) | collective-permute-done | bytes 262176 | tf_op jit(solution)/shard_map/ppermute | solution.py:26
  31.1 4.4 %collective-permute-start.5 = (f32[256,256]{1,0:T(8,128)S(1)}, f32[256,256]{1,0:T(8,128)S(1)}, u32[]{:S(2)}, u32[]{:S(2)}) collective-permute-start(f32[256,256]{1,0:T(8,128)S(1)} %collective-permute-done.3.refs_1_), channel_id=1, source_target_pairs={{0,96},{1,97},{2,98},{3,99},{4,100},{5,101},{6,102},{7,103},{8,104... | collective-permute-start | bytes 786440 | tf_op jit(solution)/shard_map/ppermute | solution.py:46
  35.5 1.0 constant_dynamic-update-slice_fusion.1
  36.5 1.0 constant_dynamic-update-slice_fusion.refs_2_.refs_7_
  37.4 0.0 collective-permute-done.8.refs_4_
  37.5 6.1 %collective-permute-start.1 = (f32[1024,256]{1,0:T(8,128)}, f32[1024,256]{1,0:T(8,128)S(1)}, u32[]{:S(2)}, u32[]{:S(2)}) collective-permute-start(f32[1024,256]{1,0:T(8,128)} %collective-permute-done.refs_0_), channel_id=1, source_target_pairs={{0,1},{1,2},{2,3},{3,0},{4,5},{5,6},{6,7},{7,4},{8,9},{9,10},{10,1... | collective-permute-start | bytes 3145736 | tf_op jit(solution)/shard_map/ppermute | solution.py:26
  43.6 0.0 collective-permute-done.4.refs_2_
  43.6 1.3 collective-permute-start.13
  44.9 0.0 collective-permute-done.5.refs_3_
  44.9 1.9 %collective-permute-start.14 = (f32[512,256]{1,0:T(8,128)S(1)}, f32[512,256]{1,0:T(8,128)S(1)}, u32[]{:S(2)}, u32[]{:S(2)}) collective-permute-start(f32[512,256]{1,0:T(8,128)S(1)} %constant_dynamic-update-slice_fusion.refs_2_.refs_7_), channel_id=1, source_target_pairs={{0,96},{32,0},{1,97},{33,1},{2,98},{34,2},{3,99},{35,3},{4,100},{3... | collective-permute-start | bytes 1572872 | tf_op jit(solution)/shard_map/ppermute | solution.py:46
  46.8 0.0 collective-permute-done.16.refs_6_
  46.8 5.4 %collective-permute-start.24 = (f32[1024,256]{1,0:T(8,128)}, f32[1024,256]{1,0:T(8,128)S(1)}, u32[]{:S(2)}, u32[]{:S(2)}) collective-permute-start(f32[1024,256]{1,0:T(8,128)} %collective-permute-done.16.refs_6_), channel_id=1, source_target_pairs={{0,3},{1,0},{2,1},{3,2},{4,7},{5,4},{6,5},{7,6},{8,11},{9,8},{10,9... | collective-permute-start | bytes 3145736 | tf_op jit(solution)/shard_map/ppermute | solution.py:26
  52.2 3.7 %shard_map.28 = (f32[8,768,256]{2,1,0:T(8,128)S(1)}, bf16[2048,512]{1,0:T(8,128)(2,1)S(1)}) custom-call(s32[64]{0:T(128)S(1)} %broadcast_add_fusion.2.tab_ref, f32[1024,256]{1,0:T(8,128)S(1)} %copy-done.1, f32[1024,256]{1,0:T(8,128)S(1)} %collective-permute-done.2.slab_ref.refs_1_, f32[256,256]{1,0:T(8,128)S(1)} %get-tuple-element.32.refs_2_, ...), custom_call_target="tpu_custom_call" | custom-call | flops 6442450944 | bytes 12582912 | tf_op jit(solution)/shard_map/pallas_call | solution.py:172
  55.9 0.7 collective-permute-start.9
  56.6 0.7 collective-permute-done.14.refs_4_.refs_9_
  57.3 0.7 collective-permute-start.6
  58.0 4.2 %collective-permute-start.17 = (f32[512,256]{1,0:T(8,128)S(1)}, f32[512,256]{1,0:T(8,128)S(1)}, u32[]{:S(2)}, u32[]{:S(2)}) collective-permute-start(f32[512,256]{1,0:T(8,128)S(1)} %collective-permute-done.14.refs_4_.refs_9_), channel_id=1, source_target_pairs={{0,96},{96,64},{1,97},{97,65},{2,98},{98,66},{3,99},{99,67},{4,100... | collective-permute-start | bytes 1572872 | tf_op jit(solution)/shard_map/ppermute | solution.py:46
  62.2 7.6 %shard_map.29 = (f32[8,768,256]{2,1,0:T(8,128)S(1)}, bf16[2048,512]{1,0:T(8,128)(2,1)S(1)}, bf16[2048,512]{1,0:T(8,128)(2,1)S(1)}) custom-call(s32[64]{0:T(128)S(1)} %broadcast_add_fusion.2.tab_ref, f32[1024,256]{1,0:T(8,128)} %collective-permute-done.refs_0_, f32[1024,256]{1,0:T(8,128)S(1)} %collective-permute-done.10.refs_1_, ...), custom_call_target="tpu_custom_call", output_to_operand_aliasing={{0}: (11, {})} | custom-call | flops 6442450944 | bytes 12582912 | tf_op jit(solution)/shard_map/pallas_call | solution.py:172
  69.9 4.3 %shard_map.30 = (f32[8,64,512]{2,1,0:T(8,128)S(1)}, f32[8,64,512]{2,1,0:T(8,128)S(1)}, f32[8,64,512]{2,1,0:T(8,128)S(1)}, f32[8,64,512]{2,1,0:T(8,128)S(1)}) custom-call(s32[64]{0:T(128)S(1)} %broadcast_add_fusion.2.tab_ref, f32[1024,256]{1,0:T(8,128)S(1)} %collective-permute-done.1.refs_0_, f32[256,256]{1,0:T(8,128)S(1)} %collective-permute-done.3.refs_1_, ...), custom_call_target="tpu_custom_call" | custom-call | flops 3221225472 | bytes 12582912 | tf_op jit(solution)/shard_map/pallas_call | solution.py:172
  74.1 0.1 collective-permute-start.18
  74.2 4.3 %shard_map.31 = (f32[8,64,512]{2,1,0:T(8,128)S(1)}, f32[4,64,512]{2,1,0:T(8,128)S(1)}, f32[4,64,512]{2,1,0:T(8,128)S(1)}, f32[8,64,512]{2,1,0:T(8,128)S(1)}, f32[8,64,512]{2,1,0:T(8,128)S(1)}) custom-call(s32[64]{0:T(128)S(1)} %broadcast_add_fusion.2.tab_ref, f32[1024,256]{1,0:T(8,128)S(1)} %collective-permute-done.24.refs_0_, ...), custom_call_target="tpu_custom_call" | custom-call | flops 3221225472 | bytes 12582912 | tf_op jit(solution)/shard_map/pallas_call | solution.py:172
  78.5 4.0 %collective-permute-start.25 = (f32[8,64,512]{2,1,0:T(8,128)S(1)}, f32[8,64,512]{2,1,0:T(8,128)S(1)}, u32[]{:S(2)}, u32[]{:S(2)}) collective-permute-start(f32[8,64,512]{2,1,0:T(8,128)S(1)} %get-tuple-element.46), channel_id=1, source_target_pairs={{0,12},{1,13},{2,14},{3,15},{4,0},{5,1},{6,2},{7,3},{8,4},{9,5},{1... | collective-permute-start | bytes 3145736 | tf_op jit(solution)/shard_map/ppermute | solution.py:26
  82.5 3.4 %collective-permute-start.20 = (f32[8,64,512]{2,1,0:T(8,128)S(1)}, f32[8,64,512]{2,1,0:T(8,128)S(1)}, u32[]{:S(2)}, u32[]{:S(2)}) collective-permute-start(f32[8,64,512]{2,1,0:T(8,128)S(1)} %get-tuple-element.43), channel_id=1, source_target_pairs={{0,12},{1,13},{2,14},{3,15},{4,0},{5,1},{6,2},{7,3},{8,4},{9,5},{1... | collective-permute-start | bytes 3145736 | tf_op jit(solution)/shard_map/ppermute | solution.py:26
  85.9 4.7 %collective-permute-done.18 = f32[8,64,512]{2,1,0:T(8,128)S(1)} collective-permute-done((f32[8,64,512]{2,1,0:T(8,128)S(1)}, f32[8,64,512]{2,1,0:T(8,128)S(1)}, u32[]{:S(2)}, u32[]{:S(2)}) %collective-permute-start.18) | collective-permute-done | bytes 1048608 | tf_op jit(solution)/shard_map/ppermute | solution.py:26
  90.6 0.2 add.262
  90.8 2.1 %collective-permute-start.19 = (f32[8,64,512]{2,1,0:T(8,128)S(1)}, f32[8,64,512]{2,1,0:T(8,128)S(1)}, u32[]{:S(2)}, u32[]{:S(2)}) collective-permute-start(f32[8,64,512]{2,1,0:T(8,128)S(1)} %add.262), channel_id=1, source_target_pairs={{0,4},{1,5},{2,6},{3,7},{4,8},{5,9},{6,10},{7,11},{8,12},{9,13},{1... | collective-permute-start | bytes 3145736 | tf_op jit(solution)/shard_map/ppermute | solution.py:26
  92.9 4.8 %collective-permute-done.25 = f32[8,64,512]{2,1,0:T(8,128)S(1)} collective-permute-done((f32[8,64,512]{2,1,0:T(8,128)S(1)}, f32[8,64,512]{2,1,0:T(8,128)S(1)}, u32[]{:S(2)}, u32[]{:S(2)}) %collective-permute-start.25) | collective-permute-done | bytes 1048608 | tf_op jit(solution)/shard_map/ppermute | solution.py:26
  97.7 0.2 add.271
  97.9 0.3 collective-permute-start.26
  98.2 1.5 %collective-permute-start.27 = (f32[4,64,512]{2,1,0:T(8,128)S(1)}, f32[4,64,512]{2,1,0:T(8,128)S(1)}, u32[]{:S(2)}, u32[]{:S(2)}) collective-permute-start(f32[4,64,512]{2,1,0:T(8,128)S(1)} %get-tuple-element.47), channel_id=1, source_target_pairs={{0,4},{1,5},{2,6},{3,7},{4,8},{5,9},{6,10},{7,11},{8,12},{9,13},{1... | collective-permute-start | bytes 1572872 | tf_op jit(solution)/shard_map/ppermute | solution.py:26
  99.8 1.4 collective-permute-start.30
  101.1 7.8 %collective-permute-done.20 = f32[8,64,512]{2,1,0:T(8,128)S(1)} collective-permute-done((f32[8,64,512]{2,1,0:T(8,128)S(1)}, f32[8,64,512]{2,1,0:T(8,128)S(1)}, u32[]{:S(2)}, u32[]{:S(2)}) %collective-permute-start.20) | collective-permute-done | bytes 1048608 | tf_op jit(solution)/shard_map/ppermute | solution.py:26
  108.9 0.3 slice_add_fusion.8
  109.3 6.6 %collective-permute-start.21 = (f32[2,64,512]{2,1,0:T(8,128)S(1)}, f32[2,64,512]{2,1,0:T(8,128)S(1)}, u32[]{:S(2)}, u32[]{:S(2)}) collective-permute-start(f32[2,64,512]{2,1,0:T(8,128)S(1)} %get-tuple-element.51), channel_id=1, source_target_pairs={{0,1},{1,2},{2,3},{3,0},{4,5},{5,6},{6,7},{7,4},{8,9},{9,10},{10,1... | collective-permute-start | bytes 786440 | tf_op jit(solution)/shard_map/ppermute | solution.py:26
  115.9 1.1 collective-permute-start.22
  117.0 2.4 %collective-permute-start.23 = (f32[2,64,512]{2,1,0:T(8,128)S(1)}, f32[2,64,512]{2,1,0:T(8,128)S(1)}, u32[]{:S(2)}, u32[]{:S(2)}) collective-permute-start(f32[2,64,512]{2,1,0:T(8,128)S(1)} %get-tuple-element.49), channel_id=1, source_target_pairs={{0,3},{1,0},{2,1},{3,2},{4,7},{5,4},{6,5},{7,6},{8,11},{9,8},{10,9... | collective-permute-start | bytes 786440 | tf_op jit(solution)/shard_map/ppermute | solution.py:26
  119.4 0.8 collective-permute-done.26
  120.2 0.3 slice_add_fusion
  120.5 14.3 %collective-permute-start.28 = (f32[2,64,512]{2,1,0:T(8,128)S(1)}, f32[2,64,512]{2,1,0:T(8,128)S(1)}, u32[]{:S(2)}, u32[]{:S(2)}) collective-permute-start(f32[2,64,512]{2,1,0:T(8,128)S(1)} %get-tuple-element.57), channel_id=1, source_target_pairs={{0,16},{1,17},{2,18},{3,19},{4,20},{5,21},{6,22},{7,23},{8,24},{9,... | collective-permute-start | bytes 786440 | tf_op jit(solution)/shard_map/ppermute | solution.py:26
  134.8 3.3 %collective-permute-start.32 = (f32[2,64,512]{2,1,0:T(8,128)S(1)}, f32[2,64,512]{2,1,0:T(8,128)S(1)}, u32[]{:S(2)}, u32[]{:S(2)}) collective-permute-start(f32[2,64,512]{2,1,0:T(8,128)S(1)} %get-tuple-element.53), channel_id=1, source_target_pairs={{0,19},{1,16},{2,17},{3,18},{4,23},{5,20},{6,21},{7,22},{8,27},{9,... | collective-permute-start | bytes 786440 | tf_op jit(solution)/shard_map/ppermute | solution.py:26
  138.1 4.5 %collective-permute-done.29.refs_5_ = f32[2,64,512]{2,1,0:T(8,128)S(1)} collective-permute-done((f32[2,64,512]{2,1,0:T(8,128)S(1)}, f32[2,64,512]{2,1,0:T(8,128)S(1)}, u32[]{:S(2)}, u32[]{:S(2)}) %collective-permute-start.29) | collective-permute-done | bytes 262176 | tf_op jit(solution)/shard_map/ppermute | solution.py:26
  142.6 4.0 %collective-permute-done.31.refs_6_ = f32[2,64,512]{2,1,0:T(8,128)S(1)} collective-permute-done((f32[2,64,512]{2,1,0:T(8,128)S(1)}, f32[2,64,512]{2,1,0:T(8,128)S(1)}, u32[]{:S(2)}, u32[]{:S(2)}) %collective-permute-start.31) | collective-permute-done | bytes 262176 | tf_op jit(solution)/shard_map/ppermute | solution.py:26
  146.6 2.6 %join.1 = f32[1,2,512,512]{3,2,1,0:T(8,128)} custom-call(s32[3]{0:T(128)S(1)} %pad_add_fusion.at_ref, f32[2,64,512]{2,1,0:T(8,128)S(1)} %get-tuple-element.52.refs_0_, f32[2,64,512]{2,1,0:T(8,128)S(1)} %collective-permute-done.21.refs_1_, f32[2,64,512]{2,1,0:T(8,128)S(1)} %collective-permute-done.22.refs_2_, ...), custom_call_target="tpu_custom_call" | custom-call | flops 1000000 | bytes 4194304 | tf_op jit(solution)/shard_map/join/pallas_call | solution.py:201
  (29 shorter events, 0.1 us)
Async XLA Ops:
  0.0 19.8 %copy-start.2 = (s32[16,16]{1,0:T(8,128)S(1)}, s32[16,16]{1,0:T(8,128)}, u32[]{:S(2)}) copy-start(s32[16,16]{1,0:T(8,128)} %param.3) | copy-start | bytes 3076
  0.0 4.2 %collective-permute-start.2 = (f32[1024,256]{1,0:T(8,128)}, f32[1024,256]{1,0:T(8,128)S(1)}, u32[]{:S(2)}, u32[]{:S(2)}) collective-permute-start(f32[1024,256]{1,0:T(8,128)} %refs_0_.1), channel_id=1, source_target_pairs={{0,16},{16,0},{1,17},{17,1},{2,18},{18,2},{3,19},{19,3},{4,20},{20... | collective-permute-start | bytes 3145736 | tf_op jit(solution)/shard_map/ppermute | solution.py:42
  1.4 15.6 %collective-permute-start = (f32[1024,256]{1,0:T(8,128)}, f32[1024,256]{1,0:T(8,128)}, u32[]{:S(2)}, u32[]{:S(2)}) collective-permute-start(f32[1024,256]{1,0:T(8,128)} %refs_0_.1), channel_id=1, source_target_pairs={{0,1},{1,2},{2,3},{3,0},{4,5},{5,6},{6,7},{7,4},{8,9},{9,10},{10,1... | collective-permute-start | bytes 3145736 | tf_op jit(solution)/shard_map/ppermute | solution.py:26
  2.8 15.7 %collective-permute-start.15 = (f32[1024,256]{1,0:T(8,128)}, f32[1024,256]{1,0:T(8,128)}, u32[]{:S(2)}, u32[]{:S(2)}) collective-permute-start(f32[1024,256]{1,0:T(8,128)} %refs_0_.1), channel_id=1, source_target_pairs={{0,3},{1,0},{2,1},{3,2},{4,7},{5,4},{6,5},{7,6},{8,11},{9,8},{10,9... | collective-permute-start | bytes 3145736 | tf_op jit(solution)/shard_map/ppermute | solution.py:26
  4.3 42.6 %collective-permute-start.16 = (f32[1024,256]{1,0:T(8,128)S(1)}, f32[1024,256]{1,0:T(8,128)}, u32[]{:S(2)}, u32[]{:S(2)}) collective-permute-start(f32[1024,256]{1,0:T(8,128)S(1)} %collective-permute-done.2.slab_ref.refs_1_), channel_id=1, source_target_pairs={{0,3},{1,0},{2,1},{3,2},{4,7},{5,4},{6,5},{7,6},{8,11},{9,8},{10,9... | collective-permute-start | bytes 3145736 | tf_op jit(solution)/shard_map/ppermute | solution.py:26
  6.8 1.2 copy-start
  8.0 44.2 %copy-start.1 = (f32[1024,256]{1,0:T(8,128)S(1)}, f32[1024,256]{1,0:T(8,128)}, u32[]{:S(2)}) copy-start(f32[1024,256]{1,0:T(8,128)} %refs_0_.1) | copy-start | bytes 3145732
  9.2 10.8 %collective-permute-start.7 = (f32[256,256]{1,0:T(8,128)S(1)}, f32[256,256]{1,0:T(8,128)}, u32[]{:S(2)}, u32[]{:S(2)}) collective-permute-start(f32[256,256]{1,0:T(8,128)S(1)} %get-tuple-element.32.refs_2_), channel_id=1, source_target_pairs={{0,32},{32,64},{64,96},{1,33},{33,65},{65,97},{2,34},{34,66},{66,9... | collective-permute-start | bytes 786440 | tf_op jit(solution)/shard_map/ppermute | solution.py:46
  13.1 11.3 %collective-permute-start.11 = (f32[256,256]{1,0:T(8,128)S(1)}, f32[256,256]{1,0:T(8,128)}, u32[]{:S(2)}, u32[]{:S(2)}) collective-permute-start(f32[256,256]{1,0:T(8,128)S(1)} %get-tuple-element.34), channel_id=1, source_target_pairs={{0,1},{1,2},{2,3},{3,0},{4,5},{5,6},{6,7},{7,4},{8,9},{9,10},{10,1... | collective-permute-start | bytes 786440 | tf_op jit(solution)/shard_map/ppermute | solution.py:26
  17.0 14.1 %collective-permute-start.12 = (f32[256,256]{1,0:T(8,128)S(1)}, f32[256,256]{1,0:T(8,128)}, u32[]{:S(2)}, u32[]{:S(2)}) collective-permute-start(f32[256,256]{1,0:T(8,128)S(1)} %get-tuple-element.35), channel_id=1, source_target_pairs={{0,3},{1,0},{2,1},{3,2},{4,7},{5,4},{6,5},{7,6},{8,11},{9,8},{10,9... | collective-permute-start | bytes 786440 | tf_op jit(solution)/shard_map/ppermute | solution.py:26
  18.5 7.0 %collective-permute-start.3 = (f32[256,256]{1,0:T(8,128)S(1)}, f32[256,256]{1,0:T(8,128)S(1)}, u32[]{:S(2)}, u32[]{:S(2)}) collective-permute-start(f32[256,256]{1,0:T(8,128)S(1)} %get-tuple-element.31), channel_id=1, source_target_pairs={{0,2},{1,3},{2,0},{3,1},{4,6},{5,7},{6,4},{7,5},{8,10},{9,11},{10,... | collective-permute-start | bytes 786440 | tf_op jit(solution)/shard_map/ppermute | solution.py:26
  20.0 17.5 %collective-permute-start.8 = (f32[256,256]{1,0:T(8,128)S(1)}, f32[256,256]{1,0:T(8,128)S(1)}, u32[]{:S(2)}, u32[]{:S(2)}) collective-permute-start(f32[256,256]{1,0:T(8,128)S(1)} %get-tuple-element.32.refs_2_), channel_id=1, source_target_pairs={{0,96},{1,97},{2,98},{3,99},{4,100},{5,101},{6,102},{7,103},{8,104... | collective-permute-start | bytes 786440 | tf_op jit(solution)/shard_map/ppermute | solution.py:46
  24.4 33.5 %collective-permute-start.10 = (f32[1024,256]{1,0:T(8,128)S(1)}, f32[1024,256]{1,0:T(8,128)S(1)}, u32[]{:S(2)}, u32[]{:S(2)}) collective-permute-start(f32[1024,256]{1,0:T(8,128)S(1)} %collective-permute-done.2.slab_ref.refs_1_), channel_id=1, source_target_pairs={{0,1},{1,2},{2,3},{3,0},{4,5},{5,6},{6,7},{7,4},{8,9},{9,10},{10,1... | collective-permute-start | bytes 3145736 | tf_op jit(solution)/shard_map/ppermute | solution.py:26
  25.5 18.0 %collective-permute-start.4 = (f32[256,256]{1,0:T(8,128)S(1)}, f32[256,256]{1,0:T(8,128)S(1)}, u32[]{:S(2)}, u32[]{:S(2)}) collective-permute-start(f32[256,256]{1,0:T(8,128)S(1)} %collective-permute-done.3.refs_1_), channel_id=1, source_target_pairs={{0,32},{32,64},{64,96},{1,33},{33,65},{65,97},{2,34},{34,66},{66,9... | collective-permute-start | bytes 786440 | tf_op jit(solution)/shard_map/ppermute | solution.py:46
  31.1 13.8 %collective-permute-start.5 = (f32[256,256]{1,0:T(8,128)S(1)}, f32[256,256]{1,0:T(8,128)S(1)}, u32[]{:S(2)}, u32[]{:S(2)}) collective-permute-start(f32[256,256]{1,0:T(8,128)S(1)} %collective-permute-done.3.refs_1_), channel_id=1, source_target_pairs={{0,96},{1,97},{2,98},{3,99},{4,100},{5,101},{6,102},{7,103},{8,104... | collective-permute-start | bytes 786440 | tf_op jit(solution)/shard_map/ppermute | solution.py:46
  37.5 32.4 %collective-permute-start.1 = (f32[1024,256]{1,0:T(8,128)}, f32[1024,256]{1,0:T(8,128)S(1)}, u32[]{:S(2)}, u32[]{:S(2)}) collective-permute-start(f32[1024,256]{1,0:T(8,128)} %collective-permute-done.refs_0_), channel_id=1, source_target_pairs={{0,1},{1,2},{2,3},{3,0},{4,5},{5,6},{6,7},{7,4},{8,9},{9,10},{10,1... | collective-permute-start | bytes 3145736 | tf_op jit(solution)/shard_map/ppermute | solution.py:26
  43.6 12.3 %collective-permute-start.13 = (f32[512,256]{1,0:T(8,128)S(1)}, f32[512,256]{1,0:T(8,128)S(1)}, u32[]{:S(2)}, u32[]{:S(2)}) collective-permute-start(f32[512,256]{1,0:T(8,128)S(1)} %constant_dynamic-update-slice_fusion.refs_2_.refs_7_), channel_id=1, source_target_pairs={{0,32},{32,64},{64,96},{1,33},{33,65},{65,97},{2,34},{34,66},{66,9... | collective-permute-start | bytes 1572872 | tf_op jit(solution)/shard_map/ppermute | solution.py:46
  44.9 12.4 %collective-permute-start.14 = (f32[512,256]{1,0:T(8,128)S(1)}, f32[512,256]{1,0:T(8,128)S(1)}, u32[]{:S(2)}, u32[]{:S(2)}) collective-permute-start(f32[512,256]{1,0:T(8,128)S(1)} %constant_dynamic-update-slice_fusion.refs_2_.refs_7_), channel_id=1, source_target_pairs={{0,96},{32,0},{1,97},{33,1},{2,98},{34,2},{3,99},{35,3},{4,100},{3... | collective-permute-start | bytes 1572872 | tf_op jit(solution)/shard_map/ppermute | solution.py:46
  46.8 27.4 %collective-permute-start.24 = (f32[1024,256]{1,0:T(8,128)}, f32[1024,256]{1,0:T(8,128)S(1)}, u32[]{:S(2)}, u32[]{:S(2)}) collective-permute-start(f32[1024,256]{1,0:T(8,128)} %collective-permute-done.16.refs_6_), channel_id=1, source_target_pairs={{0,3},{1,0},{2,1},{3,2},{4,7},{5,4},{6,5},{7,6},{8,11},{9,8},{10,9... | collective-permute-start | bytes 3145736 | tf_op jit(solution)/shard_map/ppermute | solution.py:26
  55.9 13.9 %collective-permute-start.9 = (f32[256,256]{1,0:T(8,128)}, f32[256,256]{1,0:T(8,128)S(1)}, u32[]{:S(2)}, u32[]{:S(2)}) collective-permute-start(f32[256,256]{1,0:T(8,128)} %collective-permute-done.7.refs_3_), channel_id=1, source_target_pairs={{32,64},{64,96},{33,65},{65,97},{34,66},{66,98},{35,67},{67,99},{3... | collective-permute-start | bytes 786440 | tf_op jit(solution)/shard_map/ppermute | solution.py:46
  57.3 12.6 %collective-permute-start.6 = (f32[256,256]{1,0:T(8,128)S(1)}, f32[256,256]{1,0:T(8,128)S(1)}, u32[]{:S(2)}, u32[]{:S(2)}) collective-permute-start(f32[256,256]{1,0:T(8,128)S(1)} %collective-permute-done.4.refs_2_), channel_id=1, source_target_pairs={{32,64},{64,96},{33,65},{65,97},{34,66},{66,98},{35,67},{67,99},{3... | collective-permute-start | bytes 786440 | tf_op jit(solution)/shard_map/ppermute | solution.py:46
  58.0 11.9 %collective-permute-start.17 = (f32[512,256]{1,0:T(8,128)S(1)}, f32[512,256]{1,0:T(8,128)S(1)}, u32[]{:S(2)}, u32[]{:S(2)}) collective-permute-start(f32[512,256]{1,0:T(8,128)S(1)} %collective-permute-done.14.refs_4_.refs_9_), channel_id=1, source_target_pairs={{0,96},{96,64},{1,97},{97,65},{2,98},{98,66},{3,99},{99,67},{4,100... | collective-permute-start | bytes 1572872 | tf_op jit(solution)/shard_map/ppermute | solution.py:46
  74.1 16.5 %collective-permute-start.18 = (f32[8,64,512]{2,1,0:T(8,128)S(1)}, f32[8,64,512]{2,1,0:T(8,128)S(1)}, u32[]{:S(2)}, u32[]{:S(2)}) collective-permute-start(f32[8,64,512]{2,1,0:T(8,128)S(1)} %get-tuple-element.42), channel_id=1, source_target_pairs={{0,4},{1,5},{2,6},{3,7},{4,8},{5,9},{6,10},{7,11},{8,12},{9,13},{1... | collective-permute-start | bytes 3145736 | tf_op jit(solution)/shard_map/ppermute | solution.py:26
  78.5 19.2 %collective-permute-start.25 = (f32[8,64,512]{2,1,0:T(8,128)S(1)}, f32[8,64,512]{2,1,0:T(8,128)S(1)}, u32[]{:S(2)}, u32[]{:S(2)}) collective-permute-start(f32[8,64,512]{2,1,0:T(8,128)S(1)} %get-tuple-element.46), channel_id=1, source_target_pairs={{0,12},{1,13},{2,14},{3,15},{4,0},{5,1},{6,2},{7,3},{8,4},{9,5},{1... | collective-permute-start | bytes 3145736 | tf_op jit(solution)/shard_map/ppermute | solution.py:26
  82.5 26.5 %collective-permute-start.20 = (f32[8,64,512]{2,1,0:T(8,128)S(1)}, f32[8,64,512]{2,1,0:T(8,128)S(1)}, u32[]{:S(2)}, u32[]{:S(2)}) collective-permute-start(f32[8,64,512]{2,1,0:T(8,128)S(1)} %get-tuple-element.43), channel_id=1, source_target_pairs={{0,12},{1,13},{2,14},{3,15},{4,0},{5,1},{6,2},{7,3},{8,4},{9,5},{1... | collective-permute-start | bytes 3145736 | tf_op jit(solution)/shard_map/ppermute | solution.py:26
  90.8 18.1 %collective-permute-start.19 = (f32[8,64,512]{2,1,0:T(8,128)S(1)}, f32[8,64,512]{2,1,0:T(8,128)S(1)}, u32[]{:S(2)}, u32[]{:S(2)}) collective-permute-start(f32[8,64,512]{2,1,0:T(8,128)S(1)} %add.262), channel_id=1, source_target_pairs={{0,4},{1,5},{2,6},{3,7},{4,8},{5,9},{6,10},{7,11},{8,12},{9,13},{1... | collective-permute-start | bytes 3145736 | tf_op jit(solution)/shard_map/ppermute | solution.py:26
  97.9 22.3 %collective-permute-start.26 = (f32[8,64,512]{2,1,0:T(8,128)S(1)}, f32[8,64,512]{2,1,0:T(8,128)S(1)}, u32[]{:S(2)}, u32[]{:S(2)}) collective-permute-start(f32[8,64,512]{2,1,0:T(8,128)S(1)} %add.271), channel_id=1, source_target_pairs={{0,12},{1,13},{2,14},{3,15},{4,0},{5,1},{6,2},{7,3},{8,4},{9,5},{1... | collective-permute-start | bytes 3145736 | tf_op jit(solution)/shard_map/ppermute | solution.py:26
  98.2 18.7 %collective-permute-start.27 = (f32[4,64,512]{2,1,0:T(8,128)S(1)}, f32[4,64,512]{2,1,0:T(8,128)S(1)}, u32[]{:S(2)}, u32[]{:S(2)}) collective-permute-start(f32[4,64,512]{2,1,0:T(8,128)S(1)} %get-tuple-element.47), channel_id=1, source_target_pairs={{0,4},{1,5},{2,6},{3,7},{4,8},{5,9},{6,10},{7,11},{8,12},{9,13},{1... | collective-permute-start | bytes 1572872 | tf_op jit(solution)/shard_map/ppermute | solution.py:26
  99.8 19.6 %collective-permute-start.30 = (f32[4,64,512]{2,1,0:T(8,128)S(1)}, f32[4,64,512]{2,1,0:T(8,128)S(1)}, u32[]{:S(2)}, u32[]{:S(2)}) collective-permute-start(f32[4,64,512]{2,1,0:T(8,128)S(1)} %get-tuple-element.48), channel_id=1, source_target_pairs={{0,4},{1,5},{2,6},{3,7},{4,8},{5,9},{6,10},{7,11},{8,12},{9,13},{1... | collective-permute-start | bytes 1572872 | tf_op jit(solution)/shard_map/ppermute | solution.py:26
  109.3 25.5 %collective-permute-start.21 = (f32[2,64,512]{2,1,0:T(8,128)S(1)}, f32[2,64,512]{2,1,0:T(8,128)S(1)}, u32[]{:S(2)}, u32[]{:S(2)}) collective-permute-start(f32[2,64,512]{2,1,0:T(8,128)S(1)} %get-tuple-element.51), channel_id=1, source_target_pairs={{0,1},{1,2},{2,3},{3,0},{4,5},{5,6},{6,7},{7,4},{8,9},{9,10},{10,1... | collective-permute-start | bytes 786440 | tf_op jit(solution)/shard_map/ppermute | solution.py:26
  115.9 19.0 %collective-permute-start.22 = (f32[2,64,512]{2,1,0:T(8,128)S(1)}, f32[2,64,512]{2,1,0:T(8,128)S(1)}, u32[]{:S(2)}, u32[]{:S(2)}) collective-permute-start(f32[2,64,512]{2,1,0:T(8,128)S(1)} %get-tuple-element.50), channel_id=1, source_target_pairs={{0,2},{1,3},{2,0},{3,1},{4,6},{5,7},{6,4},{7,5},{8,10},{9,11},{10,... | collective-permute-start | bytes 786440 | tf_op jit(solution)/shard_map/ppermute | solution.py:26
  117.0 21.2 %collective-permute-start.23 = (f32[2,64,512]{2,1,0:T(8,128)S(1)}, f32[2,64,512]{2,1,0:T(8,128)S(1)}, u32[]{:S(2)}, u32[]{:S(2)}) collective-permute-start(f32[2,64,512]{2,1,0:T(8,128)S(1)} %get-tuple-element.49), channel_id=1, source_target_pairs={{0,3},{1,0},{2,1},{3,2},{4,7},{5,4},{6,5},{7,6},{8,11},{9,8},{10,9... | collective-permute-start | bytes 786440 | tf_op jit(solution)/shard_map/ppermute | solution.py:26
  120.5 17.6 %collective-permute-start.28 = (f32[2,64,512]{2,1,0:T(8,128)S(1)}, f32[2,64,512]{2,1,0:T(8,128)S(1)}, u32[]{:S(2)}, u32[]{:S(2)}) collective-permute-start(f32[2,64,512]{2,1,0:T(8,128)S(1)} %get-tuple-element.57), channel_id=1, source_target_pairs={{0,16},{1,17},{2,18},{3,19},{4,20},{5,21},{6,22},{7,23},{8,24},{9,... | collective-permute-start | bytes 786440 | tf_op jit(solution)/shard_map/ppermute | solution.py:26
  134.8 7.8 %collective-permute-start.29 = (f32[2,64,512]{2,1,0:T(8,128)S(1)}, f32[2,64,512]{2,1,0:T(8,128)S(1)}, u32[]{:S(2)}, u32[]{:S(2)}) collective-permute-start(f32[2,64,512]{2,1,0:T(8,128)S(1)} %get-tuple-element.58), channel_id=1, source_target_pairs={{0,17},{1,18},{2,19},{3,16},{4,21},{5,22},{6,23},{7,20},{8,25},{9,... | collective-permute-start | bytes 786440 | tf_op jit(solution)/shard_map/ppermute | solution.py:26
  134.8 11.8 %collective-permute-start.31 = (f32[2,64,512]{2,1,0:T(8,128)S(1)}, f32[2,64,512]{2,1,0:T(8,128)S(1)}, u32[]{:S(2)}, u32[]{:S(2)}) collective-permute-start(f32[2,64,512]{2,1,0:T(8,128)S(1)} %get-tuple-element.54), channel_id=1, source_target_pairs={{0,18},{1,19},{2,16},{3,17},{4,22},{5,23},{6,20},{7,21},{8,26},{9,... | collective-permute-start | bytes 786440 | tf_op jit(solution)/shard_map/ppermute | solution.py:26
  134.8 11.7 %collective-permute-start.32 = (f32[2,64,512]{2,1,0:T(8,128)S(1)}, f32[2,64,512]{2,1,0:T(8,128)S(1)}, u32[]{:S(2)}, u32[]{:S(2)}) collective-permute-start(f32[2,64,512]{2,1,0:T(8,128)S(1)} %get-tuple-element.53), channel_id=1, source_target_pairs={{0,19},{1,16},{2,17},{3,18},{4,23},{5,20},{6,21},{7,22},{8,27},{9,... | collective-permute-start | bytes 786440 | tf_op jit(solution)/shard_map/ppermute | solution.py:26
